TPU v7x, 128 devices: a whole 4x4x4 slice. The times are simulated.
128 devices in a mesh: ka: 4 (over x_lo, core), rows: 32 (over x_hi, y, z).
Axes of the slice: x: 4 (x_hi: 2, x_lo: 2; x = x_hi * 2 + x_lo), y: 4, z: 4, core: 2. Of those that a mesh axis runs over, the one named last changes fastest.
Arguments:
- hoppings: bfloat16 [32, 384, 128, 128], P('rows', 'ka'), may hold values from -0.046875 to 0.046875
- tile_rows: int32 [32, 384], P('rows', 'ka'), may hold values from 0 to 95, as said below
- tile_cols: int32 [32, 384], P('rows', 'ka'), may hold values from 0 to 95, as said below
- tile_lats: int32 [32, 384], P('rows', 'ka'), may hold values from 0 to 8
- tile_counts: int32 [32, 4], P('rows', 'ka'), may hold values from 48 to 96, as said below
- phase_angle: float32 [8, 9], P('ka'), may hold values from -3.140625 to 3.140625
- vectors: bfloat16 [8, 2, 12288, 256], P('ka', None, 'rows'), may hold values from -6 to 6
Outputs:
- bloch_product: float32 [8, 2, 12288, 256], P('ka', None, 'rows')
Inputs may be any that keep to these rules, and one draw needn't show every extreme that they name: `tile_rows`: slots of row block r (first index) hold tile rows r * 3 to (r + 1) * 3 - 1; several slots may name the same block. `tile_cols`: the cyclic distance between a slot's tile column and its tile row is at most 16, and both distances 16 occur in every row block. `tile_counts`: the live slots of a device are the first ones of its part of the list; some device has all 96 live.
All inputs are finite; a program needn't handle non-finite values.
Results may differ from a plain program's by a relative error of at most 0.0029.
Values may be sent and summed in bfloat16 or wider, within the bound.
A program may use at most 128 MiB of HBM per device.

v0:
```python
import jax
import jax.numpy as jnp
from jax import lax
from jax.sharding import PartitionSpec as P

NLAT = 9
BAND = 16


def side_by_side(arrays, axis, dim, along):
    widths = [a.shape[along] for a in arrays]
    both = jnp.concatenate(arrays, axis=along)
    filled = lax.all_gather(both, axis, axis=dim, tiled=True)
    return tuple(jnp.split(filled, [sum(widths[:k]) for k in range(1, len(widths))], axis=along))


def passed_along(block, axis, distance):
    devices = range(lax.axis_size(axis))
    route = [((i - distance) % len(devices), i) for i in devices]
    return lax.ppermute(block, axis, route)


def body(hoppings, tile_rows, tile_cols, tile_lats, tile_counts, phase_angle, vectors):
    tile_extent = hoppings.shape[2]
    per_device = hoppings.shape[1]
    group_size = lax.axis_size("ka")
    row_shards = lax.axis_size("rows")
    row_tiles = vectors.shape[2] // tile_extent
    total_tiles = row_tiles * row_shards
    reach_shards = (BAND + row_tiles - 1) // row_tiles
    width_tiles = (2 * reach_shards + 1) * row_tiles
    vec_count = vectors.shape[3]
    kpoint_total = vectors.shape[0]
    row_rank = lax.axis_index("rows")
    window_start = (row_rank - reach_shards) * row_tiles
    all_hop, every_row_list, all_cols, all_lats, all_counts = (
        lax.all_gather(hoppings, "ka", axis=1, tiled=True),
        *side_by_side((tile_rows, tile_cols, tile_lats), "ka", 1, 0),
        lax.all_gather(tile_counts, "ka", axis=1, tiled=True),
    )
    slot_count = group_size * per_device
    slot_index = lax.iota(jnp.int32, slot_count)
    active_slot = slot_index % per_device < jnp.repeat(all_counts[0], per_device)
    activity_flags = active_slot.astype(jnp.float32)
    local_row = every_row_list[0] - row_rank * row_tiles
    place = jnp.mod(all_cols[0] - window_start, total_tiles)
    block_ids = (local_row * width_tiles + place).astype(jnp.int32)
    block_count = row_tiles * width_tiles
    member = (lax.iota(jnp.int32, block_count)[:, None] == block_ids[None, :]).astype(jnp.float32)
    lat_onehot = (all_lats[0][:, None] == lax.iota(jnp.int32, NLAT)[None, :]).astype(jnp.float32)
    phase_weights = jnp.stack([jnp.cos(phase_angle), jnp.sin(phase_angle)], axis=1)
    slot_weights = (
        jnp.einsum("kpn,sn->kps", phase_weights, lat_onehot, precision=lax.Precision.HIGHEST)
        * activity_flags[None, None, :]
    )
    build_weights = (slot_weights[:, :, None, :] * member[None, None, :, :]).reshape(
        kpoint_total * 2 * block_count, slot_count
    )
    tiles_flat = all_hop[0].astype(jnp.float32).reshape(slot_count, tile_extent * tile_extent)
    built = jnp.dot(
        build_weights,
        tiles_flat,
        precision=lax.Precision.HIGHEST,
        preferred_element_type=jnp.float32,
    )
    matrices = built.astype(jnp.bfloat16).reshape(
        kpoint_total, 2, row_tiles, width_tiles, tile_extent, tile_extent
    )
    outputs = []
    for kpoint in range(kpoint_total):
        matrix = matrices[kpoint]
        own_rows = vectors[kpoint]
        later = []
        current = own_rows
        for step in range(reach_shards):
            current = passed_along(current, "rows", -1)
            later.append(current)
        earlier = []
        current = own_rows
        for step in range(reach_shards):
            current = passed_along(current, "rows", 1)
            earlier.append(current)
        pieces = earlier[::-1] + [own_rows] + later
        window = jnp.concatenate(pieces, axis=1).reshape(2, width_tiles, tile_extent, vec_count)
        product = jnp.einsum(
            "ptwab,qwbv->ptaqv", matrix, window, preferred_element_type=jnp.float32
        )
        real_part = product[0, :, :, 0] - product[1, :, :, 1]
        imag_part = product[0, :, :, 1] + product[1, :, :, 0]
        outputs.append(
            jnp.stack([real_part, imag_part]).reshape(2, row_tiles * tile_extent, vec_count)
        )
    return jnp.stack(outputs)


def solution(mesh):
    return jax.shard_map(
        body,
        mesh=mesh,
        in_specs=(
            P("rows", "ka", None, None),
            P("rows", "ka"),
            P("rows", "ka"),
            P("rows", "ka"),
            P("rows", "ka"),
            P("ka", None),
            P("ka", None, "rows", None),
        ),
        out_specs=P("ka", None, "rows", None),
        check_vma=False,
    )
```

profile of v0, /device:TPU:1, one launch (start us, length us, event | category | flops | bytes accessed | tf_op | source)
XLA Modules:
  0.0 320.7 jit_solution(5804360235614088463)
XLA Ops:
  7.3 1.2 slice_bitcast_fusion.1
  8.4 2.5 collective-permute-start.12
  11.0 7.1 %collective-permute-start.6 = (bf16[2,384,256]{2,1,0:T(8,128)(2,1)S(1)}, bf16[2,384,256]{2,1,0:T(8,128)(2,1)S(1)}, u32[]{:S(2)}, u32[]{:S(2)}) collective-permute-start(bf16[2,384,256]{2,1,0:T(8,128)(2,1)S(1)} %get-tuple-element.15), channel_id=1, source_target_pairs={{1,0},{2,1},{3,2},{4,3},{5,4},{6,5},{7,6},{8,7},{9,8},{10,9},{11,1... | collective-permute-start | bytes 1179656 | tf_op jit(solution)/shard_map/ppermute | solution.py:20
  18.1 7.2 %collective-permute-start.18 = (bf16[2,384,256]{2,1,0:T(8,128)(2,1)S(1)}, bf16[2,384,256]{2,1,0:T(8,128)(2,1)S(1)}, u32[]{:S(2)}, u32[]{:S(2)}) collective-permute-start(bf16[2,384,256]{2,1,0:T(8,128)(2,1)S(1)} %get-tuple-element.16), channel_id=1, source_target_pairs={{1,0},{2,1},{3,2},{4,3},{5,4},{6,5},{7,6},{8,7},{9,8},{10,9},{11,1... | collective-permute-start | bytes 1179656 | tf_op jit(solution)/shard_map/ppermute | solution.py:20
  25.3 1.5 collective-permute-done.12
  26.8 7.2 %collective-permute-start.7 = (bf16[2,384,256]{2,1,0:T(8,128)(2,1)S(1)}, bf16[2,384,256]{2,1,0:T(8,128)(2,1)S(1)}, u32[]{:S(2)}, u32[]{:S(2)}) collective-permute-start(bf16[2,384,256]{2,1,0:T(8,128)(2,1)S(1)} %collective-permute-done.6), channel_id=1, source_target_pairs={{1,0},{2,1},{3,2},{4,3},{5,4},{6,5},{7,6},{8,7},{9,8},{10,9},{11,1... | collective-permute-start | bytes 1179656 | tf_op jit(solution)/shard_map/ppermute | solution.py:20
  34.0 2.0 collective-permute-done
  36.0 6.3 %collective-permute-done.18 = bf16[2,384,256]{2,1,0:T(8,128)(2,1)S(1)} collective-permute-done((bf16[2,384,256]{2,1,0:T(8,128)(2,1)S(1)}, bf16[2,384,256]{2,1,0:T(8,128)(2,1)S(1)}, u32[]{:S(2)}, u32[]{:S(2)}) %collective-permute-start.18) | collective-permute-done | bytes 393248 | tf_op jit(solution)/shard_map/ppermute | solution.py:20
  42.2 7.9 %collective-permute-start.19 = (bf16[2,384,256]{2,1,0:T(8,128)(2,1)S(1)}, bf16[2,384,256]{2,1,0:T(8,128)(2,1)S(1)}, u32[]{:S(2)}, u32[]{:S(2)}) collective-permute-start(bf16[2,384,256]{2,1,0:T(8,128)(2,1)S(1)} %collective-permute-done.18), channel_id=1, source_target_pairs={{1,0},{2,1},{3,2},{4,3},{5,4},{6,5},{7,6},{8,7},{9,8},{10,9},{11,1... | collective-permute-start | bytes 1179656 | tf_op jit(solution)/shard_map/ppermute | solution.py:20
  50.1 2.6 collective-permute-done.13
  53.4 1.2 dynamic-slice
  55.4 20.8 %all-reduce = s32[4]{0:T(128)S(1)} all-reduce(s32[4]{0:T(128)S(1)} %bitcast_dynamic-update-slice_fusion), channel_id=1, replica_groups=mesh['ka'=4,'rows'=32] {'ka'}, use_global_device_ids=true, to_apply=%add | all-reduce | flops 4 | bytes 32
  76.4 11.6 %collective-permute-start.8 = (bf16[2,384,256]{2,1,0:T(8,128)(2,1)S(1)}, bf16[2,384,256]{2,1,0:T(8,128)(2,1)}, u32[]{:S(2)}, u32[]{:S(2)}) collective-permute-start(bf16[2,384,256]{2,1,0:T(8,128)(2,1)S(1)} %collective-permute-done.7), channel_id=1, source_target_pairs={{1,0},{2,1},{3,2},{4,3},{5,4},{6,5},{7,6},{8,7},{9,8},{10,9},{11,1... | collective-permute-start | bytes 1179656 | tf_op jit(solution)/shard_map/ppermute | solution.py:20
  88.0 7.2 %collective-permute-start.20 = (bf16[2,384,256]{2,1,0:T(8,128)(2,1)S(1)}, bf16[2,384,256]{2,1,0:T(8,128)(2,1)}, u32[]{:S(2)}, u32[]{:S(2)}) collective-permute-start(bf16[2,384,256]{2,1,0:T(8,128)(2,1)S(1)} %collective-permute-done.19), channel_id=1, source_target_pairs={{1,0},{2,1},{3,2},{4,3},{5,4},{6,5},{7,6},{8,7},{9,8},{10,9},{11,1... | collective-permute-start | bytes 1179656 | tf_op jit(solution)/shard_map/ppermute | solution.py:20
  95.9 8.5 %collective-permute-done.8 = bf16[2,384,256]{2,1,0:T(8,128)(2,1)} collective-permute-done((bf16[2,384,256]{2,1,0:T(8,128)(2,1)S(1)}, bf16[2,384,256]{2,1,0:T(8,128)(2,1)}, u32[]{:S(2)}, u32[]{:S(2)}) %collective-permute-start.8) | collective-permute-done | bytes 393248 | tf_op jit(solution)/shard_map/ppermute | solution.py:20
  104.4 8.0 %collective-permute-start.9 = (bf16[2,384,256]{2,1,0:T(8,128)(2,1)}, bf16[2,384,256]{2,1,0:T(8,128)(2,1)}, u32[]{:S(2)}, u32[]{:S(2)}) collective-permute-start(bf16[2,384,256]{2,1,0:T(8,128)(2,1)} %collective-permute-done.8), channel_id=1, source_target_pairs={{1,0},{2,1},{3,2},{4,3},{5,4},{6,5},{7,6},{8,7},{9,8},{10,9},{11,1... | collective-permute-start | bytes 1179656 | tf_op jit(solution)/shard_map/ppermute | solution.py:20
  112.4 8.8 %collective-permute-done.20 = bf16[2,384,256]{2,1,0:T(8,128)(2,1)} collective-permute-done((bf16[2,384,256]{2,1,0:T(8,128)(2,1)S(1)}, bf16[2,384,256]{2,1,0:T(8,128)(2,1)}, u32[]{:S(2)}, u32[]{:S(2)}) %collective-permute-start.20) | collective-permute-done | bytes 393248 | tf_op jit(solution)/shard_map/ppermute | solution.py:20
  121.2 8.0 %collective-permute-start.21 = (bf16[2,384,256]{2,1,0:T(8,128)(2,1)}, bf16[2,384,256]{2,1,0:T(8,128)(2,1)}, u32[]{:S(2)}, u32[]{:S(2)}) collective-permute-start(bf16[2,384,256]{2,1,0:T(8,128)(2,1)} %collective-permute-done.20), channel_id=1, source_target_pairs={{1,0},{2,1},{3,2},{4,3},{5,4},{6,5},{7,6},{8,7},{9,8},{10,9},{11,1... | collective-permute-start | bytes 1179656 | tf_op jit(solution)/shard_map/ppermute | solution.py:20
  130.0 30.1 %all-gather = s32[4,96,3]{1,2,0:T(4,128)S(1)} all-gather(s32[1,96,3]{1,2,0:T(4,128)S(1)} %add_bitcast_fusion), channel_id=1, replica_groups=mesh['ka'=4,'rows'=32] {'ka'}, dimensions={0}, use_global_device_ids=true | all-gather | bytes 5760 | tf_op jit(solution)/shard_map/all_gather | solution.py:13
  160.2 8.0 %collective-permute-start.10 = (bf16[2,384,256]{2,1,0:T(8,128)(2,1)}, bf16[2,384,256]{2,1,0:T(8,128)(2,1)}, u32[]{:S(2)}, u32[]{:S(2)}) collective-permute-start(bf16[2,384,256]{2,1,0:T(8,128)(2,1)} %collective-permute-done.9), channel_id=1, source_target_pairs={{1,0},{2,1},{3,2},{4,3},{5,4},{6,5},{7,6},{8,7},{9,8},{10,9},{11,1... | collective-permute-start | bytes 1179656 | tf_op jit(solution)/shard_map/ppermute | solution.py:20
  168.3 7.2 %collective-permute-start.22 = (bf16[2,384,256]{2,1,0:T(8,128)(2,1)}, bf16[2,384,256]{2,1,0:T(8,128)(2,1)}, u32[]{:S(2)}, u32[]{:S(2)}) collective-permute-start(bf16[2,384,256]{2,1,0:T(8,128)(2,1)} %collective-permute-done.21), channel_id=1, source_target_pairs={{1,0},{2,1},{3,2},{4,3},{5,4},{6,5},{7,6},{8,7},{9,8},{10,9},{11,1... | collective-permute-start | bytes 1179656 | tf_op jit(solution)/shard_map/ppermute | solution.py:20
  175.8 10.1 %collective-permute-done.10 = bf16[2,384,256]{2,1,0:T(8,128)(2,1)} collective-permute-done((bf16[2,384,256]{2,1,0:T(8,128)(2,1)}, bf16[2,384,256]{2,1,0:T(8,128)(2,1)}, u32[]{:S(2)}, u32[]{:S(2)}) %collective-permute-start.10) | collective-permute-done | bytes 393248 | tf_op jit(solution)/shard_map/ppermute | solution.py:20
  185.9 7.9 %collective-permute-start.11 = (bf16[2,384,256]{2,1,0:T(8,128)(2,1)}, bf16[2,384,256]{2,1,0:T(8,128)(2,1)S(1)}, u32[]{:S(2)}, u32[]{:S(2)}) collective-permute-start(bf16[2,384,256]{2,1,0:T(8,128)(2,1)} %collective-permute-done.10), channel_id=1, source_target_pairs={{1,0},{2,1},{3,2},{4,3},{5,4},{6,5},{7,6},{8,7},{9,8},{10,9},{11,1... | collective-permute-start | bytes 1179656 | tf_op jit(solution)/shard_map/ppermute | solution.py:20
  193.8 8.9 %collective-permute-done.22 = bf16[2,384,256]{2,1,0:T(8,128)(2,1)} collective-permute-done((bf16[2,384,256]{2,1,0:T(8,128)(2,1)}, bf16[2,384,256]{2,1,0:T(8,128)(2,1)}, u32[]{:S(2)}, u32[]{:S(2)}) %collective-permute-start.22) | collective-permute-done | bytes 393248 | tf_op jit(solution)/shard_map/ppermute | solution.py:20
  202.7 7.9 %collective-permute-start.23 = (bf16[2,384,256]{2,1,0:T(8,128)(2,1)}, bf16[2,384,256]{2,1,0:T(8,128)(2,1)S(1)}, u32[]{:S(2)}, u32[]{:S(2)}) collective-permute-start(bf16[2,384,256]{2,1,0:T(8,128)(2,1)} %collective-permute-done.22), channel_id=1, source_target_pairs={{1,0},{2,1},{3,2},{4,3},{5,4},{6,5},{7,6},{8,7},{9,8},{10,9},{11,1... | collective-permute-start | bytes 1179656 | tf_op jit(solution)/shard_map/ppermute | solution.py:20
  210.7 1.8 constant_dynamic-update-slice_fusion.25
  212.5 1.8 constant_dynamic-update-slice_fusion.24
  214.3 1.8 constant_dynamic-update-slice_fusion.23
  216.1 1.8 constant_dynamic-update-slice_fusion.22
  217.8 1.8 constant_dynamic-update-slice_fusion.21
  219.6 1.8 constant_dynamic-update-slice_fusion.20
  221.5 1.1 constant_dynamic-update-slice_fusion.11
  222.5 1.0 constant_dynamic-update-slice_fusion.10
  223.6 1.0 constant_dynamic-update-slice_fusion.9
  225.6 1.0 constant_dynamic-update-slice_fusion.3
  230.2 1.8 constant_dynamic-update-slice_fusion.16
  232.0 1.8 constant_dynamic-update-slice_fusion.15
  233.8 1.8 constant_dynamic-update-slice_fusion.14
  235.6 2.2 copy-done.9
  238.6 27.5 %convolution_convert_fusion = bf16[468,16384]{1,0:T(8,128)(2,1)S(1)} fusion(f32[468,384]{1,0:T(8,128)S(1)} %mul.53, bf16[48,8,128,128]{3,2,1,0:T(8,128)(2,1)} %bitcast.92), kind=kOutput, calls=%fused_computation | convolution fusion | flops 35340484608 | bytes 28637184 | tf_op jit(solution)/shard_map/dot_general | solution.py:60
  266.1 4.1 %fusion.29 = (bf16[234,16384]{1,0:T(8,128)(2,1)}, bf16[234,16384]{1,0:T(8,128)(2,1)S(1)}) fusion(bf16[468,16384]{1,0:T(8,128)(2,1)S(1)} %convolution_convert_fusion), kind=kLoop, calls=%fused_computation.70 | loop fusion | bytes 30670848 | tf_op jit(solution)/shard_map/slice | solution.py:71
  270.2 8.7 %copy.24 = bf16[30,8,128,128]{3,2,1,0:T(8,128)(2,1)} copy(bf16[30,8,128,128]{3,1,2,0:T(8,128)(2,1)} %bitcast.78) | data formatting | bytes 15728640
  278.9 9.6 %slice.60 = bf16[234,128,128]{2,1,0:T(8,128)(2,1)} slice(bf16[240,128,128]{2,1,0:T(8,128)(2,1)} %bitcast.79), slice={[0:234], [0:128], [0:128]} | slice | bytes 15335424
  288.5 5.5 %copy.25 = bf16[30,8,128,128]{3,2,1,0:T(8,128)(2,1)} copy(bf16[30,8,128,128]{3,1,2,0:T(8,128)(2,1)S(1)} %bitcast.77) | data formatting | bytes 15728640
  293.9 4.9 %slice.61 = bf16[234,128,128]{2,1,0:T(8,128)(2,1)S(1)} slice(bf16[240,128,128]{2,1,0:T(8,128)(2,1)} %bitcast.80), slice={[0:234], [0:128], [0:128]} | slice | bytes 15335424
  298.8 7.4 %fusion.6 = f32[2,3,128,2,256]{4,2,3,1,0:T(8,128)S(1)} fusion(bf16[2,39,128,256,1,1]{3,2,1,0,5,4:T(8,128)(2,1)} %bitcast.88, bf16[2,3,39,128,128,1]{4,3,2,1,0,5:T(8,128)(2,1)} %bitcast.82), kind=kOutput, calls=%fused_computation.8 | convolution fusion | flops 3925868544 | bytes 14352384 | tf_op jit(solution)/shard_map/ptwab,qwbv->ptaqv/dot_general | solution.py:85
  306.3 6.2 %fusion.9 = f32[2,3,128,2,256]{4,2,3,1,0:T(8,128)S(1)} fusion(bf16[2,39,128,256,1,1]{3,2,1,0,5,4:T(8,128)(2,1)} %bitcast.24, bf16[2,3,39,128,128,1]{4,3,2,1,0,5:T(8,128)(2,1)S(1)} %bitcast.81), kind=kOutput, calls=%fused_computation.9 | convolution fusion | flops 3925868544 | bytes 14352384 | tf_op jit(solution)/shard_map/ptwab,qwbv->ptaqv/dot_general | solution.py:85
  312.6 1.2 maximum_maximum_fusion
  (77 shorter events, 9.1 us)
Async XLA Ops:
  6.5 232.1 %all-gather.3.cloned.1.call-start = ((), (), s32[]{:S(2)}) async-start(), calls=%async_computation | async-start | bytes 15728640 | tf_op jit(solution)/shard_map/all_gather | solution.py:37
  8.4 18.4 %collective-permute-start.12 = (bf16[2,384,256]{2,1,0:T(8,128)(2,1)S(1)}, bf16[2,384,256]{2,1,0:T(8,128)(2,1)S(1)}, u32[]{:S(2)}, u32[]{:S(2)}) collective-permute-start(bf16[2,384,256]{2,1,0:T(8,128)(2,1)S(1)} %get-tuple-element.16), channel_id=1, source_target_pairs={{31,0},{0,1},{1,2},{2,3},{3,4},{4,5},{5,6},{6,7},{7,8},{8,9},{9,10... | collective-permute-start | bytes 1179656 | tf_op jit(solution)/shard_map/ppermute | solution.py:20
  11.0 15.9 %collective-permute-start.6 = (bf16[2,384,256]{2,1,0:T(8,128)(2,1)S(1)}, bf16[2,384,256]{2,1,0:T(8,128)(2,1)S(1)}, u32[]{:S(2)}, u32[]{:S(2)}) collective-permute-start(bf16[2,384,256]{2,1,0:T(8,128)(2,1)S(1)} %get-tuple-element.15), channel_id=1, source_target_pairs={{1,0},{2,1},{3,2},{4,3},{5,4},{6,5},{7,6},{8,7},{9,8},{10,9},{11,1... | collective-permute-start | bytes 1179656 | tf_op jit(solution)/shard_map/ppermute | solution.py:20
  18.1 17.9 %collective-permute-start = (bf16[2,384,256]{2,1,0:T(8,128)(2,1)S(1)}, bf16[2,384,256]{2,1,0:T(8,128)(2,1)S(1)}, u32[]{:S(2)}, u32[]{:S(2)}) collective-permute-start(bf16[2,384,256]{2,1,0:T(8,128)(2,1)S(1)} %get-tuple-element.15), channel_id=1, source_target_pairs={{31,0},{0,1},{1,2},{2,3},{3,4},{4,5},{5,6},{6,7},{7,8},{8,9},{9,10... | collective-permute-start | bytes 1179656 | tf_op jit(solution)/shard_map/ppermute | solution.py:20
  18.1 24.1 %collective-permute-start.18 = (bf16[2,384,256]{2,1,0:T(8,128)(2,1)S(1)}, bf16[2,384,256]{2,1,0:T(8,128)(2,1)S(1)}, u32[]{:S(2)}, u32[]{:S(2)}) collective-permute-start(bf16[2,384,256]{2,1,0:T(8,128)(2,1)S(1)} %get-tuple-element.16), channel_id=1, source_target_pairs={{1,0},{2,1},{3,2},{4,3},{5,4},{6,5},{7,6},{8,7},{9,8},{10,9},{11,1... | collective-permute-start | bytes 1179656 | tf_op jit(solution)/shard_map/ppermute | solution.py:20
  26.8 148.6 %copy-start.5 = (bf16[2,384,256]{2,1,0:T(8,128)(2,1)}, bf16[2,384,256]{2,1,0:T(8,128)(2,1)S(1)}, u32[]{:S(2)}) copy-start(bf16[2,384,256]{2,1,0:T(8,128)(2,1)S(1)} %collective-permute-done.12) | copy-start | bytes 1179652
  26.8 26.0 %collective-permute-start.13 = (bf16[2,384,256]{2,1,0:T(8,128)(2,1)S(1)}, bf16[2,384,256]{2,1,0:T(8,128)(2,1)S(1)}, u32[]{:S(2)}, u32[]{:S(2)}) collective-permute-start(bf16[2,384,256]{2,1,0:T(8,128)(2,1)S(1)} %collective-permute-done.12), channel_id=1, source_target_pairs={{31,0},{0,1},{1,2},{2,3},{3,4},{4,5},{5,6},{6,7},{7,8},{8,9},{9,10... | collective-permute-start | bytes 1179656 | tf_op jit(solution)/shard_map/ppermute | solution.py:20
  26.8 49.6 %collective-permute-start.7 = (bf16[2,384,256]{2,1,0:T(8,128)(2,1)S(1)}, bf16[2,384,256]{2,1,0:T(8,128)(2,1)S(1)}, u32[]{:S(2)}, u32[]{:S(2)}) collective-permute-start(bf16[2,384,256]{2,1,0:T(8,128)(2,1)S(1)} %collective-permute-done.6), channel_id=1, source_target_pairs={{1,0},{2,1},{3,2},{4,3},{5,4},{6,5},{7,6},{8,7},{9,8},{10,9},{11,1... | collective-permute-start | bytes 1179656 | tf_op jit(solution)/shard_map/ppermute | solution.py:20
  36.0 52.0 %collective-permute-start.1 = (bf16[2,384,256]{2,1,0:T(8,128)(2,1)S(1)}, bf16[2,384,256]{2,1,0:T(8,128)(2,1)S(1)}, u32[]{:S(2)}, u32[]{:S(2)}) collective-permute-start(bf16[2,384,256]{2,1,0:T(8,128)(2,1)S(1)} %collective-permute-done), channel_id=1, source_target_pairs={{31,0},{0,1},{1,2},{2,3},{3,4},{4,5},{5,6},{6,7},{7,8},{8,9},{9,10... | collective-permute-start | bytes 1179656 | tf_op jit(solution)/shard_map/ppermute | solution.py:20
  42.2 45.7 %collective-permute-start.19 = (bf16[2,384,256]{2,1,0:T(8,128)(2,1)S(1)}, bf16[2,384,256]{2,1,0:T(8,128)(2,1)S(1)}, u32[]{:S(2)}, u32[]{:S(2)}) collective-permute-start(bf16[2,384,256]{2,1,0:T(8,128)(2,1)S(1)} %collective-permute-done.18), channel_id=1, source_target_pairs={{1,0},{2,1},{3,2},{4,3},{5,4},{6,5},{7,6},{8,7},{9,8},{10,9},{11,1... | collective-permute-start | bytes 1179656 | tf_op jit(solution)/shard_map/ppermute | solution.py:20
  52.8 122.8 %copy-start.8 = (bf16[2,384,256]{2,1,0:T(8,128)(2,1)}, bf16[2,384,256]{2,1,0:T(8,128)(2,1)S(1)}, u32[]{:S(2)}) copy-start(bf16[2,384,256]{2,1,0:T(8,128)(2,1)S(1)} %collective-permute-done.13) | copy-start | bytes 1179652
  52.8 42.4 %collective-permute-start.14 = (bf16[2,384,256]{2,1,0:T(8,128)(2,1)S(1)}, bf16[2,384,256]{2,1,0:T(8,128)(2,1)}, u32[]{:S(2)}, u32[]{:S(2)}) collective-permute-start(bf16[2,384,256]{2,1,0:T(8,128)(2,1)S(1)} %collective-permute-done.13), channel_id=1, source_target_pairs={{31,0},{0,1},{1,2},{2,3},{3,4},{4,5},{5,6},{6,7},{7,8},{8,9},{9,10... | collective-permute-start | bytes 1179656 | tf_op jit(solution)/shard_map/ppermute | solution.py:20
  76.4 99.2 %copy-start.1 = (bf16[2,384,256]{2,1,0:T(8,128)(2,1)}, bf16[2,384,256]{2,1,0:T(8,128)(2,1)S(1)}, u32[]{:S(2)}) copy-start(bf16[2,384,256]{2,1,0:T(8,128)(2,1)S(1)} %collective-permute-done.7) | copy-start | bytes 1179652
  76.4 28.0 %collective-permute-start.8 = (bf16[2,384,256]{2,1,0:T(8,128)(2,1)S(1)}, bf16[2,384,256]{2,1,0:T(8,128)(2,1)}, u32[]{:S(2)}, u32[]{:S(2)}) collective-permute-start(bf16[2,384,256]{2,1,0:T(8,128)(2,1)S(1)} %collective-permute-done.7), channel_id=1, source_target_pairs={{1,0},{2,1},{3,2},{4,3},{5,4},{6,5},{7,6},{8,7},{9,8},{10,9},{11,1... | collective-permute-start | bytes 1179656 | tf_op jit(solution)/shard_map/ppermute | solution.py:20
  88.0 87.5 %copy-start.6 = (bf16[2,384,256]{2,1,0:T(8,128)(2,1)}, bf16[2,384,256]{2,1,0:T(8,128)(2,1)S(1)}, u32[]{:S(2)}) copy-start(bf16[2,384,256]{2,1,0:T(8,128)(2,1)S(1)} %collective-permute-done.1) | copy-start | bytes 1179652
  88.0 24.5 %collective-permute-start.2 = (bf16[2,384,256]{2,1,0:T(8,128)(2,1)S(1)}, bf16[2,384,256]{2,1,0:T(8,128)(2,1)}, u32[]{:S(2)}, u32[]{:S(2)}) collective-permute-start(bf16[2,384,256]{2,1,0:T(8,128)(2,1)S(1)} %collective-permute-done.1), channel_id=1, source_target_pairs={{31,0},{0,1},{1,2},{2,3},{3,4},{4,5},{5,6},{6,7},{7,8},{8,9},{9,10... | collective-permute-start | bytes 1179656 | tf_op jit(solution)/shard_map/ppermute | solution.py:20
  88.0 87.7 %copy-start.3 = (bf16[2,384,256]{2,1,0:T(8,128)(2,1)}, bf16[2,384,256]{2,1,0:T(8,128)(2,1)S(1)}, u32[]{:S(2)}) copy-start(bf16[2,384,256]{2,1,0:T(8,128)(2,1)S(1)} %collective-permute-done.19) | copy-start | bytes 1179652
  88.0 33.2 %collective-permute-start.20 = (bf16[2,384,256]{2,1,0:T(8,128)(2,1)S(1)}, bf16[2,384,256]{2,1,0:T(8,128)(2,1)}, u32[]{:S(2)}, u32[]{:S(2)}) collective-permute-start(bf16[2,384,256]{2,1,0:T(8,128)(2,1)S(1)} %collective-permute-done.19), channel_id=1, source_target_pairs={{1,0},{2,1},{3,2},{4,3},{5,4},{6,5},{7,6},{8,7},{9,8},{10,9},{11,1... | collective-permute-start | bytes 1179656 | tf_op jit(solution)/shard_map/ppermute | solution.py:20
  95.2 34.1 %collective-permute-start.15 = (bf16[2,384,256]{2,1,0:T(8,128)(2,1)}, bf16[2,384,256]{2,1,0:T(8,128)(2,1)}, u32[]{:S(2)}, u32[]{:S(2)}) collective-permute-start(bf16[2,384,256]{2,1,0:T(8,128)(2,1)} %collective-permute-done.14), channel_id=1, source_target_pairs={{31,0},{0,1},{1,2},{2,3},{3,4},{4,5},{5,6},{6,7},{7,8},{8,9},{9,10... | collective-permute-start | bytes 1179656 | tf_op jit(solution)/shard_map/ppermute | solution.py:20
  104.4 55.8 %collective-permute-start.9 = (bf16[2,384,256]{2,1,0:T(8,128)(2,1)}, bf16[2,384,256]{2,1,0:T(8,128)(2,1)}, u32[]{:S(2)}, u32[]{:S(2)}) collective-permute-start(bf16[2,384,256]{2,1,0:T(8,128)(2,1)} %collective-permute-done.8), channel_id=1, source_target_pairs={{1,0},{2,1},{3,2},{4,3},{5,4},{6,5},{7,6},{8,7},{9,8},{10,9},{11,1... | collective-permute-start | bytes 1179656 | tf_op jit(solution)/shard_map/ppermute | solution.py:20
  112.4 55.8 %collective-permute-start.3 = (bf16[2,384,256]{2,1,0:T(8,128)(2,1)}, bf16[2,384,256]{2,1,0:T(8,128)(2,1)}, u32[]{:S(2)}, u32[]{:S(2)}) collective-permute-start(bf16[2,384,256]{2,1,0:T(8,128)(2,1)} %collective-permute-done.2), channel_id=1, source_target_pairs={{31,0},{0,1},{1,2},{2,3},{3,4},{4,5},{5,6},{6,7},{7,8},{8,9},{9,10... | collective-permute-start | bytes 1179656 | tf_op jit(solution)/shard_map/ppermute | solution.py:20
  121.2 47.0 %collective-permute-start.21 = (bf16[2,384,256]{2,1,0:T(8,128)(2,1)}, bf16[2,384,256]{2,1,0:T(8,128)(2,1)}, u32[]{:S(2)}, u32[]{:S(2)}) collective-permute-start(bf16[2,384,256]{2,1,0:T(8,128)(2,1)} %collective-permute-done.20), channel_id=1, source_target_pairs={{1,0},{2,1},{3,2},{4,3},{5,4},{6,5},{7,6},{8,7},{9,8},{10,9},{11,1... | collective-permute-start | bytes 1179656 | tf_op jit(solution)/shard_map/ppermute | solution.py:20
  129.3 46.2 %collective-permute-start.16 = (bf16[2,384,256]{2,1,0:T(8,128)(2,1)}, bf16[2,384,256]{2,1,0:T(8,128)(2,1)}, u32[]{:S(2)}, u32[]{:S(2)}) collective-permute-start(bf16[2,384,256]{2,1,0:T(8,128)(2,1)} %collective-permute-done.15), channel_id=1, source_target_pairs={{31,0},{0,1},{1,2},{2,3},{3,4},{4,5},{5,6},{6,7},{7,8},{8,9},{9,10... | collective-permute-start | bytes 1179656 | tf_op jit(solution)/shard_map/ppermute | solution.py:20
  160.2 25.7 %collective-permute-start.10 = (bf16[2,384,256]{2,1,0:T(8,128)(2,1)}, bf16[2,384,256]{2,1,0:T(8,128)(2,1)}, u32[]{:S(2)}, u32[]{:S(2)}) collective-permute-start(bf16[2,384,256]{2,1,0:T(8,128)(2,1)} %collective-permute-done.9), channel_id=1, source_target_pairs={{1,0},{2,1},{3,2},{4,3},{5,4},{6,5},{7,6},{8,7},{9,8},{10,9},{11,1... | collective-permute-start | bytes 1179656 | tf_op jit(solution)/shard_map/ppermute | solution.py:20
  168.2 25.6 %collective-permute-start.4 = (bf16[2,384,256]{2,1,0:T(8,128)(2,1)}, bf16[2,384,256]{2,1,0:T(8,128)(2,1)}, u32[]{:S(2)}, u32[]{:S(2)}) collective-permute-start(bf16[2,384,256]{2,1,0:T(8,128)(2,1)} %collective-permute-done.3), channel_id=1, source_target_pairs={{31,0},{0,1},{1,2},{2,3},{3,4},{4,5},{5,6},{6,7},{7,8},{8,9},{9,10... | collective-permute-start | bytes 1179656 | tf_op jit(solution)/shard_map/ppermute | solution.py:20
  168.3 34.5 %collective-permute-start.22 = (bf16[2,384,256]{2,1,0:T(8,128)(2,1)}, bf16[2,384,256]{2,1,0:T(8,128)(2,1)}, u32[]{:S(2)}, u32[]{:S(2)}) collective-permute-start(bf16[2,384,256]{2,1,0:T(8,128)(2,1)} %collective-permute-done.21), channel_id=1, source_target_pairs={{1,0},{2,1},{3,2},{4,3},{5,4},{6,5},{7,6},{8,7},{9,8},{10,9},{11,1... | collective-permute-start | bytes 1179656 | tf_op jit(solution)/shard_map/ppermute | solution.py:20
  175.4 35.2 %collective-permute-start.17 = (bf16[2,384,256]{2,1,0:T(8,128)(2,1)}, bf16[2,384,256]{2,1,0:T(8,128)(2,1)}, u32[]{:S(2)}, u32[]{:S(2)}) collective-permute-start(bf16[2,384,256]{2,1,0:T(8,128)(2,1)} %collective-permute-done.16), channel_id=1, source_target_pairs={{31,0},{0,1},{1,2},{2,3},{3,4},{4,5},{5,6},{6,7},{7,8},{8,9},{9,10... | collective-permute-start | bytes 1179656 | tf_op jit(solution)/shard_map/ppermute | solution.py:20
  175.7 49.0 %copy-start = (bf16[2,2,384,256]{3,2,1,0:T(8,128)(2,1)S(1)}, bf16[2,2,384,256]{3,2,1,0:T(8,128)(2,1)}, u32[]{:S(2)}) copy-start(bf16[2,2,384,256]{3,2,1,0:T(8,128)(2,1)} %param.13) | copy-start | bytes 2359300
  175.8 48.8 %copy-start.7 = (bf16[2,384,256]{2,1,0:T(8,128)(2,1)S(1)}, bf16[2,384,256]{2,1,0:T(8,128)(2,1)}, u32[]{:S(2)}) copy-start(bf16[2,384,256]{2,1,0:T(8,128)(2,1)} %copy-done.6) | copy-start | bytes 1179652
  185.9 49.7 %collective-permute-start.11 = (bf16[2,384,256]{2,1,0:T(8,128)(2,1)}, bf16[2,384,256]{2,1,0:T(8,128)(2,1)S(1)}, u32[]{:S(2)}, u32[]{:S(2)}) collective-permute-start(bf16[2,384,256]{2,1,0:T(8,128)(2,1)} %collective-permute-done.10), channel_id=1, source_target_pairs={{1,0},{2,1},{3,2},{4,3},{5,4},{6,5},{7,6},{8,7},{9,8},{10,9},{11,1... | collective-permute-start | bytes 1179656 | tf_op jit(solution)/shard_map/ppermute | solution.py:20
  193.8 27.6 %collective-permute-start.5 = (bf16[2,384,256]{2,1,0:T(8,128)(2,1)}, bf16[2,384,256]{2,1,0:T(8,128)(2,1)S(1)}, u32[]{:S(2)}, u32[]{:S(2)}) collective-permute-start(bf16[2,384,256]{2,1,0:T(8,128)(2,1)} %collective-permute-done.4), channel_id=1, source_target_pairs={{31,0},{0,1},{1,2},{2,3},{3,4},{4,5},{5,6},{6,7},{7,8},{8,9},{9,10... | collective-permute-start | bytes 1179656 | tf_op jit(solution)/shard_map/ppermute | solution.py:20
  202.7 32.9 %collective-permute-start.23 = (bf16[2,384,256]{2,1,0:T(8,128)(2,1)}, bf16[2,384,256]{2,1,0:T(8,128)(2,1)S(1)}, u32[]{:S(2)}, u32[]{:S(2)}) collective-permute-start(bf16[2,384,256]{2,1,0:T(8,128)(2,1)} %collective-permute-done.22), channel_id=1, source_target_pairs={{1,0},{2,1},{3,2},{4,3},{5,4},{6,5},{7,6},{8,7},{9,8},{10,9},{11,1... | collective-permute-start | bytes 1179656 | tf_op jit(solution)/shard_map/ppermute | solution.py:20
  214.3 11.3 %copy-start.2 = (bf16[2,384,256]{2,1,0:T(8,128)(2,1)S(1)}, bf16[2,384,256]{2,1,0:T(8,128)(2,1)}, u32[]{:S(2)}) copy-start(bf16[2,384,256]{2,1,0:T(8,128)(2,1)} %copy-done.1) | copy-start | bytes 1179652
  221.4 8.0 %copy-start.4 = (bf16[2,384,256]{2,1,0:T(8,128)(2,1)S(1)}, bf16[2,384,256]{2,1,0:T(8,128)(2,1)}, u32[]{:S(2)}) copy-start(bf16[2,384,256]{2,1,0:T(8,128)(2,1)} %copy-done.3) | copy-start | bytes 1179652
  235.6 2.2 copy-start.9
Sparse Core Ops, SparseCore 0:
  9.0 198.3 all-gather.2
where the time goes:
time: 322 us; the launch traced here: 321 us
  starting transfers between devices  97.8 us (30%)
  local copies, waits for them, and re-layouts  64.7 us (20%)
  blocking collectives  50.9 us (16%)
  waiting for transfers between devices  49.4 us (15%)
  matrix products  41.2 us (13%)
  between operations  14.3 us (4%)
    ppermute x24, starting transfers between devices, passed_along(): return lax.ppermute(block, axis, route)  97.8 us
    unnamed x51, local copies, waits for them, and re-layouts  57.7 us
    ppermute x24, waiting for transfers between devices, passed_along(): return lax.ppermute(block, axis, route)  48.7 us
    all_gather x1, blocking collectives, side_by_side(): filled = lax.all_gather(both, axis, axis=dim, tiled=True)  30.1 us
    dot_general x1, matrix products, body(): jnp.dot(build_weights, tiles_flat, precision=lax.Precision.HIGHEST, prefe...  27.5 us
    unnamed x1, blocking collectives  20.8 us
    dot_general x2, matrix products, body(): jnp.einsum('ptwab,qwbv->ptaqv', matrix, window, preferred_element_type=jn...  13.6 us
  transfers between devices with their start and end apart: 25, of which 8 were waited for; matrix products, arithmetic and copies ran while one was open for 10% of the time, Pallas kernels for 0%

commit v1 on v0

v1 whole, which is shorter than its diff:
```python
import functools

import jax
import jax.numpy as jnp
from jax import lax
from jax.experimental import pallas as pl
from jax.experimental.pallas import tpu as pltpu
from jax.sharding import PartitionSpec as P

MESH = pl.DeviceIdType.MESH
BAND = 16
NLAT = 9
TS = 128
NV = 256
TR = 3
BLK = TR * TS
SLOTS = 96
CHUNKS = 8
PER = SLOTS // CHUNKS
WIDE = 2 * BAND + 1
SPAN = WIDE + TR - 1
TORB = 96
HALVES = (0, 1)


class Net:
    def __init__(self, send_sem, recv_sem):
        self.send_sem, self.recv_sem = send_sem, recv_sem
        self.index, self.sent = {}, []

    def copy(self, name, src, dst, device):
        at = self.index.setdefault(name, len(self.index))
        return pltpu.make_async_remote_copy(
            src_ref=src, dst_ref=dst, send_sem=self.send_sem.at[at], recv_sem=self.recv_sem.at[at],
            device_id=device, device_id_type=MESH,
        )

    def send(self, name, when, src, dst, device):
        copy = self.copy(name, src, dst, device)
        self.sent.append((when, copy))
        guarded(when, copy.start)

    def recv(self, name, when, dst, device):
        guarded(when, self.copy(name, dst, dst, device).wait_recv)

    def finish(self):
        for when, copy in self.sent:
            guarded(when, copy.wait_send)


def guarded(when, action):
    if when is None:
        action()
    else:
        pl.when(when)(action)


def gather_kernel(hop, coords, vec, G, W, C, S, X, E, send_sem, recv_sem, local_sem):
    ka = lax.axis_index("ka")
    row = lax.axis_index("rows")
    xh, y, z = row // 16, (row // 4) % 4, row % 4
    zp, zm, z2 = (z + 1) % 4, (z + 3) % 4, (z + 2) % 4
    yp, ym = (y + 1) % 4, (y + 3) % 4

    def at(h, i, j):
        return (ka, h * 16 + i * 4 + j)

    def along(flip):
        other = (1 - ka % 2) if flip % 2 else ka % 2
        pair = (1 - ka // 2) if flip // 2 else ka // 2
        return (pair * 2 + other, row)

    up_z, down_z, up_y, down_y = at(xh, y, zp), at(xh, y, zm), at(xh, yp, z), at(xh, ym, z)
    mirror = at(1 - xh, y, z)
    peers = [along(1), along(2), along(3), up_z, down_z, up_y, down_y, mirror]
    barrier = pltpu.get_barrier_semaphore()
    for peer in peers:
        pl.semaphore_signal(barrier, inc=1, device_id=peer, device_id_type=MESH)
    first_part = (y == 1) & (z == 1)
    last_part = (y == 2) & (z == 2)
    first_hold = (y == 1) & (z == 0)
    last_hold = (y == 2) & (z == 3)
    part_sender, part_holder = first_part | last_part, first_hold | last_hold
    part_to = at(1 - xh, y, jnp.where(y == 1, 0, 3))
    part_from = at(1 - xh, y, jnp.where(y == 1, 1, 2))

    @pl.when(part_sender)
    def _():
        pl.semaphore_signal(barrier, inc=1, device_id=part_to, device_id_type=MESH)

    @pl.when(part_holder)
    def _():
        pl.semaphore_signal(barrier, inc=1, device_id=part_from, device_id_type=MESH)

    pl.semaphore_wait(barrier, len(peers) + jnp.where(part_sender | part_holder, 1, 0))

    net = Net(send_sem, recv_sem)
    send, recv = net.send, net.recv
    edge = (y == 0) | (y == 3)
    mirrored = edge | part_holder
    low, high = z == 0, z == 3
    rim = low | high
    tail = pl.ds(pl.multiple_of(jnp.where(low, 0, 2 * TS), TS), TS)
    side = pl.ds(pl.multiple_of(jnp.where(y == 1, 0, 2 * TS), TS), TS)
    HEAD, LAST = pl.ds(0, TS), pl.ds(2 * TS, TS)

    local = pltpu.make_async_copy(coords, C.at[0], local_sem)
    local.start()
    for flip in (1, 2, 3):
        send(f"c{flip}", None, coords, C.at[flip], along(flip))
    for h in HALVES:
        send(f"m{h}", mirrored, vec.at[h], S.at[z, h], mirror)
    for h in HALVES:
        send(f"mp{h}", part_sender, vec.at[h, :, side], S.at[z, h, :, side], part_to)

    def z_own(u, h):
        if u < 0:
            send(f"z-{h}", None, vec.at[h], W.at[6 + z - zp, h], up_z)
        else:
            send(f"z+{h}", None, vec.at[h], W.at[6 + z - zm, h], down_z)

    def z_shadow(u, h):
        if u < 0:
            send(f"s-{h}", edge, S.at[z, h], S.at[z, h], up_z)
        else:
            send(f"s+{h}", edge, S.at[z, h], S.at[z, h], down_z)

    member = {0: z, -1: zm, 1: zp, 2: z2}

    def y_copies(u, h, shadow):
        m = member[u]
        dz = m - z
        if shadow:
            src = S.at[m, h]
            down_ok, up_ok = y == 0, y == 3
        else:
            src = vec.at[h] if u == 0 else W.at[6 + dz, h]
            down_ok, up_ok = y > 0, y < 3
        down_dst, up_dst = W.at[10 + dz, h], W.at[2 + dz, h]
        if u == 0:
            send(f"y-{u}{h}", down_ok, src, down_dst, down_y)
            send(f"y+{u}{h}", up_ok, src, up_dst, up_y)
        elif u == -1:
            send(f"y-{u}{h}", down_ok & (z != 0), src, down_dst, down_y)
            send(f"y+{u}{h}", up_ok, src, up_dst, up_y)
        elif u == 1:
            send(f"y-{u}{h}", down_ok, src, down_dst, down_y)
            send(f"y+{u}{h}", up_ok & (z != 3), src, up_dst, up_y)
        else:
            send(f"y-{u}{h}", down_ok & (z >= 2), src, down_dst, down_y)
            send(f"y-{u}{h}", down_ok & (z < 2), src.at[:, HEAD], down_dst.at[:, HEAD], down_y)
            send(f"y+{u}{h}", up_ok & (z < 2), src, up_dst, up_y)
            send(f"y+{u}{h}", up_ok & (z >= 2), src.at[:, LAST], up_dst.at[:, LAST], up_y)

    def y_arrived(u, h):
        dz = member[u] - z
        down_dst, up_dst = W.at[10 + dz, h], W.at[2 + dz, h]
        if u == 2:
            recv(f"y-{u}{h}", z >= 2, down_dst, up_y)
            recv(f"y-{u}{h}", z < 2, down_dst.at[:, HEAD], up_y)
            recv(f"y+{u}{h}", z < 2, up_dst, down_y)
            recv(f"y+{u}{h}", z >= 2, up_dst.at[:, LAST], down_y)
        else:
            recv(f"y-{u}{h}", (z != 0) if u == -1 else None, down_dst, up_y)
            recv(f"y+{u}{h}", (z != 3) if u == 1 else None, up_dst, down_y)

    z_own(-1, 0)
    z_own(1, 1)
    for h in HALVES:
        y_copies(0, h, False)
    for c in range(CHUNKS):
        part = pl.ds(c * PER, PER)
        send(f"x{c}", None, hop.at[part], G.at[1, part], along(2))
    send("sib", None, hop, G.at[0], along(1))

    recv("m0", mirrored, S.at[z, 0], mirror)
    z_shadow(-1, 0)
    z_own(-1, 1)
    z_own(1, 0)
    z_shadow(1, 0)
    y_copies(0, 0, True)
    recv("z-0", None, W.at[6 + zm - z, 0], down_z)
    send("w0", None, W.at[6 + zm - z, 0], W.at[6 + zm - zp, 0], up_z)
    y_copies(-1, 0, False)
    recv("z+1", None, W.at[6 + zp - z, 1], up_z)
    send("w1", None, W.at[6 + zp - z, 1], W.at[6 + zp - zm, 1], down_z)
    y_copies(1, 1, False)
    y_near = jnp.where(low, ym, yp)
    near = at(xh, y_near, z)
    near_src = at(xh, jnp.where(low, yp, ym), z)
    hold = jnp.where(y == 1, 0, 3)
    hold_part = jnp.where(y == 1, 1, 2)
    hold_to = at(xh, jnp.where(y == 1, 0, 3), z)
    hold_from = at(xh, jnp.where(y == 0, 1, 2), z)
    relay_rim = ((y == 0) & low) | ((y == 3) & high)
    real_rim = (low & (y > 0)) | (high & (y < 3))
    send("e0", part_holder, S.at[hold, 0], E.at[0, 0], hold_to)

    recv("m1", mirrored, S.at[z, 1], mirror)
    z_shadow(1, 1)
    z_shadow(-1, 1)
    y_copies(0, 1, True)
    send("e1", part_holder, S.at[hold, 1], E.at[0, 1], hold_to)
    recv("z-1", None, W.at[6 + zm - z, 1], down_z)
    y_copies(-1, 1, False)
    recv("z+0", None, W.at[6 + zp - z, 0], up_z)
    y_copies(1, 0, False)
    for h in HALVES:
        recv(f"mp{h}", part_holder, S.at[hold_part, h, :, side], part_from)
        send(f"ep{h}", part_holder, S.at[hold_part, h, :, side], E.at[1, h, :, side], hold_to)

    block = jnp.where(low, 10, 2)
    beside = jnp.where(low, 11, 1)
    for h in HALVES:
        y_arrived(0, h)
        send(f"d{h}", real_rim, W.at[block, h], X.at[0, h], near)
    recv("w0", None, W.at[6 + z2 - z, 0], down_z)
    y_copies(2, 0, False)
    recv("w1", None, W.at[6 + z2 - z, 1], up_z)
    y_copies(2, 1, False)
    recv("s-0", edge, S.at[zm, 0], down_z)
    send("v0", edge, S.at[zm, 0], S.at[zm, 0], up_z)
    y_copies(-1, 0, True)
    recv("s+0", edge, S.at[zp, 0], up_z)
    y_copies(1, 0, True)
    for h in HALVES:
        recv(f"e{h}", relay_rim, E.at[0, h], hold_from)
        send(f"d{h}", relay_rim, E.at[0, h], X.at[0, h], near)
    recv("s+1", edge, S.at[zp, 1], up_z)
    send("v1", edge, S.at[zp, 1], S.at[zp, 1], down_z)
    y_copies(1, 1, True)
    recv("s-1", edge, S.at[zm, 1], down_z)
    y_copies(-1, 1, True)
    for h in HALVES:
        recv(f"ep{h}", relay_rim, E.at[1, h, :, tail], hold_from)
        send(f"dp{h}", relay_rim, E.at[1, h, :, tail], X.at[1, h, :, tail], near)
    rim_to = at(xh, y, jnp.where(low, 3, 0))
    far = jnp.where(low, 11, 1)
    far_part = jnp.where(low, 12, 0)
    for h in HALVES:
        recv(f"d{h}", rim, X.at[0, h], near_src)
        send(f"f{h}", rim, X.at[0, h], W.at[far, h], rim_to)
    for h in HALVES:
        y_arrived(1, h)
        y_arrived(-1, h)
        send(f"dp{h}", real_rim, W.at[beside, h, :, tail], X.at[1, h, :, tail], near)
    recv("v0", edge, S.at[z2, 0], down_z)
    y_copies(2, 0, True)
    recv("v1", edge, S.at[z2, 1], up_z)
    y_copies(2, 1, True)

    def forward(c):
        part = pl.ds(c * PER, PER)
        recv(f"x{c}", None, G.at[1, part], along(2))
        send(f"o{c}", None, G.at[1, part], G.at[2, part], along(1))

    for c in range(3):
        forward(c)
    for h in HALVES:
        recv(f"dp{h}", rim, X.at[1, h, :, tail], near_src)
        send(f"fp{h}", rim, X.at[1, h, :, tail], W.at[far_part, h, :, tail], rim_to)
    forward(3)
    got = jnp.where(low, 1, 11)
    got_part = jnp.where(low, 0, 12)
    got_tail = pl.ds(pl.multiple_of(jnp.where(low, 2 * TS, 0), TS), TS)
    next_to = at(xh, y, jnp.where(low, 1, 2))
    for h in HALVES:
        recv(f"f{h}", rim, W.at[got, h], rim_to)
        send(f"l{h}", rim, W.at[got, h, :, got_tail], W.at[got_part, h, :, got_tail], next_to)
    for c in range(4, CHUNKS - 1):
        forward(c)
    inner = (z == 1) | (z == 2)
    inner_part = jnp.where(z == 1, 0, 12)
    inner_tail = pl.ds(pl.multiple_of(jnp.where(z == 1, 2 * TS, 0), TS), TS)
    inner_from = at(xh, y, jnp.where(z == 1, 0, 3))
    for h in HALVES:
        y_arrived(2, h)
        recv(f"fp{h}", rim, W.at[got_part, h, :, got_tail], rim_to)
        recv(f"l{h}", inner, W.at[inner_part, h, :, inner_tail], inner_from)
    for flip in (1, 2, 3):
        recv(f"c{flip}", None, C.at[flip], along(flip))
    recv("sib", None, G.at[0], along(1))
    forward(CHUNKS - 1)
    for c in range(CHUNKS):
        recv(f"o{c}", None, G.at[2, pl.ds(c * PER, PER)], along(1))
    net.finish()
    local.wait()


def gather_all(hop, coords, vec):
    block = vec.shape
    any_space = pl.BlockSpec(memory_space=pl.ANY)
    sems = 80
    return pl.pallas_call(
        gather_kernel,
        out_shape=(
            jax.ShapeDtypeStruct((3,) + hop.shape, hop.dtype),
            jax.ShapeDtypeStruct((13,) + block, vec.dtype),
            jax.ShapeDtypeStruct((4,) + coords.shape, coords.dtype),
            jax.ShapeDtypeStruct((4,) + block, vec.dtype),
            jax.ShapeDtypeStruct((2,) + block, vec.dtype),
            jax.ShapeDtypeStruct((2,) + block, vec.dtype),
        ),
        in_specs=[any_space] * 3,
        out_specs=(any_space,) * 6,
        scratch_shapes=[
            pltpu.SemaphoreType.DMA((sems,)),
            pltpu.SemaphoreType.DMA((sems,)),
            pltpu.SemaphoreType.DMA,
        ],
        compiler_params=pltpu.CompilerParams(collective_id=0, has_side_effects=True),
        name="gather",
    )(hop, coords, vec)[:3]


def product_kernel(C, table, hop, G, vec, W, out, T, V, H, head, chain, sems):
    row = lax.axis_index("rows")
    copies = [pltpu.make_async_copy(hop, T.at[pl.ds(0, SLOTS)], sems.at[0])]
    for m in range(3):
        copies.append(
            pltpu.make_async_copy(G.at[m], T.at[pl.ds((m + 1) * SLOTS, SLOTS)], sems.at[m + 1])
        )
    windows = []
    for j in range(13):
        for q in range(2):
            lanes = pl.ds(q * NV, NV)
            if j == 0:
                src, start, size = W.at[j, :, q, pl.ds(2 * TS, TS)], 0, TS
            elif j == 12:
                src, start, size = W.at[j, :, q, pl.ds(0, TS)], (SPAN - 1) * TS, TS
            else:
                src = vec.at[:, q] if j == 6 else W.at[j, :, q]
                start, size = (TR * (j - 6) + BAND) * TS, BLK
            windows.append(
                pltpu.make_async_copy(src, V.at[:, pl.ds(start, size), lanes], sems.at[4 + 2 * j + q])
            )
    for copy in copies + windows:
        copy.start()

    def clear(b, _):
        head[b] = -1
        return 0

    lax.fori_loop(0, TR * WIDE, clear, 0)
    for m in range(4):

        def link(i, _, m=m):
            r = C[m, 0, i] - row * TR
            w = C[m, 1, i] - (row * TR + r - BAND)
            w = jnp.where(w < 0, w + TORB, w)
            w = jnp.where(w >= TORB, w - TORB, w)
            b = r * WIDE + w
            chain[m * SLOTS + i] = head[b]
            head[b] = m * SLOTS + i
            return 0

        lax.fori_loop(0, C[m, 3, 0], link, 0)
    for copy in copies:
        copy.wait()

    half = TS // 2

    def weights(s, ok):
        m = s // SLOTS
        lat = C[m, 2, s - m * SLOTS]
        return [jnp.where(ok, table[i, lat], 0.0) for i in range(4)]

    for r in range(TR):

        def build(w, _, r=r):
            cols = pl.ds(pl.multiple_of(w * TS, TS), TS)
            first = head[r * WIDE + w]
            for part in range(2):
                rows = pl.ds(part * half, half)

                def step(carry):
                    s, accs = carry[0], carry[1:]
                    s2 = chain[s]
                    ok = s2 >= 0
                    s2 = jnp.where(ok, s2, s)
                    after = jnp.where(ok, chain[s2], -1)
                    one = T[s, rows, :].astype(jnp.float32)
                    two = T[s2, rows, :].astype(jnp.float32)
                    w1, w2 = weights(s, True), weights(s2, ok)
                    return (after,) + tuple(
                        acc + (one * a + two * b) for acc, a, b in zip(accs, w1, w2)
                    )

                zero = jnp.zeros((half, TS), jnp.float32)
                res = lax.while_loop(lambda c: c[0] >= 0, step, (first, zero, zero, zero, zero))
                for k in range(2):
                    for p in range(2):
                        H[k, r, pl.ds(p * TS + part * half, half), cols] = res[1 + 2 * k + p].astype(
                            jnp.bfloat16
                        )
            return 0

        lax.fori_loop(0, WIDE, build, 0)
    for copy in windows:
        copy.wait()
    for k in range(2):
        for r in range(TR):
            o = jnp.dot(
                H[k, r], V[k, pl.ds(r * TS, WIDE * TS), :], preferred_element_type=jnp.float32
            )
            rows = pl.ds(r * TS, TS)
            out[k, 0, rows, :] = o[:TS, :NV] - o[TS:, NV:]
            out[k, 1, rows, :] = o[:TS, NV:] + o[TS:, :NV]


def product(C, table, hop, G, vec, W):
    any_space = pl.BlockSpec(memory_space=pl.ANY)
    smem = pl.BlockSpec(memory_space=pltpu.SMEM)
    return pl.pallas_call(
        product_kernel,
        out_shape=jax.ShapeDtypeStruct((2, 2, BLK, NV), jnp.float32),
        in_specs=[smem, smem] + [any_space] * 4,
        out_specs=pl.BlockSpec(memory_space=pltpu.VMEM),
        scratch_shapes=[
            pltpu.VMEM((4 * SLOTS, TS, TS), jnp.bfloat16),
            pltpu.VMEM((2, SPAN * TS, 2 * NV), jnp.bfloat16),
            pltpu.VMEM((2, TR, 2 * TS, WIDE * TS), jnp.bfloat16),
            pltpu.SMEM((128,), jnp.int32),
            pltpu.SMEM((4 * SLOTS,), jnp.int32),
            pltpu.SemaphoreType.DMA((30,)),
        ],
        compiler_params=pltpu.CompilerParams(vmem_limit_bytes=56 * 1024 * 1024),
        name="product",
    )(C, table, hop, G, vec, W)


def body(hoppings, tile_rows, tile_cols, tile_lats, tile_counts, phase_angle, vectors):
    hop = hoppings[0]
    counts = jnp.broadcast_to(tile_counts, (1, SLOTS))
    coords = jnp.concatenate([tile_rows, tile_cols, tile_lats, counts], axis=0)
    coords = jnp.pad(coords, ((0, 4), (0, 128 - SLOTS)))
    table = jnp.stack([jnp.cos(phase_angle), jnp.sin(phase_angle)], axis=1).reshape(4, NLAT)
    G, W, C = gather_all(hop, coords, vectors)
    return product(C, table, hop, G, vectors, W)


def solution(mesh):
    return jax.shard_map(
        body,
        mesh=mesh,
        in_specs=(
            P("rows", "ka", None, None),
            P("rows", "ka"),
            P("rows", "ka"),
            P("rows", "ka"),
            P("rows", "ka"),
            P("ka", None),
            P("ka", None, "rows", None),
        ),
        out_specs=P("ka", None, "rows", None),
        check_vma=False,
    )
```

time: 322 us -> 142 us (0.44)
  Pallas kernels: 0 us -> 137 us
  starting transfers between devices: 97.8 us -> 0 us
  local copies, waits for them, and re-layouts: 64.7 us -> 1.3 us
  blocking collectives: 50.9 us -> 0 us
  waiting for transfers between devices: 49.4 us -> 0 us
  matrix products: 41.2 us -> 0 us
  between operations: 14.3 us -> 0.69 us
    pallas_call x0 -> x2, Pallas kernels: none -> 137 us  [the longest x1 102 us: gather_all(): pl.pallas_call(gather_kernel, out_shape=(jax.ShapeDtypeStruct((3,) + hop....]
    ppermute x24 -> x0, starting transfers between devices: 97.8 us -> none  [passed_along(): return lax.ppermute(block, axis, route)]
    unnamed x51 -> x2, local copies, waits for them, and re-layouts: 57.7 us -> 0.01 us
    ppermute x24 -> x0, waiting for transfers between devices: 48.7 us -> none  [passed_along(): return lax.ppermute(block, axis, route)]
    dot_general x4 -> x0, matrix products: 41.2 us -> none  [the longest x1 27.5 us: body(): jnp.dot(build_weights, tiles_flat, precision=lax.Precision.HIGHEST, prefe...]
    all_gather x1 -> x0, blocking collectives: 30.1 us -> none  [side_by_side(): filled = lax.all_gather(both, axis, axis=dim, tiled=True)]
    unnamed x1 -> x0, blocking collectives: 20.8 us -> none
    slice x1 -> x0, local copies, waits for them, and re-layouts: 4.06 us -> none  [body(): matrix = matrices[kpoint]]
  transfers between devices with their start and end apart: 25 -> 0, of which waited for: 8 -> 0; matrix products, arithmetic and copies ran while one was open for 10% -> 0% of each run, Pallas kernels for 0% -> 0%
where the time goes in v1:
time: 142 us; the launch traced here: 139 us
  Pallas kernels  137 us (96%)
    pallas_call x1, Pallas kernels, gather_all(): pl.pallas_call(gather_kernel, out_shape=(jax.ShapeDtypeStruct((3,) + hop....  102 us
    pallas_call x1, Pallas kernels, product(): pl.pallas_call(product_kernel, out_shape=jax.ShapeDtypeStruct((2, 2, BLK,...  34.6 us

profile of v1, /device:TPU:1, one launch (start us, length us, event | category | flops | bytes accessed | tf_op | source)
XLA Modules:
  0.0 139.3 jit_solution(8451953993463069110)
XLA Ops:
  0.0 0.0 copy-start
  0.7 0.1 pad.10.clone
  0.7 0.8 add_add_fusion
  1.5 0.6 pad.4.coords
  2.1 102.0 %gather.1 = (bf16[3,96,128,128]{3,2,1,0:T(8,128)(2,1)}, bf16[13,2,2,384,256]{4,3,2,1,0:T(8,128)(2,1)}, s32[4,8,128]{2,1,0:T(8,128)}, bf16[4,2,2,384,256]{4,3,2,1...) custom-call(bf16[96,128,128]{2,1,0:T(8,128)(2,1)} %bitcast.10, ...), custom_call_target="tpu_custom_call" | custom-call | tf_op jit(solution)/shard_map/gather/pallas_call | solution.py:294
  104.1 0.0 copy-done
  104.1 0.6 copy.8
  104.7 34.6 %product.1 = f32[2,2,384,256]{3,2,1,0:T(8,128)} custom-call(s32[4,8,128]{2,1,0:T(8,128)} %get-tuple-element.8.C, f32[4,9]{1,0:T(4,128)} %bitcast.12, bf16[96,128,128]{2,1,0:T(8,128)(2,1)} %bitcast.11, bf16[3,96,128,128]{3,2,1,0:T(8,128)(2,1)} %get-tuple-element.9.G, bf16[2,2,384,256]{3,2,1,0:T(8,128)(2,1)} %vec.3, ...), custom_call_target="tpu_custom_call" | custom-call | tf_op jit(solution)/shard_map/product/pallas_call | solution.py:414
  (2 shorter events, 0.0 us)
Async XLA Ops:
  0.0 104.1 %copy-start = (f32[2,9]{1,0:T(2,128)S(1)}, f32[2,9]{1,0:T(2,128)}, u32[]{:S(2)}) copy-start(f32[2,9]{1,0:T(2,128)} %param.12) | copy-start | bytes 220

commit v2 on v1

--- a/solution.py
+++ b/solution.py
@@ -55,7 +55,7 @@
         pl.when(when)(action)
 
 
-def gather_kernel(hop, coords, vec, G, W, C, S, X, E, send_sem, recv_sem, local_sem):
+def gather_kernel(hop, rows, cols, lats, live, vec, G, W, CR, CC, CL, CN, S, X, E, send_sem, recv_sem, local_sem):
     ka = lax.axis_index("ka")
     row = lax.axis_index("rows")
     xh, y, z = row // 16, (row // 4) % 4, row % 4
@@ -104,10 +104,13 @@
     side = pl.ds(pl.multiple_of(jnp.where(y == 1, 0, 2 * TS), TS), TS)
     HEAD, LAST = pl.ds(0, TS), pl.ds(2 * TS, TS)
 
-    local = pltpu.make_async_copy(coords, C.at[0], local_sem)
-    local.start()
+    lists = ((rows, CR), (cols, CC), (lats, CL), (live, CN))
+    local = [pltpu.make_async_copy(src, dst.at[0], local_sem.at[i]) for i, (src, dst) in enumerate(lists)]
+    for copy in local:
+        copy.start()
     for flip in (1, 2, 3):
-        send(f"c{flip}", None, coords, C.at[flip], along(flip))
+        for i, (src, dst) in enumerate(lists):
+            send(f"c{flip}{i}", None, src, dst.at[flip], along(flip))
     for h in HALVES:
         send(f"m{h}", mirrored, vec.at[h], S.at[z, h], mirror)
     for h in HALVES:
@@ -278,42 +281,44 @@
         recv(f"fp{h}", rim, W.at[got_part, h, :, got_tail], rim_to)
         recv(f"l{h}", inner, W.at[inner_part, h, :, inner_tail], inner_from)
     for flip in (1, 2, 3):
-        recv(f"c{flip}", None, C.at[flip], along(flip))
+        for i, (_, dst) in enumerate(lists):
+            recv(f"c{flip}{i}", None, dst.at[flip], along(flip))
     recv("sib", None, G.at[0], along(1))
     forward(CHUNKS - 1)
     for c in range(CHUNKS):
         recv(f"o{c}", None, G.at[2, pl.ds(c * PER, PER)], along(1))
     net.finish()
-    local.wait()
-
-
-def gather_all(hop, coords, vec):
+    for copy in local:
+        copy.wait()
+
+
+def gather_all(hop, lists, vec):
     block = vec.shape
     any_space = pl.BlockSpec(memory_space=pl.ANY)
-    sems = 80
+    sems = 96
     return pl.pallas_call(
         gather_kernel,
         out_shape=(
             jax.ShapeDtypeStruct((3,) + hop.shape, hop.dtype),
             jax.ShapeDtypeStruct((13,) + block, vec.dtype),
-            jax.ShapeDtypeStruct((4,) + coords.shape, coords.dtype),
+            *[jax.ShapeDtypeStruct((4,) + a.shape, a.dtype) for a in lists],
             jax.ShapeDtypeStruct((4,) + block, vec.dtype),
             jax.ShapeDtypeStruct((2,) + block, vec.dtype),
             jax.ShapeDtypeStruct((2,) + block, vec.dtype),
         ),
-        in_specs=[any_space] * 3,
-        out_specs=(any_space,) * 6,
+        in_specs=[any_space] * 6,
+        out_specs=(any_space,) * 9,
         scratch_shapes=[
             pltpu.SemaphoreType.DMA((sems,)),
             pltpu.SemaphoreType.DMA((sems,)),
-            pltpu.SemaphoreType.DMA,
+            pltpu.SemaphoreType.DMA((4,)),
         ],
         compiler_params=pltpu.CompilerParams(collective_id=0, has_side_effects=True),
         name="gather",
-    )(hop, coords, vec)[:3]
-
-
-def product_kernel(C, table, hop, G, vec, W, out, T, V, H, head, chain, sems):
+    )(hop, *lists, vec)[:6]
+
+
+def product_kernel(cosine, sine, hop, G, vec, W, CR, CC, CL, CN, out, T, V, H, NR, NC, NL, NN, sems):
     row = lax.axis_index("rows")
     copies = [pltpu.make_async_copy(hop, T.at[pl.ds(0, SLOTS)], sems.at[0])]
     for m in range(3):
@@ -334,109 +339,82 @@
             windows.append(
                 pltpu.make_async_copy(src, V.at[:, pl.ds(start, size), lanes], sems.at[4 + 2 * j + q])
             )
-    for copy in copies + windows:
+    scalars = [
+        pltpu.make_async_copy(src, dst, sems.at[30 + i])
+        for i, (src, dst) in enumerate(((CR, NR), (CC, NC), (CL, NL), (CN, NN)))
+    ]
+    for copy in scalars + copies + windows:
         copy.start()
 
-    def clear(b, _):
-        head[b] = -1
+    def clear(i, _):
+        rows = pl.ds(pl.multiple_of(i * 8, 8), 8)
+        for k in range(2):
+            for r in range(TR):
+                H[k, r, rows, :] = jnp.zeros((8, WIDE * TS), jnp.float32)
         return 0
 
-    lax.fori_loop(0, TR * WIDE, clear, 0)
+    lax.fori_loop(0, 2 * TS // 8, clear, 0)
+    for copy in scalars:
+        copy.wait()
+    part = 32
     for m in range(4):
-
-        def link(i, _, m=m):
-            r = C[m, 0, i] - row * TR
-            w = C[m, 1, i] - (row * TR + r - BAND)
-            w = jnp.where(w < 0, w + TORB, w)
-            w = jnp.where(w >= TORB, w - TORB, w)
-            b = r * WIDE + w
-            chain[m * SLOTS + i] = head[b]
-            head[b] = m * SLOTS + i
+        copies[m].wait()
+        count = NN[m, 0, 0]
+
+        def add(i, _, m=m, count=count):
+            for one in (2 * i, 2 * i + 1):
+                r = jnp.clip(NR[m, 0, one] - row * TR, 0, TR - 1)
+                w = NC[m, 0, one] - (row * TR + r - BAND)
+                w = jnp.where(w < 0, w + TORB, w)
+                w = jnp.clip(jnp.where(w >= TORB, w - TORB, w), 0, WIDE - 1)
+                cols = pl.ds(pl.multiple_of(w * TS, TS), TS)
+                lat = NL[m, 0, one]
+                scale = [jnp.where(one < count, t[k, lat], 0.0) for k in range(2) for t in (cosine, sine)]
+                for at in range(0, TS, part):
+                    tile = T[m * SLOTS + one, pl.ds(at, part), :].astype(jnp.float32)
+                    for k in range(2):
+                        for p in range(2):
+                            H[k, r, pl.ds(p * TS + at, part), cols] += tile * scale[2 * k + p]
             return 0
 
-        lax.fori_loop(0, C[m, 3, 0], link, 0)
-    for copy in copies:
-        copy.wait()
-
-    half = TS // 2
-
-    def weights(s, ok):
-        m = s // SLOTS
-        lat = C[m, 2, s - m * SLOTS]
-        return [jnp.where(ok, table[i, lat], 0.0) for i in range(4)]
-
-    for r in range(TR):
-
-        def build(w, _, r=r):
-            cols = pl.ds(pl.multiple_of(w * TS, TS), TS)
-            first = head[r * WIDE + w]
-            for part in range(2):
-                rows = pl.ds(part * half, half)
-
-                def step(carry):
-                    s, accs = carry[0], carry[1:]
-                    s2 = chain[s]
-                    ok = s2 >= 0
-                    s2 = jnp.where(ok, s2, s)
-                    after = jnp.where(ok, chain[s2], -1)
-                    one = T[s, rows, :].astype(jnp.float32)
-                    two = T[s2, rows, :].astype(jnp.float32)
-                    w1, w2 = weights(s, True), weights(s2, ok)
-                    return (after,) + tuple(
-                        acc + (one * a + two * b) for acc, a, b in zip(accs, w1, w2)
-                    )
-
-                zero = jnp.zeros((half, TS), jnp.float32)
-                res = lax.while_loop(lambda c: c[0] >= 0, step, (first, zero, zero, zero, zero))
-                for k in range(2):
-                    for p in range(2):
-                        H[k, r, pl.ds(p * TS + part * half, half), cols] = res[1 + 2 * k + p].astype(
-                            jnp.bfloat16
-                        )
-            return 0
-
-        lax.fori_loop(0, WIDE, build, 0)
+        lax.fori_loop(0, (count + 1) // 2, add, 0)
     for copy in windows:
         copy.wait()
     for k in range(2):
         for r in range(TR):
             o = jnp.dot(
-                H[k, r], V[k, pl.ds(r * TS, WIDE * TS), :], preferred_element_type=jnp.float32
+                H[k, r].astype(jnp.bfloat16), V[k, pl.ds(r * TS, WIDE * TS), :], preferred_element_type=jnp.float32
             )
             rows = pl.ds(r * TS, TS)
             out[k, 0, rows, :] = o[:TS, :NV] - o[TS:, NV:]
             out[k, 1, rows, :] = o[:TS, NV:] + o[TS:, :NV]
 
 
-def product(C, table, hop, G, vec, W):
+def product(cosine, sine, hop, G, vec, W, lists):
     any_space = pl.BlockSpec(memory_space=pl.ANY)
     smem = pl.BlockSpec(memory_space=pltpu.SMEM)
     return pl.pallas_call(
         product_kernel,
         out_shape=jax.ShapeDtypeStruct((2, 2, BLK, NV), jnp.float32),
-        in_specs=[smem, smem] + [any_space] * 4,
+        in_specs=[smem, smem] + [any_space] * 8,
         out_specs=pl.BlockSpec(memory_space=pltpu.VMEM),
         scratch_shapes=[
             pltpu.VMEM((4 * SLOTS, TS, TS), jnp.bfloat16),
             pltpu.VMEM((2, SPAN * TS, 2 * NV), jnp.bfloat16),
-            pltpu.VMEM((2, TR, 2 * TS, WIDE * TS), jnp.bfloat16),
-            pltpu.SMEM((128,), jnp.int32),
-            pltpu.SMEM((4 * SLOTS,), jnp.int32),
-            pltpu.SemaphoreType.DMA((30,)),
+            pltpu.VMEM((2, TR, 2 * TS, WIDE * TS), jnp.float32),
+            *[pltpu.SMEM((4, 1, SLOTS), jnp.int32)] * 4,
+            pltpu.SemaphoreType.DMA((34,)),
         ],
-        compiler_params=pltpu.CompilerParams(vmem_limit_bytes=56 * 1024 * 1024),
+        compiler_params=pltpu.CompilerParams(vmem_limit_bytes=60 * 1024 * 1024),
         name="product",
-    )(C, table, hop, G, vec, W)
+    )(cosine, sine, hop, G, vec, W, *lists)
 
 
 def body(hoppings, tile_rows, tile_cols, tile_lats, tile_counts, phase_angle, vectors):
     hop = hoppings[0]
-    counts = jnp.broadcast_to(tile_counts, (1, SLOTS))
-    coords = jnp.concatenate([tile_rows, tile_cols, tile_lats, counts], axis=0)
-    coords = jnp.pad(coords, ((0, 4), (0, 128 - SLOTS)))
-    table = jnp.stack([jnp.cos(phase_angle), jnp.sin(phase_angle)], axis=1).reshape(4, NLAT)
-    G, W, C = gather_all(hop, coords, vectors)
-    return product(C, table, hop, G, vectors, W)
+    live = jnp.broadcast_to(tile_counts, (1, SLOTS))
+    G, W, *lists = gather_all(hop, (tile_rows, tile_cols, tile_lats, live), vectors)
+    return product(jnp.cos(phase_angle), jnp.sin(phase_angle), hop, G, vectors, W, lists)
 
 
 def solution(mesh):

time: 142 us -> 125 us (0.88); the launches traced: 139 us -> 125 us
  Pallas kernels: 137 us -> 123 us
    pallas_call x1, Pallas kernels: 34.6 us -> 20.9 us  [product(): pl.pallas_call(product_kernel, out_shape=jax.ShapeDtypeStruct((2, 2, BLK,...]
where the time goes in v2:
time: 125 us
  Pallas kernels  123 us (98%)
    pallas_call x1, Pallas kernels, gather_all(): pl.pallas_call(gather_kernel, out_shape=(jax.ShapeDtypeStruct((3,) + hop....  102 us
    pallas_call x1, Pallas kernels, product(): pl.pallas_call(product_kernel, out_shape=jax.ShapeDtypeStruct((2, 2, BLK,...  20.9 us

profile of v2, /device:TPU:1, one launch (start us, length us, event | category | flops | bytes accessed | tf_op | source)
XLA Modules:
  0.0 125.3 jit_solution(3031533692569843062)
XLA Ops:
  0.0 0.0 copy-start
  0.7 0.6 broadcast_in_dim.8.live
  1.3 102.5 %gather.1 = (bf16[3,96,128,128]{3,2,1,0:T(8,128)(2,1)}, bf16[13,2,2,384,256]{4,3,2,1,0:T(8,128)(2,1)}, s32[4,1,96]{2,1,0:T(1,128)}, s32[4,1,96]{2,1,0:T(1,128)},...) custom-call(bf16[96,128,128]{2,1,0:T(8,128)(2,1)} %bitcast.3, ...), custom_call_target="tpu_custom_call" | custom-call | tf_op jit(solution)/shard_map/gather/pallas_call | solution.py:299
  103.8 0.0 copy-done
  103.8 0.6 fusion
  104.4 20.9 %product.1 = f32[2,2,384,256]{3,2,1,0:T(8,128)} custom-call(f32[2,9]{1,0:T(2,128)} %get-tuple-element.18.cosine, f32[2,9]{1,0:T(2,128)} %get-tuple-element.17.sine, bf16[96,128,128]{2,1,0:T(8,128)(2,1)} %bitcast.4, bf16[3,96,128,128]{3,2,1,0:T(8,128)(2,1)} %get-tuple-element.11.G, bf16[2,2,384,256]{3,2,1,0:T(8,128)(2,1)} %vec.3, ...), custom_call_target="tpu_custom_call" | custom-call | tf_op jit(solution)/shard_map/product/pallas_call | solution.py:396
Async XLA Ops:
  0.0 103.8 %copy-start = (f32[2,9]{1,0:T(2,128)S(1)}, f32[2,9]{1,0:T(2,128)}, u32[]{:S(2)}) copy-start(f32[2,9]{1,0:T(2,128)} %param.12) | copy-start | bytes 220

commit v3 on v2

v3 whole, which is shorter than its diff:
```python
import functools

import jax
import jax.numpy as jnp
from jax import lax
from jax.experimental import pallas as pl
from jax.experimental.pallas import tpu as pltpu
from jax.sharding import PartitionSpec as P

MESH = pl.DeviceIdType.MESH
BAND = 16
NLAT = 9
TS = 128
NV = 256
TR = 3
BLK = TR * TS
SLOTS = 96
CHUNKS = 8
PER = SLOTS // CHUNKS
AROUND = 8
WIDE = 2 * BAND + 1
SPAN = WIDE + TR - 1
TORB = 96
HALVES = (0, 1)


class Net:
    def __init__(self, send_sem, recv_sem):
        self.send_sem, self.recv_sem = send_sem, recv_sem
        self.index, self.sent = {}, []

    def copy(self, name, src, dst, device):
        at = self.index.setdefault(name, len(self.index))
        return pltpu.make_async_remote_copy(
            src_ref=src, dst_ref=dst, send_sem=self.send_sem.at[at], recv_sem=self.recv_sem.at[at],
            device_id=device, device_id_type=MESH,
        )

    def send(self, name, when, src, dst, device):
        copy = self.copy(name, src, dst, device)
        self.sent.append((when, copy))
        guarded(when, copy.start)

    def recv(self, name, when, dst, device):
        guarded(when, self.copy(name, dst, dst, device).wait_recv)

    def finish(self):
        for when, copy in self.sent:
            guarded(when, copy.wait_send)


def guarded(when, action):
    if when is None:
        action()
    else:
        pl.when(when)(action)


def gather_kernel(hop, rows, cols, lats, live, vec, G, W, CR, CC, CL, CN, S, X, E, R, send_sem, recv_sem, local_sem):
    ka = lax.axis_index("ka")
    row = lax.axis_index("rows")
    xh, y, z = row // 16, (row // 4) % 4, row % 4
    zp, zm, z2 = (z + 1) % 4, (z + 3) % 4, (z + 2) % 4
    yp, ym = (y + 1) % 4, (y + 3) % 4

    def at(h, i, j):
        return (ka, h * 16 + i * 4 + j)

    def along(flip):
        other = (1 - ka % 2) if flip % 2 else ka % 2
        pair = (1 - ka // 2) if flip // 2 else ka // 2
        return (pair * 2 + other, row)

    up_z, down_z, up_y, down_y = at(xh, y, zp), at(xh, y, zm), at(xh, yp, z), at(xh, ym, z)
    mirror = at(1 - xh, y, z)
    low, high = z == 0, z == 3
    mid = (z == 1) | (z == 2)
    top, base = y == 3, y == 0
    down_y = at(jnp.where(base, 1 - xh, xh), ym, z)
    up_y = at(jnp.where(top, 1 - xh, xh), yp, z)
    inner_y = at(xh, jnp.where(base, 3, jnp.where(top, 0, y)), z)
    crossing = ((y == 1) & high) | ((y == 2) & low)
    part_sender = ((y == 1) & (z == 1)) | ((y == 2) & (z == 2))
    part_to = at(1 - xh, y, jnp.where(y == 1, 3, 0))
    part_from = at(1 - xh, y, jnp.where(y == 1, 1, 2))
    split = ((y == 1) & low) | ((y == 2) & high)
    outer = base | top
    beside_y = at(xh, jnp.where(y < 2, 1 - y, 5 - y), z)
    over = at(xh, jnp.where(y == 1, 0, 3), jnp.where(y == 1, 3, 0))
    over_from = at(xh, jnp.where(base, 1, 2), z)
    split_from = at(xh, jnp.where(base, 1, 2), 3 - z)
    relay = (base & high) | (top & low)
    relayed = (top & high) | (base & low)
    barrier = pltpu.get_barrier_semaphore()

    def greet(peer):
        pl.semaphore_signal(barrier, inc=1, device_id=peer, device_id_type=MESH)

    for peer in (along(1), along(2), along(3), up_z, down_z, up_y, down_y):
        greet(peer)
    pl.when(part_sender)(lambda: greet(part_to))
    pl.when(crossing)(lambda: greet(part_from))
    pl.when(crossing | split)(lambda: greet(mirror))
    pl.when(split)(lambda: greet(over))
    pl.when(relay)(lambda: greet(split_from))
    pl.when(relay | relayed)(lambda: greet(inner_y))
    extra = jnp.where(part_sender, 1, 0) + jnp.where(crossing | split, 2, 0)
    extra = extra + jnp.where(relay | relayed, 1, 0) + jnp.where(relay, 1, 0)
    pl.semaphore_wait(barrier, 7 + extra)

    net = Net(send_sem, recv_sem)
    send, recv = net.send, net.recv
    HEAD, LAST = pl.ds(0, TS), pl.ds(2 * TS, TS)

    def tail(first):
        return pl.ds(pl.multiple_of(jnp.where(first, 0, 2 * TS), TS), TS)

    lists = ((rows, CR), (cols, CC), (lats, CL), (live, CN))
    local = [pltpu.make_async_copy(src, dst.at[0], local_sem.at[i]) for i, (src, dst) in enumerate(lists)]
    for copy in local:
        copy.start()

    member = {0: z, -1: zm, 1: zp, 2: z2}

    def y_sends(u, h):
        dz = member[u] - z
        src = vec.at[h] if u == 0 else W.at[6 + dz, h]
        down_dst, up_dst = W.at[10 + dz, h], W.at[2 + dz, h]
        down_ok, up_ok = (None, None) if u == 0 else (y > 0, y < 3)
        if u == 2:
            send(f"y-{u}{h}", down_ok & (z >= 2), src, down_dst, down_y)
            send(f"y-{u}{h}", down_ok & (z < 2), src.at[:, HEAD], down_dst.at[:, HEAD], down_y)
            send(f"y+{u}{h}", up_ok & (z < 2), src, up_dst, up_y)
            send(f"y+{u}{h}", up_ok & (z >= 2), src.at[:, LAST], up_dst.at[:, LAST], up_y)
        else:
            send(f"y-{u}{h}", down_ok & (z != 0) if u == -1 else down_ok, src, down_dst, down_y)
            send(f"y+{u}{h}", up_ok & (z != 3) if u == 1 else up_ok, src, up_dst, up_y)

    def y_recvs(u, h):
        dz = member[u] - z
        down_dst, up_dst = W.at[10 + dz, h], W.at[2 + dz, h]
        down_ok, up_ok = (None, None) if u == 0 else (y < 3, y > 0)
        if u == 2:
            recv(f"y-{u}{h}", down_ok & (z >= 2), down_dst, up_y)
            recv(f"y-{u}{h}", down_ok & (z < 2), down_dst.at[:, HEAD], up_y)
            recv(f"y+{u}{h}", up_ok & (z < 2), up_dst, down_y)
            recv(f"y+{u}{h}", up_ok & (z >= 2), up_dst.at[:, LAST], down_y)
        else:
            recv(f"y-{u}{h}", down_ok & (z != 0) if u == -1 else down_ok, down_dst, up_y)
            recv(f"y+{u}{h}", up_ok & (z != 3) if u == 1 else up_ok, up_dst, down_y)

    def both(when, ok):
        return ok if when is None else when & ok

    def spread(h):
        a, b = (None, None) if h else (top, base)
        send(f"a1{h}", both(a, z < 3), W.at[10, h], W.at[9, h], up_z)
        send(f"b1{h}", both(b, z > 0), W.at[2, h], W.at[3, h], down_z)
        send(f"a2{h}", a, W.at[10, h], W.at[jnp.where(low, 7, 11), h], down_z)
        send(f"b2{h}", b, W.at[2, h], W.at[jnp.where(high, 5, 1), h], up_z)

    def spread_on(h):
        a, b = (None, None) if h else (top, base)
        recv(f"a1{h}", both(a, z > 0), W.at[9, h], down_z)
        recv(f"b1{h}", both(b, z < 3), W.at[3, h], up_z)
        recv(f"a2{h}", a, W.at[jnp.where(high, 7, 11), h], up_z)
        recv(f"b2{h}", b, W.at[jnp.where(low, 5, 1), h], down_z)
        if h:
            send(f"a3{h}", mid, W.at[9, h], W.at[8, h], up_z)
            send(f"b3{h}", mid, W.at[3, h], W.at[4, h], down_z)
        else:
            send(f"a3{h}", both(a, low | high), W.at[jnp.where(low, 11, 7), h], W.at[8, h], down_z)
            send(f"b3{h}", both(b, low | high), W.at[jnp.where(low, 5, 1), h], W.at[4, h], up_z)
        send(f"a4{h}", both(a, mid), W.at[11, h, :, HEAD], W.at[12, h, :, HEAD], down_z)
        send(f"b4{h}", both(b, mid), W.at[1, h, :, LAST], W.at[0, h, :, LAST], up_z)

    def spread_last(h):
        a, b = (None, None) if h else (top, base)
        recv(f"a3{h}", both(a, z >= 2), W.at[8, h], down_z)
        recv(f"b3{h}", both(b, z < 2), W.at[4, h], down_z)
        recv(f"a4{h}", both(a, z < 2), W.at[12, h, :, HEAD], up_z)
        recv(f"b4{h}", both(b, z >= 2), W.at[0, h, :, LAST], down_z)

    near_to, near_from = (low & (y > 0)) | (high & (y < 3)), (low & (y < 3)) | (high & (y > 0))
    near = at(xh, jnp.where(low, ym, yp), z)
    near_src = at(xh, jnp.where(low, yp, ym), z)
    across = at(xh, y, jnp.where(low, 3, 0))
    across_from = (high & (y < 3)) | (low & (y > 0))
    block, beside = jnp.where(low, 10, 2), jnp.where(low, 11, 1)
    far, far_part = jnp.where(low, 11, 1), jnp.where(low, 12, 0)
    got, got_part = jnp.where(low, 1, 11), jnp.where(low, 0, 12)

    def second(h):
        send(f"d{h}", near_to, W.at[block, h], X.at[0, h], near)

    def second_part(h, ok):
        send(f"dp{h}", near_to & ok, W.at[beside, h, :, tail(low)], X.at[1, h, :, tail(low)], near)

    crossed = jnp.where(y == 1, 3, 9)

    def cross():
        send("g0", crossing, W.at[crossed, 0], S.at[0, 0], mirror)

    z_dst_up, z_dst_down = W.at[6 + z - zp], W.at[6 + z - zm]
    y_sends(0, 1)
    send("z-0", None, vec.at[0], z_dst_up.at[0], up_z)
    send("z+1", None, vec.at[1], z_dst_down.at[1], down_z)
    y_sends(0, 0)
    send("z-1", None, vec.at[1], z_dst_up.at[1], up_z)
    send("z+0", None, vec.at[0], z_dst_down.at[0], down_z)
    for h in HALVES:
        send(f"gp{h}", part_sender, vec.at[h, :, tail(y == 1)], S.at[1, h, :, tail(y == 1)], part_to)

    def pieces(c):
        if c < CHUNKS - 1:
            return ((f"{c}", None, pl.ds(c * PER, PER)),)
        end = SLOTS - AROUND
        return (("e", None, pl.ds(c * PER, end - c * PER)), ("f", ~outer, pl.ds(end, AROUND)))

    def chunk(c):
        for name, when, part in pieces(c):
            send(f"x{name}", when, hop.at[part], G.at[1, part], along(2))

    def forward(c):
        for name, when, part in pieces(c):
            recv(f"x{name}", when, G.at[1, part], along(2))
            send(f"o{name}", when, G.at[1, part], G.at[2, part], along(1))

    around = pl.ds(SLOTS - AROUND, AROUND)
    send("g1", split, vec.at[1], S.at[0, 1], mirror)
    send("r", outer, hop.at[around], R.at[0], beside_y)
    for c in range(3):
        chunk(c)
    for flip in (1, 2, 3):
        for i, (src, dst) in enumerate(lists):
            send(f"c{flip}{i}", None, src, dst.at[flip], along(flip))
    send("sib", None, hop, G.at[0], along(1))

    recv("z-0", None, W.at[6 + zm - z, 0], down_z)
    send("w0", None, W.at[6 + zm - z, 0], W.at[6 + zm - zp, 0], up_z)
    y_sends(-1, 0)
    recv("z+1", None, W.at[6 + zp - z, 1], up_z)
    send("w1", None, W.at[6 + zp - z, 1], W.at[6 + zp - zm, 1], down_z)
    y_recvs(0, 1)
    spread(1)
    second(1)
    recv("z+0", None, W.at[6 + zp - z, 0], up_z)
    y_sends(1, 0)
    recv("z-1", None, W.at[6 + zm - z, 1], down_z)
    cross()
    recv("r", ~outer, R.at[0], beside_y)
    send("q", ~outer, R.at[0], R.at[1], along(2))
    for c in range(3, CHUNKS):
        chunk(c)
    recv("g1", split, S.at[0, 1], mirror)
    send("e1", split, S.at[0, 1], E.at[0, 1], over)
    y_recvs(0, 0)
    second(0)
    spread(0)
    recv("w0", None, W.at[6 + z2 - z, 0], down_z)
    y_sends(2, 0)
    recv("w1", None, W.at[6 + z2 - z, 1], up_z)
    for h in HALVES:
        recv(f"d{h}", near_from, X.at[0, h], near_src)
        send(f"f{h}", near_from, X.at[0, h], W.at[far, h], across)
    recv("g0", crossing, S.at[0, 0], mirror)
    send("e0", crossing, S.at[0, 0], E.at[0, 0], beside_y)
    for h in HALVES:
        recv(f"gp{h}", crossing, S.at[1, h, :, tail(y == 1)], part_from)
        send(f"ep{h}", crossing, S.at[1, h, :, tail(y == 1)], E.at[1, h, :, tail(y == 1)], beside_y)
    y_recvs(-1, 0)
    y_recvs(1, 0)
    second_part(0, (low & (y < 3)) | (high & (y > 0)))
    spread_on(1)
    second_part(1, low | high)
    spread_on(0)
    second_part(0, (low & top) | (high & base))
    for h in HALVES:
        recv(f"e{h}", relay, E.at[0, h], split_from if h else over_from)
        send(f"f{h}", relay, E.at[0, h], W.at[got, h], inner_y)
        recv(f"ep{h}", relay, E.at[1, h, :, tail(high)], over_from)
        send(f"fp{h}", relay, E.at[1, h, :, tail(high)], W.at[got_part, h, :, tail(high)], inner_y)
    recv("q", ~outer, R.at[1], along(2))
    send("p", ~outer, R.at[1], G.at[1, around], beside_y)
    for c in range(3):
        forward(c)
    for h in HALVES:
        recv(f"dp{h}", near_from, X.at[1, h, :, tail(low)], near_src)
        send(f"fp{h}", near_from, X.at[1, h, :, tail(low)], W.at[far_part, h, :, tail(low)], across)
    rim = low | high
    next_to = at(xh, y, jnp.where(low, 1, 2))
    for h in HALVES:
        recv(f"f{h}", rim, W.at[got, h], across)
        send(f"l{h}", rim, W.at[got, h, :, tail(high)], W.at[got_part, h, :, tail(high)], next_to)
    for c in range(3, CHUNKS - 2):
        forward(c)
    y_recvs(2, 0)
    for h in HALVES:
        spread_last(h)
        recv(f"fp{h}", rim, W.at[got_part, h, :, tail(high)], across)
        recv(f"l{h}", mid, W.at[jnp.where(z == 1, 0, 12), h, :, tail(z == 2)], at(xh, y, jnp.where(z == 1, 0, 3)))
    for flip in (1, 2, 3):
        for i, (_, dst) in enumerate(lists):
            recv(f"c{flip}{i}", None, dst.at[flip], along(flip))
    recv("sib", None, G.at[0], along(1))
    recv("p", outer, G.at[1, around], beside_y)
    send("of", outer, G.at[1, around], G.at[2, around], along(1))
    for c in range(CHUNKS - 2, CHUNKS):
        forward(c)
    for c in range(CHUNKS):
        for name, _, part in pieces(c):
            recv(f"o{name}", None, G.at[2, part], along(1))
    net.finish()
    for copy in local:
        copy.wait()


def gather_all(hop, lists, vec):
    block = vec.shape
    any_space = pl.BlockSpec(memory_space=pl.ANY)
    sems = 104
    return pl.pallas_call(
        gather_kernel,
        out_shape=(
            jax.ShapeDtypeStruct((3,) + hop.shape, hop.dtype),
            jax.ShapeDtypeStruct((13,) + block, vec.dtype),
            *[jax.ShapeDtypeStruct((4,) + a.shape, a.dtype) for a in lists],
            *[jax.ShapeDtypeStruct((2,) + block, vec.dtype)] * 3,
            jax.ShapeDtypeStruct((2, AROUND) + hop.shape[1:], hop.dtype),
        ),
        in_specs=[any_space] * 6,
        out_specs=(any_space,) * 10,
        scratch_shapes=[
            pltpu.SemaphoreType.DMA((sems,)),
            pltpu.SemaphoreType.DMA((sems,)),
            pltpu.SemaphoreType.DMA((4,)),
        ],
        compiler_params=pltpu.CompilerParams(collective_id=0, has_side_effects=True),
        name="gather",
    )(hop, *lists, vec)[:6]


def product_kernel(cosine, sine, hop, G, vec, W, CR, CC, CL, CN, out, T, V, H, NR, NC, NL, NN, sems):
    row = lax.axis_index("rows")
    copies = [pltpu.make_async_copy(hop, T.at[pl.ds(0, SLOTS)], sems.at[0])]
    for m in range(3):
        copies.append(
            pltpu.make_async_copy(G.at[m], T.at[pl.ds((m + 1) * SLOTS, SLOTS)], sems.at[m + 1])
        )
    windows = []
    for j in range(13):
        for q in range(2):
            lanes = pl.ds(q * NV, NV)
            if j == 0:
                src, start, size = W.at[j, :, q, pl.ds(2 * TS, TS)], 0, TS
            elif j == 12:
                src, start, size = W.at[j, :, q, pl.ds(0, TS)], (SPAN - 1) * TS, TS
            else:
                src = vec.at[:, q] if j == 6 else W.at[j, :, q]
                start, size = (TR * (j - 6) + BAND) * TS, BLK
            windows.append(
                pltpu.make_async_copy(src, V.at[:, pl.ds(start, size), lanes], sems.at[4 + 2 * j + q])
            )
    scalars = [
        pltpu.make_async_copy(src, dst, sems.at[30 + i])
        for i, (src, dst) in enumerate(((CR, NR), (CC, NC), (CL, NL), (CN, NN)))
    ]
    for copy in scalars + copies + windows:
        copy.start()

    def clear(i, _):
        rows = pl.ds(pl.multiple_of(i * 8, 8), 8)
        for k in range(2):
            for r in range(TR):
                H[k, r, rows, :] = jnp.zeros((8, WIDE * TS), jnp.float32)
        return 0

    lax.fori_loop(0, 2 * TS // 8, clear, 0)
    for copy in scalars:
        copy.wait()
    part = 32
    for m in range(4):
        copies[m].wait()
        count = NN[m, 0, 0]

        def add(i, _, m=m, count=count):
            for one in (2 * i, 2 * i + 1):
                r = jnp.clip(NR[m, 0, one] - row * TR, 0, TR - 1)
                w = NC[m, 0, one] - (row * TR + r - BAND)
                w = jnp.where(w < 0, w + TORB, w)
                w = jnp.clip(jnp.where(w >= TORB, w - TORB, w), 0, WIDE - 1)
                cols = pl.ds(pl.multiple_of(w * TS, TS), TS)
                lat = NL[m, 0, one]
                scale = [jnp.where(one < count, t[k, lat], 0.0) for k in range(2) for t in (cosine, sine)]
                for at in range(0, TS, part):
                    tile = T[m * SLOTS + one, pl.ds(at, part), :].astype(jnp.float32)
                    for k in range(2):
                        for p in range(2):
                            H[k, r, pl.ds(p * TS + at, part), cols] += tile * scale[2 * k + p]
            return 0

        lax.fori_loop(0, (count + 1) // 2, add, 0)
    for copy in windows:
        copy.wait()
    for k in range(2):
        for r in range(TR):
            o = jnp.dot(
                H[k, r].astype(jnp.bfloat16), V[k, pl.ds(r * TS, WIDE * TS), :], preferred_element_type=jnp.float32
            )
            rows = pl.ds(r * TS, TS)
            out[k, 0, rows, :] = o[:TS, :NV] - o[TS:, NV:]
            out[k, 1, rows, :] = o[:TS, NV:] + o[TS:, :NV]


def product(cosine, sine, hop, G, vec, W, lists):
    any_space = pl.BlockSpec(memory_space=pl.ANY)
    smem = pl.BlockSpec(memory_space=pltpu.SMEM)
    return pl.pallas_call(
        product_kernel,
        out_shape=jax.ShapeDtypeStruct((2, 2, BLK, NV), jnp.float32),
        in_specs=[smem, smem] + [any_space] * 8,
        out_specs=pl.BlockSpec(memory_space=pltpu.VMEM),
        scratch_shapes=[
            pltpu.VMEM((4 * SLOTS, TS, TS), jnp.bfloat16),
            pltpu.VMEM((2, SPAN * TS, 2 * NV), jnp.bfloat16),
            pltpu.VMEM((2, TR, 2 * TS, WIDE * TS), jnp.float32),
            *[pltpu.SMEM((4, 1, SLOTS), jnp.int32)] * 4,
            pltpu.SemaphoreType.DMA((34,)),
        ],
        compiler_params=pltpu.CompilerParams(vmem_limit_bytes=60 * 1024 * 1024),
        name="product",
    )(cosine, sine, hop, G, vec, W, *lists)


def body(hoppings, tile_rows, tile_cols, tile_lats, tile_counts, phase_angle, vectors):
    hop = hoppings[0]
    live = jnp.broadcast_to(tile_counts, (1, SLOTS))
    G, W, *lists = gather_all(hop, (tile_rows, tile_cols, tile_lats, live), vectors)
    return product(jnp.cos(phase_angle), jnp.sin(phase_angle), hop, G, vectors, W, lists)


def solution(mesh):
    return jax.shard_map(
        body,
        mesh=mesh,
        in_specs=(
            P("rows", "ka", None, None),
            P("rows", "ka"),
            P("rows", "ka"),
            P("rows", "ka"),
            P("rows", "ka"),
            P("ka", None),
            P("ka", None, "rows", None),
        ),
        out_specs=P("ka", None, "rows", None),
        check_vma=False,
    )
```

time: 125 us -> 117 us (0.936); the launches traced: 125 us -> 115 us
  Pallas kernels: 123 us -> 114 us
    pallas_call x1, Pallas kernels: 102 us -> 93.2 us  [gather_all(): pl.pallas_call(gather_kernel, out_shape=(jax.ShapeDtypeStruct((3,) + hop....]
where the time goes in v3:
time: 117 us; the launch traced here: 115 us
  Pallas kernels  114 us (97%)
    pallas_call x1, Pallas kernels, gather_all(): pl.pallas_call(gather_kernel, out_shape=(jax.ShapeDtypeStruct((3,) + hop....  93.2 us
    pallas_call x1, Pallas kernels, product(): pl.pallas_call(product_kernel, out_shape=jax.ShapeDtypeStruct((2, 2, BLK,...  20.5 us

profile of v3, /device:TPU:1, one launch (start us, length us, event | category | flops | bytes accessed | tf_op | source)
XLA Modules:
  0.0 115.5 jit_solution(16408831991617570569)
XLA Ops:
  0.7 0.5 broadcast_in_dim.8.live
  1.2 0.0 copy-start
  1.2 93.2 %gather.1 = (bf16[3,96,128,128]{3,2,1,0:T(8,128)(2,1)}, bf16[13,2,2,384,256]{4,3,2,1,0:T(8,128)(2,1)}, s32[4,1,96]{2,1,0:T(1,128)}, s32[4,1,96]{2,1,0:T(1,128)},...) custom-call(bf16[96,128,128]{2,1,0:T(8,128)(2,1)} %bitcast.3, ...), custom_call_target="tpu_custom_call" | custom-call | tf_op jit(solution)/shard_map/gather/pallas_call | solution.py:322
  94.3 0.0 copy-done
  94.3 0.6 fusion
  95.0 20.5 %product.1 = f32[2,2,384,256]{3,2,1,0:T(8,128)} custom-call(f32[2,9]{1,0:T(2,128)} %get-tuple-element.18.cosine, f32[2,9]{1,0:T(2,128)} %get-tuple-element.17.sine, bf16[96,128,128]{2,1,0:T(8,128)(2,1)} %bitcast.4, bf16[3,96,128,128]{3,2,1,0:T(8,128)(2,1)} %get-tuple-element.11.G, bf16[2,2,384,256]{3,2,1,0:T(8,128)(2,1)} %vec.3, ...), custom_call_target="tpu_custom_call" | custom-call | tf_op jit(solution)/shard_map/product/pallas_call | solution.py:418
Async XLA Ops:
  1.2 93.2 %copy-start = (f32[2,9]{1,0:T(2,128)S(1)}, f32[2,9]{1,0:T(2,128)}, u32[]{:S(2)}) copy-start(f32[2,9]{1,0:T(2,128)} %param.12) | copy-start | bytes 220

commit v4 on v3

--- a/solution.py
+++ b/solution.py
@@ -17,7 +17,8 @@
 SLOTS = 96
 CHUNKS = 8
 PER = SLOTS // CHUNKS
-AROUND = 8
+AROUND = 6
+GROUP = 4
 WIDE = 2 * BAND + 1
 SPAN = WIDE + TR - 1
 TORB = 96
@@ -122,11 +123,13 @@
 
     member = {0: z, -1: zm, 1: zp, 2: z2}
 
-    def y_sends(u, h):
+    def y_sends(u, h, only=None):
         dz = member[u] - z
         src = vec.at[h] if u == 0 else W.at[6 + dz, h]
         down_dst, up_dst = W.at[10 + dz, h], W.at[2 + dz, h]
         down_ok, up_ok = (None, None) if u == 0 else (y > 0, y < 3)
+        if only is not None:
+            down_ok, up_ok = down_ok & only, up_ok & only
         if u == 2:
             send(f"y-{u}{h}", down_ok & (z >= 2), src, down_dst, down_y)
             send(f"y-{u}{h}", down_ok & (z < 2), src.at[:, HEAD], down_dst.at[:, HEAD], down_y)
@@ -241,6 +244,8 @@
     y_sends(-1, 0)
     recv("z+1", None, W.at[6 + zp - z, 1], up_z)
     send("w1", None, W.at[6 + zp - z, 1], W.at[6 + zp - zm, 1], down_z)
+    recv("g1", split, S.at[0, 1], mirror)
+    send("e1", split, S.at[0, 1], E.at[0, 1], over)
     y_recvs(0, 1)
     spread(1)
     second(1)
@@ -252,34 +257,40 @@
     send("q", ~outer, R.at[0], R.at[1], along(2))
     for c in range(3, CHUNKS):
         chunk(c)
-    recv("g1", split, S.at[0, 1], mirror)
-    send("e1", split, S.at[0, 1], E.at[0, 1], over)
     y_recvs(0, 0)
     second(0)
     spread(0)
     recv("w0", None, W.at[6 + z2 - z, 0], down_z)
-    y_sends(2, 0)
+    y_sends(2, 0, ~crossing)
     recv("w1", None, W.at[6 + z2 - z, 1], up_z)
-    for h in HALVES:
+    for h in (1, 0):
         recv(f"d{h}", near_from, X.at[0, h], near_src)
         send(f"f{h}", near_from, X.at[0, h], W.at[far, h], across)
     recv("g0", crossing, S.at[0, 0], mirror)
     send("e0", crossing, S.at[0, 0], E.at[0, 0], beside_y)
+    y_sends(2, 0, crossing)
     for h in HALVES:
         recv(f"gp{h}", crossing, S.at[1, h, :, tail(y == 1)], part_from)
         send(f"ep{h}", crossing, S.at[1, h, :, tail(y == 1)], E.at[1, h, :, tail(y == 1)], beside_y)
+    def onward(h):
+        recv(f"e{h}", relay, E.at[0, h], split_from if h else over_from)
+        send(f"f{h}", relay, E.at[0, h], W.at[got, h], inner_y)
+
+    def onward_part(h):
+        recv(f"ep{h}", relay, E.at[1, h, :, tail(high)], over_from)
+        send(f"fp{h}", relay, E.at[1, h, :, tail(high)], W.at[got_part, h, :, tail(high)], inner_y)
+
     y_recvs(-1, 0)
     y_recvs(1, 0)
     second_part(0, (low & (y < 3)) | (high & (y > 0)))
     spread_on(1)
     second_part(1, low | high)
+    onward(1)
+    onward(0)
     spread_on(0)
     second_part(0, (low & top) | (high & base))
     for h in HALVES:
-        recv(f"e{h}", relay, E.at[0, h], split_from if h else over_from)
-        send(f"f{h}", relay, E.at[0, h], W.at[got, h], inner_y)
-        recv(f"ep{h}", relay, E.at[1, h, :, tail(high)], over_from)
-        send(f"fp{h}", relay, E.at[1, h, :, tail(high)], W.at[got_part, h, :, tail(high)], inner_y)
+        onward_part(h)
     recv("q", ~outer, R.at[1], along(2))
     send("p", ~outer, R.at[1], G.at[1, around], beside_y)
     for c in range(3):
@@ -289,7 +300,7 @@
         send(f"fp{h}", near_from, X.at[1, h, :, tail(low)], W.at[far_part, h, :, tail(low)], across)
     rim = low | high
     next_to = at(xh, y, jnp.where(low, 1, 2))
-    for h in HALVES:
+    for h in (1, 0):
         recv(f"f{h}", rim, W.at[got, h], across)
         send(f"l{h}", rim, W.at[got, h, :, tail(high)], W.at[got_part, h, :, tail(high)], next_to)
     for c in range(3, CHUNKS - 2):
@@ -340,13 +351,14 @@
     )(hop, *lists, vec)[:6]
 
 
-def product_kernel(cosine, sine, hop, G, vec, W, CR, CC, CL, CN, out, T, V, H, NR, NC, NL, NN, sems):
+def product_kernel(phase, hop, G, vec, W, CR, CC, CL, CN, out, T, V, H0, H1, O, NR, NC, NL, NN, factor, table, sems):
     row = lax.axis_index("rows")
     copies = [pltpu.make_async_copy(hop, T.at[pl.ds(0, SLOTS)], sems.at[0])]
     for m in range(3):
         copies.append(
             pltpu.make_async_copy(G.at[m], T.at[pl.ds((m + 1) * SLOTS, SLOTS)], sems.at[m + 1])
         )
+    H = (H0, H1)
     windows = []
     for j in range(13):
         for q in range(2):
@@ -365,78 +377,92 @@
         pltpu.make_async_copy(src, dst, sems.at[30 + i])
         for i, (src, dst) in enumerate(((CR, NR), (CC, NC), (CL, NL), (CN, NN)))
     ]
-    for copy in scalars + copies + windows:
+    for copy in scalars + copies:
         copy.start()
+    factor[0:2, :] = jnp.cos(phase[...])
+    factor[2:4, :] = jnp.sin(phase[...])
+    factors = pltpu.make_async_copy(factor, table, sems.at[34])
+    factors.start()
 
     def clear(i, _):
         rows = pl.ds(pl.multiple_of(i * 8, 8), 8)
         for k in range(2):
             for r in range(TR):
-                H[k, r, rows, :] = jnp.zeros((8, WIDE * TS), jnp.float32)
+                H[k][r, rows, :] = jnp.zeros((8, WIDE * TS), jnp.float32)
         return 0
 
     lax.fori_loop(0, 2 * TS // 8, clear, 0)
-    for copy in scalars:
+    for copy in scalars + [factors]:
         copy.wait()
     part = 32
     for m in range(4):
         copies[m].wait()
+        if m == 1:
+            for copy in windows:
+                copy.start()
         count = NN[m, 0, 0]
 
         def add(i, _, m=m, count=count):
-            for one in (2 * i, 2 * i + 1):
+            for one in [GROUP * i + j for j in range(GROUP)]:
                 r = jnp.clip(NR[m, 0, one] - row * TR, 0, TR - 1)
                 w = NC[m, 0, one] - (row * TR + r - BAND)
                 w = jnp.where(w < 0, w + TORB, w)
                 w = jnp.clip(jnp.where(w >= TORB, w - TORB, w), 0, WIDE - 1)
                 cols = pl.ds(pl.multiple_of(w * TS, TS), TS)
                 lat = NL[m, 0, one]
-                scale = [jnp.where(one < count, t[k, lat], 0.0) for k in range(2) for t in (cosine, sine)]
+                scale = [jnp.where(one < count, table[2 * p + k, lat], 0.0) for k in range(2) for p in range(2)]
                 for at in range(0, TS, part):
                     tile = T[m * SLOTS + one, pl.ds(at, part), :].astype(jnp.float32)
                     for k in range(2):
                         for p in range(2):
-                            H[k, r, pl.ds(p * TS + at, part), cols] += tile * scale[2 * k + p]
+                            H[k][r, pl.ds(p * TS + at, part), cols] += tile * scale[2 * k + p]
             return 0
 
-        lax.fori_loop(0, (count + 1) // 2, add, 0)
+        lax.fori_loop(0, (count + GROUP - 1) // GROUP, add, 0)
     for copy in windows:
         copy.wait()
+    done = []
     for k in range(2):
         for r in range(TR):
             o = jnp.dot(
-                H[k, r].astype(jnp.bfloat16), V[k, pl.ds(r * TS, WIDE * TS), :], preferred_element_type=jnp.float32
+                H[k][r].astype(jnp.bfloat16), V[k, pl.ds(r * TS, WIDE * TS), :], preferred_element_type=jnp.float32
             )
             rows = pl.ds(r * TS, TS)
-            out[k, 0, rows, :] = o[:TS, :NV] - o[TS:, NV:]
-            out[k, 1, rows, :] = o[:TS, NV:] + o[TS:, :NV]
-
-
-def product(cosine, sine, hop, G, vec, W, lists):
+            O[k, 0, rows, :] = o[:TS, :NV] - o[TS:, NV:]
+            O[k, 1, rows, :] = o[:TS, NV:] + o[TS:, :NV]
+            done.append(pltpu.make_async_copy(O.at[k, :, rows], out.at[k, :, rows], sems.at[35 + TR * k + r]))
+            done[-1].start()
+    for copy in done:
+        copy.wait()
+
+
+def product(phase, hop, G, vec, W, lists):
     any_space = pl.BlockSpec(memory_space=pl.ANY)
-    smem = pl.BlockSpec(memory_space=pltpu.SMEM)
     return pl.pallas_call(
         product_kernel,
         out_shape=jax.ShapeDtypeStruct((2, 2, BLK, NV), jnp.float32),
-        in_specs=[smem, smem] + [any_space] * 8,
-        out_specs=pl.BlockSpec(memory_space=pltpu.VMEM),
+        in_specs=[pl.BlockSpec(memory_space=pltpu.VMEM)] + [any_space] * 8,
+        out_specs=any_space,
         scratch_shapes=[
             pltpu.VMEM((4 * SLOTS, TS, TS), jnp.bfloat16),
             pltpu.VMEM((2, SPAN * TS, 2 * NV), jnp.bfloat16),
-            pltpu.VMEM((2, TR, 2 * TS, WIDE * TS), jnp.float32),
-            *[pltpu.SMEM((4, 1, SLOTS), jnp.int32)] * 4,
-            pltpu.SemaphoreType.DMA((34,)),
+            *[pltpu.VMEM((TR, 2 * TS, WIDE * TS), jnp.float32)] * 2,
+            pltpu.VMEM((2, 2, BLK, NV), jnp.float32),
+            *[pltpu.SMEM((4, 1, SLOTS), jnp.int32)] * 3,
+            pltpu.SMEM((4, 1, 1), jnp.int32),
+            pltpu.VMEM((4, NLAT), jnp.float32),
+            pltpu.SMEM((4, NLAT), jnp.float32),
+            pltpu.SemaphoreType.DMA((41,)),
         ],
         compiler_params=pltpu.CompilerParams(vmem_limit_bytes=60 * 1024 * 1024),
         name="product",
-    )(cosine, sine, hop, G, vec, W, *lists)
+    )(phase, hop, G, vec, W, *lists)
 
 
 def body(hoppings, tile_rows, tile_cols, tile_lats, tile_counts, phase_angle, vectors):
     hop = hoppings[0]
-    live = jnp.broadcast_to(tile_counts, (1, SLOTS))
-    G, W, *lists = gather_all(hop, (tile_rows, tile_cols, tile_lats, live), vectors)
-    return product(jnp.cos(phase_angle), jnp.sin(phase_angle), hop, G, vectors, W, lists)
+    G, W, *lists = gather_all(hop, (tile_rows, tile_cols, tile_lats, tile_counts), vectors)
+    return product(phase_angle, hop, G, vectors, W, lists)
 
 
 def solution(mesh):

time: 117 us -> 113 us (0.966); the launches traced: 115 us -> 113 us
    pallas_call x1, Pallas kernels: 93.2 us -> 92 us  [gather_all(): pl.pallas_call(gather_kernel, out_shape=(jax.ShapeDtypeStruct((3,) + hop....]
where the time goes in v4:
time: 113 us
  Pallas kernels  113 us (100%)
    pallas_call x1, Pallas kernels, gather_all(): pl.pallas_call(gather_kernel, out_shape=(jax.ShapeDtypeStruct((3,) + hop....  92 us
    pallas_call x1, Pallas kernels, product(): pl.pallas_call(product_kernel, out_shape=jax.ShapeDtypeStruct((2, 2, BLK,...  20.7 us

profile of v4, /device:TPU:1, one launch (start us, length us, event | category | flops | bytes accessed | tf_op | source)
XLA Modules:
  0.0 113.3 jit_solution(2047391608279399278)
XLA Ops:
  0.7 92.0 %gather.1 = (bf16[3,96,128,128]{3,2,1,0:T(8,128)(2,1)}, bf16[13,2,2,384,256]{4,3,2,1,0:T(8,128)(2,1)}, s32[4,1,96]{2,1,0:T(1,128)}, s32[4,1,96]{2,1,0:T(1,128)},...) custom-call(bf16[96,128,128]{2,1,0:T(8,128)(2,1)} %bitcast.1, ...), custom_call_target="tpu_custom_call" | custom-call | tf_op jit(solution)/shard_map/gather/pallas_call | solution.py:333
  92.6 20.7 %product.1 = f32[2,2,384,256]{3,2,1,0:T(8,128)} custom-call(f32[2,9]{1,0:T(2,128)} %phase.1, bf16[96,128,128]{2,1,0:T(8,128)(2,1)} %bitcast.2, bf16[3,96,128,128]{3,2,1,0:T(8,128)(2,1)} %get-tuple-element.11.G, bf16[2,2,384,256]{3,2,1,0:T(8,128)(2,1)} %vec.3, bf16[13,2,2,384,256]{4,3,2,1,0:T(8,128)(2,1)} %get-tuple-element.12.W, ...), custom_call_target="tpu_custom_call" | custom-call | tf_op jit(solution)/shard_map/product/pallas_call | solution.py:441

commit v5 on v4

--- a/solution.py
+++ b/solution.py
@@ -118,6 +118,7 @@
 
     lists = ((rows, CR), (cols, CC), (lats, CL), (live, CN))
     local = [pltpu.make_async_copy(src, dst.at[0], local_sem.at[i]) for i, (src, dst) in enumerate(lists)]
+    local += [pltpu.make_async_copy(vec.at[h], W.at[h, :, 6], local_sem.at[4 + h]) for h in HALVES]
     for copy in local:
         copy.start()
 
@@ -125,8 +126,8 @@
 
     def y_sends(u, h, only=None):
         dz = member[u] - z
-        src = vec.at[h] if u == 0 else W.at[6 + dz, h]
-        down_dst, up_dst = W.at[10 + dz, h], W.at[2 + dz, h]
+        src = vec.at[h] if u == 0 else W.at[h, :, 6 + dz]
+        down_dst, up_dst = W.at[h, :, 10 + dz], W.at[h, :, 2 + dz]
         down_ok, up_ok = (None, None) if u == 0 else (y > 0, y < 3)
         if only is not None:
             down_ok, up_ok = down_ok & only, up_ok & only
@@ -141,7 +142,7 @@
 
     def y_recvs(u, h):
         dz = member[u] - z
-        down_dst, up_dst = W.at[10 + dz, h], W.at[2 + dz, h]
+        down_dst, up_dst = W.at[h, :, 10 + dz], W.at[h, :, 2 + dz]
         down_ok, up_ok = (None, None) if u == 0 else (y < 3, y > 0)
         if u == 2:
             recv(f"y-{u}{h}", down_ok & (z >= 2), down_dst, up_y)
@@ -157,32 +158,32 @@
 
     def spread(h):
         a, b = (None, None) if h else (top, base)
-        send(f"a1{h}", both(a, z < 3), W.at[10, h], W.at[9, h], up_z)
-        send(f"b1{h}", both(b, z > 0), W.at[2, h], W.at[3, h], down_z)
-        send(f"a2{h}", a, W.at[10, h], W.at[jnp.where(low, 7, 11), h], down_z)
-        send(f"b2{h}", b, W.at[2, h], W.at[jnp.where(high, 5, 1), h], up_z)
+        send(f"a1{h}", both(a, z < 3), W.at[h, :, 10], W.at[h, :, 9], up_z)
+        send(f"b1{h}", both(b, z > 0), W.at[h, :, 2], W.at[h, :, 3], down_z)
+        send(f"a2{h}", a, W.at[h, :, 10], W.at[h, :, jnp.where(low, 7, 11)], down_z)
+        send(f"b2{h}", b, W.at[h, :, 2], W.at[h, :, jnp.where(high, 5, 1)], up_z)
 
     def spread_on(h):
         a, b = (None, None) if h else (top, base)
-        recv(f"a1{h}", both(a, z > 0), W.at[9, h], down_z)
-        recv(f"b1{h}", both(b, z < 3), W.at[3, h], up_z)
-        recv(f"a2{h}", a, W.at[jnp.where(high, 7, 11), h], up_z)
-        recv(f"b2{h}", b, W.at[jnp.where(low, 5, 1), h], down_z)
+        recv(f"a1{h}", both(a, z > 0), W.at[h, :, 9], down_z)
+        recv(f"b1{h}", both(b, z < 3), W.at[h, :, 3], up_z)
+        recv(f"a2{h}", a, W.at[h, :, jnp.where(high, 7, 11)], up_z)
+        recv(f"b2{h}", b, W.at[h, :, jnp.where(low, 5, 1)], down_z)
         if h:
-            send(f"a3{h}", mid, W.at[9, h], W.at[8, h], up_z)
-            send(f"b3{h}", mid, W.at[3, h], W.at[4, h], down_z)
+            send(f"a3{h}", mid, W.at[h, :, 9], W.at[h, :, 8], up_z)
+            send(f"b3{h}", mid, W.at[h, :, 3], W.at[h, :, 4], down_z)
         else:
-            send(f"a3{h}", both(a, low | high), W.at[jnp.where(low, 11, 7), h], W.at[8, h], down_z)
-            send(f"b3{h}", both(b, low | high), W.at[jnp.where(low, 5, 1), h], W.at[4, h], up_z)
-        send(f"a4{h}", both(a, mid), W.at[11, h, :, HEAD], W.at[12, h, :, HEAD], down_z)
-        send(f"b4{h}", both(b, mid), W.at[1, h, :, LAST], W.at[0, h, :, LAST], up_z)
+            send(f"a3{h}", both(a, low | high), W.at[h, :, jnp.where(low, 11, 7)], W.at[h, :, 8], down_z)
+            send(f"b3{h}", both(b, low | high), W.at[h, :, jnp.where(low, 5, 1)], W.at[h, :, 4], up_z)
+        send(f"a4{h}", both(a, mid), W.at[h, :, 11, HEAD], W.at[h, :, 12, HEAD], down_z)
+        send(f"b4{h}", both(b, mid), W.at[h, :, 1, LAST], W.at[h, :, 0, LAST], up_z)
 
     def spread_last(h):
         a, b = (None, None) if h else (top, base)
-        recv(f"a3{h}", both(a, z >= 2), W.at[8, h], down_z)
-        recv(f"b3{h}", both(b, z < 2), W.at[4, h], down_z)
-        recv(f"a4{h}", both(a, z < 2), W.at[12, h, :, HEAD], up_z)
-        recv(f"b4{h}", both(b, z >= 2), W.at[0, h, :, LAST], down_z)
+        recv(f"a3{h}", both(a, z >= 2), W.at[h, :, 8], down_z)
+        recv(f"b3{h}", both(b, z < 2), W.at[h, :, 4], down_z)
+        recv(f"a4{h}", both(a, z < 2), W.at[h, :, 12, HEAD], up_z)
+        recv(f"b4{h}", both(b, z >= 2), W.at[h, :, 0, LAST], down_z)
 
     near_to, near_from = (low & (y > 0)) | (high & (y < 3)), (low & (y < 3)) | (high & (y > 0))
     near = at(xh, jnp.where(low, ym, yp), z)
@@ -194,23 +195,22 @@
     got, got_part = jnp.where(low, 1, 11), jnp.where(low, 0, 12)
 
     def second(h):
-        send(f"d{h}", near_to, W.at[block, h], X.at[0, h], near)
+        send(f"d{h}", near_to, W.at[h, :, block], X.at[0, h], near)
 
     def second_part(h, ok):
-        send(f"dp{h}", near_to & ok, W.at[beside, h, :, tail(low)], X.at[1, h, :, tail(low)], near)
+        send(f"dp{h}", near_to & ok, W.at[h, :, beside, tail(low)], X.at[1, h, :, tail(low)], near)
 
     crossed = jnp.where(y == 1, 3, 9)
 
     def cross():
-        send("g0", crossing, W.at[crossed, 0], S.at[0, 0], mirror)
-
-    z_dst_up, z_dst_down = W.at[6 + z - zp], W.at[6 + z - zm]
+        send("g0", crossing, W.at[0, :, crossed], S.at[0, 0], mirror)
+
     y_sends(0, 1)
-    send("z-0", None, vec.at[0], z_dst_up.at[0], up_z)
-    send("z+1", None, vec.at[1], z_dst_down.at[1], down_z)
+    send("z-0", None, vec.at[0], W.at[0, :, 6 + z - zp], up_z)
+    send("z+1", None, vec.at[1], W.at[1, :, 6 + z - zm], down_z)
     y_sends(0, 0)
-    send("z-1", None, vec.at[1], z_dst_up.at[1], up_z)
-    send("z+0", None, vec.at[0], z_dst_down.at[0], down_z)
+    send("z-1", None, vec.at[1], W.at[1, :, 6 + z - zp], up_z)
+    send("z+0", None, vec.at[0], W.at[0, :, 6 + z - zm], down_z)
     for h in HALVES:
         send(f"gp{h}", part_sender, vec.at[h, :, tail(y == 1)], S.at[1, h, :, tail(y == 1)], part_to)
 
@@ -239,19 +239,19 @@
             send(f"c{flip}{i}", None, src, dst.at[flip], along(flip))
     send("sib", None, hop, G.at[0], along(1))
 
-    recv("z-0", None, W.at[6 + zm - z, 0], down_z)
-    send("w0", None, W.at[6 + zm - z, 0], W.at[6 + zm - zp, 0], up_z)
+    recv("z-0", None, W.at[0, :, 6 + zm - z], down_z)
+    send("w0", None, W.at[0, :, 6 + zm - z], W.at[0, :, 6 + zm - zp], up_z)
     y_sends(-1, 0)
-    recv("z+1", None, W.at[6 + zp - z, 1], up_z)
-    send("w1", None, W.at[6 + zp - z, 1], W.at[6 + zp - zm, 1], down_z)
+    recv("z+1", None, W.at[1, :, 6 + zp - z], up_z)
+    send("w1", None, W.at[1, :, 6 + zp - z], W.at[1, :, 6 + zp - zm], down_z)
     recv("g1", split, S.at[0, 1], mirror)
     send("e1", split, S.at[0, 1], E.at[0, 1], over)
     y_recvs(0, 1)
     spread(1)
     second(1)
-    recv("z+0", None, W.at[6 + zp - z, 0], up_z)
+    recv("z+0", None, W.at[0, :, 6 + zp - z], up_z)
     y_sends(1, 0)
-    recv("z-1", None, W.at[6 + zm - z, 1], down_z)
+    recv("z-1", None, W.at[1, :, 6 + zm - z], down_z)
     cross()
     recv("r", ~outer, R.at[0], beside_y)
     send("q", ~outer, R.at[0], R.at[1], along(2))
@@ -260,12 +260,12 @@
     y_recvs(0, 0)
     second(0)
     spread(0)
-    recv("w0", None, W.at[6 + z2 - z, 0], down_z)
+    recv("w0", None, W.at[0, :, 6 + z2 - z], down_z)
     y_sends(2, 0, ~crossing)
-    recv("w1", None, W.at[6 + z2 - z, 1], up_z)
+    recv("w1", None, W.at[1, :, 6 + z2 - z], up_z)
     for h in (1, 0):
         recv(f"d{h}", near_from, X.at[0, h], near_src)
-        send(f"f{h}", near_from, X.at[0, h], W.at[far, h], across)
+        send(f"f{h}", near_from, X.at[0, h], W.at[h, :, far], across)
     recv("g0", crossing, S.at[0, 0], mirror)
     send("e0", crossing, S.at[0, 0], E.at[0, 0], beside_y)
     y_sends(2, 0, crossing)
@@ -274,11 +274,11 @@
         send(f"ep{h}", crossing, S.at[1, h, :, tail(y == 1)], E.at[1, h, :, tail(y == 1)], beside_y)
     def onward(h):
         recv(f"e{h}", relay, E.at[0, h], split_from if h else over_from)
-        send(f"f{h}", relay, E.at[0, h], W.at[got, h], inner_y)
+        send(f"f{h}", relay, E.at[0, h], W.at[h, :, got], inner_y)
 
     def onward_part(h):
         recv(f"ep{h}", relay, E.at[1, h, :, tail(high)], over_from)
-        send(f"fp{h}", relay, E.at[1, h, :, tail(high)], W.at[got_part, h, :, tail(high)], inner_y)
+        send(f"fp{h}", relay, E.at[1, h, :, tail(high)], W.at[h, :, got_part, tail(high)], inner_y)
 
     y_recvs(-1, 0)
     y_recvs(1, 0)
@@ -297,19 +297,19 @@
         forward(c)
     for h in HALVES:
         recv(f"dp{h}", near_from, X.at[1, h, :, tail(low)], near_src)
-        send(f"fp{h}", near_from, X.at[1, h, :, tail(low)], W.at[far_part, h, :, tail(low)], across)
+        send(f"fp{h}", near_from, X.at[1, h, :, tail(low)], W.at[h, :, far_part, tail(low)], across)
     rim = low | high
     next_to = at(xh, y, jnp.where(low, 1, 2))
     for h in (1, 0):
-        recv(f"f{h}", rim, W.at[got, h], across)
-        send(f"l{h}", rim, W.at[got, h, :, tail(high)], W.at[got_part, h, :, tail(high)], next_to)
+        recv(f"f{h}", rim, W.at[h, :, got], across)
+        send(f"l{h}", rim, W.at[h, :, got, tail(high)], W.at[h, :, got_part, tail(high)], next_to)
     for c in range(3, CHUNKS - 2):
         forward(c)
     y_recvs(2, 0)
     for h in HALVES:
         spread_last(h)
-        recv(f"fp{h}", rim, W.at[got_part, h, :, tail(high)], across)
-        recv(f"l{h}", mid, W.at[jnp.where(z == 1, 0, 12), h, :, tail(z == 2)], at(xh, y, jnp.where(z == 1, 0, 3)))
+        recv(f"fp{h}", rim, W.at[h, :, got_part, tail(high)], across)
+        recv(f"l{h}", mid, W.at[h, :, jnp.where(z == 1, 0, 12), tail(z == 2)], at(xh, y, jnp.where(z == 1, 0, 3)))
     for flip in (1, 2, 3):
         for i, (_, dst) in enumerate(lists):
             recv(f"c{flip}{i}", None, dst.at[flip], along(flip))
@@ -334,50 +334,33 @@
         gather_kernel,
         out_shape=(
             jax.ShapeDtypeStruct((3,) + hop.shape, hop.dtype),
-            jax.ShapeDtypeStruct((13,) + block, vec.dtype),
+            jax.ShapeDtypeStruct(block[:2] + (13,) + block[2:], vec.dtype),
             *[jax.ShapeDtypeStruct((4,) + a.shape, a.dtype) for a in lists],
             *[jax.ShapeDtypeStruct((2,) + block, vec.dtype)] * 3,
             jax.ShapeDtypeStruct((2, AROUND) + hop.shape[1:], hop.dtype),
         ),
-        in_specs=[any_space] * 6,
+        in_specs=[pl.BlockSpec(memory_space=pltpu.HBM)] * 6,
         out_specs=(any_space,) * 10,
         scratch_shapes=[
             pltpu.SemaphoreType.DMA((sems,)),
             pltpu.SemaphoreType.DMA((sems,)),
-            pltpu.SemaphoreType.DMA((4,)),
+            pltpu.SemaphoreType.DMA((6,)),
         ],
-        compiler_params=pltpu.CompilerParams(collective_id=0, has_side_effects=True),
+        compiler_params=pltpu.CompilerParams(
+            collective_id=0, has_side_effects=True, vmem_limit_bytes=1024 * 1024
+        ),
         name="gather",
     )(hop, *lists, vec)[:6]
 
 
-def product_kernel(phase, hop, G, vec, W, CR, CC, CL, CN, out, T, V, H0, H1, O, NR, NC, NL, NN, factor, table, sems):
+def product_kernel(phase, hop, G, W, CR, CC, CL, CN, out, H0, H1, O, NR, NC, NL, NN, factor, table, sems):
     row = lax.axis_index("rows")
-    copies = [pltpu.make_async_copy(hop, T.at[pl.ds(0, SLOTS)], sems.at[0])]
-    for m in range(3):
-        copies.append(
-            pltpu.make_async_copy(G.at[m], T.at[pl.ds((m + 1) * SLOTS, SLOTS)], sems.at[m + 1])
-        )
     H = (H0, H1)
-    windows = []
-    for j in range(13):
-        for q in range(2):
-            lanes = pl.ds(q * NV, NV)
-            if j == 0:
-                src, start, size = W.at[j, :, q, pl.ds(2 * TS, TS)], 0, TS
-            elif j == 12:
-                src, start, size = W.at[j, :, q, pl.ds(0, TS)], (SPAN - 1) * TS, TS
-            else:
-                src = vec.at[:, q] if j == 6 else W.at[j, :, q]
-                start, size = (TR * (j - 6) + BAND) * TS, BLK
-            windows.append(
-                pltpu.make_async_copy(src, V.at[:, pl.ds(start, size), lanes], sems.at[4 + 2 * j + q])
-            )
     scalars = [
         pltpu.make_async_copy(src, dst, sems.at[30 + i])
         for i, (src, dst) in enumerate(((CR, NR), (CC, NC), (CL, NL), (CN, NN)))
     ]
-    for copy in scalars + copies:
+    for copy in scalars:
         copy.start()
     factor[0:2, :] = jnp.cos(phase[...])
     factor[2:4, :] = jnp.sin(phase[...])
@@ -396,13 +379,10 @@
         copy.wait()
     part = 32
     for m in range(4):
-        copies[m].wait()
-        if m == 1:
-            for copy in windows:
-                copy.start()
         count = NN[m, 0, 0]
-
-        def add(i, _, m=m, count=count):
+        slots = G.at[m - 1] if m else hop
+
+        def add(i, _, m=m, count=count, slots=slots):
             for one in [GROUP * i + j for j in range(GROUP)]:
                 r = jnp.clip(NR[m, 0, one] - row * TR, 0, TR - 1)
                 w = NC[m, 0, one] - (row * TR + r - BAND)
@@ -412,40 +392,44 @@
                 lat = NL[m, 0, one]
                 scale = [jnp.where(one < count, table[2 * p + k, lat], 0.0) for k in range(2) for p in range(2)]
                 for at in range(0, TS, part):
-                    tile = T[m * SLOTS + one, pl.ds(at, part), :].astype(jnp.float32)
+                    tile = slots[one, pl.ds(at, part), :].astype(jnp.float32)
                     for k in range(2):
                         for p in range(2):
                             H[k][r, pl.ds(p * TS + at, part), cols] += tile * scale[2 * k + p]
             return 0
 
         lax.fori_loop(0, (count + GROUP - 1) // GROUP, add, 0)
-    for copy in windows:
-        copy.wait()
     done = []
     for k in range(2):
         for r in range(TR):
-            o = jnp.dot(
-                H[k][r].astype(jnp.bfloat16), V[k, pl.ds(r * TS, WIDE * TS), :], preferred_element_type=jnp.float32
-            )
+            left = H[k][r].astype(jnp.bfloat16)
             rows = pl.ds(r * TS, TS)
-            O[k, 0, rows, :] = o[:TS, :NV] - o[TS:, NV:]
-            O[k, 1, rows, :] = o[:TS, NV:] + o[TS:, :NV]
+            first = (r + 2) * TS
+            o = [
+                jnp.dot(
+                    left,
+                    W[k, q].reshape(13 * BLK, NV)[first : first + WIDE * TS],
+                    preferred_element_type=jnp.float32,
+                )
+                for q in range(2)
+            ]
+            O[k, 0, rows, :] = o[0][:TS] - o[1][TS:]
+            O[k, 1, rows, :] = o[1][:TS] + o[0][TS:]
             done.append(pltpu.make_async_copy(O.at[k, :, rows], out.at[k, :, rows], sems.at[35 + TR * k + r]))
             done[-1].start()
     for copy in done:
         copy.wait()
 
 
-def product(phase, hop, G, vec, W, lists):
+def product(phase, hop, G, W, lists):
     any_space = pl.BlockSpec(memory_space=pl.ANY)
+    vmem = pl.BlockSpec(memory_space=pltpu.VMEM)
     return pl.pallas_call(
         product_kernel,
         out_shape=jax.ShapeDtypeStruct((2, 2, BLK, NV), jnp.float32),
-        in_specs=[pl.BlockSpec(memory_space=pltpu.VMEM)] + [any_space] * 8,
+        in_specs=[vmem] * 4 + [any_space] * 4,
         out_specs=any_space,
         scratch_shapes=[
-            pltpu.VMEM((4 * SLOTS, TS, TS), jnp.bfloat16),
-            pltpu.VMEM((2, SPAN * TS, 2 * NV), jnp.bfloat16),
             *[pltpu.VMEM((TR, 2 * TS, WIDE * TS), jnp.float32)] * 2,
             pltpu.VMEM((2, 2, BLK, NV), jnp.float32),
             *[pltpu.SMEM((4, 1, SLOTS), jnp.int32)] * 3,
@@ -454,15 +438,15 @@
             pltpu.SMEM((4, NLAT), jnp.float32),
             pltpu.SemaphoreType.DMA((41,)),
         ],
-        compiler_params=pltpu.CompilerParams(vmem_limit_bytes=60 * 1024 * 1024),
+        compiler_params=pltpu.CompilerParams(vmem_limit_bytes=31 * 1024 * 1024),
         name="product",
-    )(phase, hop, G, vec, W, *lists)
+    )(phase, hop, G, W, *lists)
 
 
 def body(hoppings, tile_rows, tile_cols, tile_lats, tile_counts, phase_angle, vectors):
     hop = hoppings[0]
     G, W, *lists = gather_all(hop, (tile_rows, tile_cols, tile_lats, tile_counts), vectors)
-    return product(phase_angle, hop, G, vectors, W, lists)
+    return product(phase_angle, hop, G, W, lists)
 
 
 def solution(mesh):

time: 113 us -> 116 us (1.027)
  local copies, waits for them, and re-layouts: 0 us -> 4.99 us
  Pallas kernels: 113 us -> 111 us
    unnamed x0 -> x14, local copies, waits for them, and re-layouts: none -> 4.99 us
    pallas_call x1, Pallas kernels: 20.7 us -> 19.3 us  [product(): pl.pallas_call(product_kernel, out_shape=jax.ShapeDtypeStruct((2, 2, BLK,...]
where the time goes in v5:
time: 116 us
  Pallas kernels  111 us (96%)
  local copies, waits for them, and re-layouts  4.99 us (4%)
    pallas_call x1, Pallas kernels, gather_all(): pl.pallas_call(gather_kernel, out_shape=(jax.ShapeDtypeStruct((3,) + hop....  91.4 us
    pallas_call x1, Pallas kernels, product(): pl.pallas_call(product_kernel, out_shape=jax.ShapeDtypeStruct((2, 2, BLK,...  19.3 us
    unnamed x14, local copies, waits for them, and re-layouts  4.99 us

profile of v5, /device:TPU:1, one launch (start us, length us, event | category | flops | bytes accessed | tf_op | source)
XLA Modules:
  0.0 116.3 jit_solution(8034739600709511381)
XLA Ops:
  0.7 0.0 copy-start
  0.7 1.9 %copy-done = bf16[1,96,128,128]{3,2,1,0:T(8,128)(2,1)S(1)} copy-done((bf16[1,96,128,128]{3,2,1,0:T(8,128)(2,1)S(1)}, bf16[1,96,128,128]{3,2,1,0:T(8,128)(2,1)}, u32[]{:S(2)}) %copy-start) | copy-done | bytes 3145752
  2.5 0.0 copy-start.2
  2.5 1.1 copy-done.2
  3.7 0.0 copy-start.4
  3.7 0.7 copy-done.4
  4.3 0.0 copy-start.5
  4.3 0.7 copy-done.5
  5.0 0.0 copy-start.6
  5.0 0.7 copy-done.6
  5.6 0.0 copy-start.1
  5.6 0.0 copy-start.3
  5.6 91.4 %gather.1 = (bf16[3,96,128,128]{3,2,1,0:T(8,128)(2,1)S(1)}, bf16[2,2,13,384,256]{4,3,2,1,0:T(8,128)(2,1)S(1)}, s32[4,1,96]{2,1,0:T(1,128)S(1)}, s32[4,1,96]{2,1,...) custom-call(bf16[96,128,128]{2,1,0:T(8,128)(2,1)S(1)} %bitcast.1, ...), custom_call_target="tpu_custom_call" | custom-call | tf_op jit(solution)/shard_map/gather/pallas_call | solution.py:333
  97.1 0.0 copy-done.1
  97.1 0.0 copy-done.3
  97.1 19.3 %product.1 = f32[2,2,384,256]{3,2,1,0:T(8,128)} custom-call(f32[2,9]{1,0:T(2,128)S(1)} %copy-done.3, bf16[96,128,128]{2,1,0:T(8,128)(2,1)S(1)} %bitcast.2, bf16[3,96,128,128]{3,2,1,0:T(8,128)(2,1)S(1)} %get-tuple-element.11.G, bf16[2,2,13,384,256]{4,3,2,1,0:T(8,128)(2,1)S(1)} %get-tuple-element.12.W, s32[4,1,96]{2,1,0:T(1,128)S(1)} %get-tuple-element.13.CR, ...), custom_call_target="tpu_custom_call" | custom-call | tf_op jit(solution)/shard_map/product/pallas_call | solution.py:427
Async XLA Ops:
  0.7 1.9 %copy-start = (bf16[1,96,128,128]{3,2,1,0:T(8,128)(2,1)S(1)}, bf16[1,96,128,128]{3,2,1,0:T(8,128)(2,1)}, u32[]{:S(2)}) copy-start(bf16[1,96,128,128]{3,2,1,0:T(8,128)(2,1)} %param.7) | copy-start | bytes 9437188
  2.5 1.1 copy-start.2
  3.7 0.7 copy-start.4
  4.3 0.7 copy-start.5
  5.0 0.7 copy-start.6
  5.6 91.4 %copy-start.1 = (bf16[1,96,128,128]{3,2,1,0:T(8,128)(2,1)S(1)}, bf16[1,96,128,128]{3,2,1,0:T(8,128)(2,1)}, u32[]{:S(2)}) copy-start(bf16[1,96,128,128]{3,2,1,0:T(8,128)(2,1)} %param.7) | copy-start | bytes 9437188
  5.6 91.4 %copy-start.3 = (f32[2,9]{1,0:T(2,128)S(1)}, f32[2,9]{1,0:T(2,128)}, u32[]{:S(2)}) copy-start(f32[2,9]{1,0:T(2,128)} %phase.1) | copy-start | bytes 220

commit v6 on v5

--- a/solution.py
+++ b/solution.py
@@ -18,6 +18,7 @@
 CHUNKS = 8
 PER = SLOTS // CHUNKS
 AROUND = 6
+GATHER_VMEM = 1024 * 1024
 GROUP = 4
 WIDE = 2 * BAND + 1
 SPAN = WIDE + TR - 1
@@ -119,6 +120,7 @@
     lists = ((rows, CR), (cols, CC), (lats, CL), (live, CN))
     local = [pltpu.make_async_copy(src, dst.at[0], local_sem.at[i]) for i, (src, dst) in enumerate(lists)]
     local += [pltpu.make_async_copy(vec.at[h], W.at[h, :, 6], local_sem.at[4 + h]) for h in HALVES]
+    local.append(pltpu.make_async_copy(hop, G.at[0], local_sem.at[6]))
     for copy in local:
         copy.start()
 
@@ -222,12 +224,12 @@
 
     def chunk(c):
         for name, when, part in pieces(c):
-            send(f"x{name}", when, hop.at[part], G.at[1, part], along(2))
+            send(f"x{name}", when, hop.at[part], G.at[2, part], along(2))
 
     def forward(c):
         for name, when, part in pieces(c):
-            recv(f"x{name}", when, G.at[1, part], along(2))
-            send(f"o{name}", when, G.at[1, part], G.at[2, part], along(1))
+            recv(f"x{name}", when, G.at[2, part], along(2))
+            send(f"o{name}", when, G.at[2, part], G.at[3, part], along(1))
 
     around = pl.ds(SLOTS - AROUND, AROUND)
     send("g1", split, vec.at[1], S.at[0, 1], mirror)
@@ -237,7 +239,7 @@
     for flip in (1, 2, 3):
         for i, (src, dst) in enumerate(lists):
             send(f"c{flip}{i}", None, src, dst.at[flip], along(flip))
-    send("sib", None, hop, G.at[0], along(1))
+    send("sib", None, hop, G.at[1], along(1))
 
     recv("z-0", None, W.at[0, :, 6 + zm - z], down_z)
     send("w0", None, W.at[0, :, 6 + zm - z], W.at[0, :, 6 + zm - zp], up_z)
@@ -292,7 +294,7 @@
     for h in HALVES:
         onward_part(h)
     recv("q", ~outer, R.at[1], along(2))
-    send("p", ~outer, R.at[1], G.at[1, around], beside_y)
+    send("p", ~outer, R.at[1], G.at[2, around], beside_y)
     for c in range(3):
         forward(c)
     for h in HALVES:
@@ -313,14 +315,14 @@
     for flip in (1, 2, 3):
         for i, (_, dst) in enumerate(lists):
             recv(f"c{flip}{i}", None, dst.at[flip], along(flip))
-    recv("sib", None, G.at[0], along(1))
-    recv("p", outer, G.at[1, around], beside_y)
-    send("of", outer, G.at[1, around], G.at[2, around], along(1))
+    recv("sib", None, G.at[1], along(1))
+    recv("p", outer, G.at[2, around], beside_y)
+    send("of", outer, G.at[2, around], G.at[3, around], along(1))
     for c in range(CHUNKS - 2, CHUNKS):
         forward(c)
     for c in range(CHUNKS):
         for name, _, part in pieces(c):
-            recv(f"o{name}", None, G.at[2, part], along(1))
+            recv(f"o{name}", None, G.at[3, part], along(1))
     net.finish()
     for copy in local:
         copy.wait()
@@ -333,27 +335,27 @@
     return pl.pallas_call(
         gather_kernel,
         out_shape=(
-            jax.ShapeDtypeStruct((3,) + hop.shape, hop.dtype),
-            jax.ShapeDtypeStruct(block[:2] + (13,) + block[2:], vec.dtype),
+            pltpu.VMEM((4,) + hop.shape, hop.dtype),
+            pltpu.VMEM(block[:2] + (13,) + block[2:], vec.dtype),
             *[jax.ShapeDtypeStruct((4,) + a.shape, a.dtype) for a in lists],
-            *[jax.ShapeDtypeStruct((2,) + block, vec.dtype)] * 3,
-            jax.ShapeDtypeStruct((2, AROUND) + hop.shape[1:], hop.dtype),
+            *[pltpu.VMEM((2,) + block, vec.dtype)] * 3,
+            pltpu.VMEM((2, AROUND) + hop.shape[1:], hop.dtype),
         ),
         in_specs=[pl.BlockSpec(memory_space=pltpu.HBM)] * 6,
         out_specs=(any_space,) * 10,
         scratch_shapes=[
             pltpu.SemaphoreType.DMA((sems,)),
             pltpu.SemaphoreType.DMA((sems,)),
-            pltpu.SemaphoreType.DMA((6,)),
+            pltpu.SemaphoreType.DMA((7,)),
         ],
         compiler_params=pltpu.CompilerParams(
-            collective_id=0, has_side_effects=True, vmem_limit_bytes=1024 * 1024
+            collective_id=0, has_side_effects=True, vmem_limit_bytes=GATHER_VMEM
         ),
         name="gather",
-    )(hop, *lists, vec)[:6]
-
-
-def product_kernel(phase, hop, G, W, CR, CC, CL, CN, out, H0, H1, O, NR, NC, NL, NN, factor, table, sems):
+    )(*[a if a.size == 1 else pltpu.with_memory_space_constraint(a, pltpu.HBM) for a in (hop, *lists, vec)])[:6]
+
+
+def product_kernel(phase, G, W, CR, CC, CL, CN, out, H0, H1, O, NR, NC, NL, NN, factor, table, sems):
     row = lax.axis_index("rows")
     H = (H0, H1)
     scalars = [
@@ -380,7 +382,7 @@
     part = 32
     for m in range(4):
         count = NN[m, 0, 0]
-        slots = G.at[m - 1] if m else hop
+        slots = G.at[m]
 
         def add(i, _, m=m, count=count, slots=slots):
             for one in [GROUP * i + j for j in range(GROUP)]:
@@ -421,13 +423,13 @@
         copy.wait()
 
 
-def product(phase, hop, G, W, lists):
+def product(phase, G, W, lists):
     any_space = pl.BlockSpec(memory_space=pl.ANY)
     vmem = pl.BlockSpec(memory_space=pltpu.VMEM)
     return pl.pallas_call(
         product_kernel,
         out_shape=jax.ShapeDtypeStruct((2, 2, BLK, NV), jnp.float32),
-        in_specs=[vmem] * 4 + [any_space] * 4,
+        in_specs=[vmem] * 3 + [any_space] * 4,
         out_specs=any_space,
         scratch_shapes=[
             *[pltpu.VMEM((TR, 2 * TS, WIDE * TS), jnp.float32)] * 2,
@@ -440,13 +442,13 @@
         ],
         compiler_params=pltpu.CompilerParams(vmem_limit_bytes=31 * 1024 * 1024),
         name="product",
-    )(phase, hop, G, W, *lists)
+    )(phase, G, W, *lists)
 
 
 def body(hoppings, tile_rows, tile_cols, tile_lats, tile_counts, phase_angle, vectors):
     hop = hoppings[0]
     G, W, *lists = gather_all(hop, (tile_rows, tile_cols, tile_lats, tile_counts), vectors)
-    return product(phase_angle, hop, G, W, lists)
+    return product(phase_angle, G, W, lists)
 
 
 def solution(mesh):

time: 116 us -> 111 us (0.957)
  local copies, waits for them, and re-layouts: 4.99 us -> 0.01 us
    unnamed x14 -> x2, local copies, waits for them, and re-layouts: 4.99 us -> 0.01 us
where the time goes in v6:
time: 111 us
  Pallas kernels  111 us (100%)
    pallas_call x1, Pallas kernels, gather_all(): pl.pallas_call(gather_kernel, out_shape=(pltpu.VMEM((4,) + hop.shape, hop...  91.6 us
    pallas_call x1, Pallas kernels, product(): pl.pallas_call(product_kernel, out_shape=jax.ShapeDtypeStruct((2, 2, BLK,...  19 us

profile of v6, /device:TPU:1, one launch (start us, length us, event | category | flops | bytes accessed | tf_op | source)
XLA Modules:
  0.0 111.2 jit_solution(3378235909191867452)
XLA Ops:
  0.7 0.0 copy-start
  0.7 91.6 %gather.1 = (bf16[4,96,128,128]{3,2,1,0:T(8,128)(2,1)S(1)}, bf16[2,2,13,384,256]{4,3,2,1,0:T(8,128)(2,1)S(1)}, s32[4,1,96]{2,1,0:T(1,128)S(1)}, s32[4,1,96]{2,1,...) custom-call(bf16[96,128,128]{2,1,0:T(8,128)(2,1)} %bitcast.1, ...), custom_call_target="tpu_custom_call" | custom-call | tf_op jit(solution)/shard_map/gather/pallas_call | solution.py:335
  92.3 0.0 copy-done
  92.3 19.0 %product.1 = f32[2,2,384,256]{3,2,1,0:T(8,128)} custom-call(f32[2,9]{1,0:T(2,128)S(1)} %copy-done, bf16[4,96,128,128]{3,2,1,0:T(8,128)(2,1)S(1)} %get-tuple-element.11.G, bf16[2,2,13,384,256]{4,3,2,1,0:T(8,128)(2,1)S(1)} %get-tuple-element.12.W, s32[4,1,96]{2,1,0:T(1,128)S(1)} %get-tuple-element.13.CR, s32[4,1,96]{2,1,0:T(1,128)S(1)} %get-tuple-element.14.CC, ...), custom_call_target="tpu_custom_call" | custom-call | tf_op jit(solution)/shard_map/product/pallas_call | solution.py:429
Async XLA Ops:
  0.7 91.6 %copy-start = (f32[2,9]{1,0:T(2,128)S(1)}, f32[2,9]{1,0:T(2,128)}, u32[]{:S(2)}) copy-start(f32[2,9]{1,0:T(2,128)} %phase.1) | copy-start | bytes 220

commit v7 on v6

v7 whole, which is shorter than its diff:
```python
import functools

import jax
import jax.numpy as jnp
from jax import lax
from jax.experimental import pallas as pl
from jax.experimental.pallas import tpu as pltpu
from jax.sharding import PartitionSpec as P

MESH = pl.DeviceIdType.MESH
BAND = 16
NLAT = 9
TS = 128
NV = 256
TR = 3
BLK = TR * TS
SLOTS = 96
CHUNKS = 8
PER = SLOTS // CHUNKS
AROUND = 6
GATHER_VMEM = 1024 * 1024
GROUP = 4
DEPTH = 2
CUT = 16
WIDE = 2 * BAND + 1
MATRIX = (TR, 2 * TS, WIDE * TS)
SPAN = WIDE + TR - 1
TORB = 96
HALVES = (0, 1)


class Net:
    def __init__(self, send_sem, recv_sem):
        self.send_sem, self.recv_sem = send_sem, recv_sem
        self.index, self.sent = {}, []

    def copy(self, name, src, dst, device):
        at = self.index.setdefault(name, len(self.index))
        return pltpu.make_async_remote_copy(
            src_ref=src, dst_ref=dst, send_sem=self.send_sem.at[at], recv_sem=self.recv_sem.at[at],
            device_id=device, device_id_type=MESH,
        )

    def send(self, name, when, src, dst, device):
        copy = self.copy(name, src, dst, device)
        self.sent.append((when, copy))
        guarded(when, copy.start)

    def recv(self, name, when, dst, device):
        guarded(when, self.copy(name, dst, dst, device).wait_recv)

    def finish(self):
        for when, copy in self.sent:
            guarded(when, copy.wait_send)


def guarded(when, action):
    if when is None:
        action()
    else:
        pl.when(when)(action)


def gather_kernel(
    angles, hop, rows, cols, lats, live, vec, GA, GB, W, H0, H1, U, CR, CC, CL, CN, S, X, E, R,
    phase, picks, factors, pick, factor, send_sem, recv_sem, local_sem,
):
    ka = lax.axis_index("ka")
    row = lax.axis_index("rows")
    xh, y, z = row // 16, (row // 4) % 4, row % 4
    zp, zm, z2 = (z + 1) % 4, (z + 3) % 4, (z + 2) % 4
    yp, ym = (y + 1) % 4, (y + 3) % 4

    def at(h, i, j):
        return (ka, h * 16 + i * 4 + j)

    def along(flip):
        other = (1 - ka % 2) if flip % 2 else ka % 2
        pair = (1 - ka // 2) if flip // 2 else ka // 2
        return (pair * 2 + other, row)

    up_z, down_z, up_y, down_y = at(xh, y, zp), at(xh, y, zm), at(xh, yp, z), at(xh, ym, z)
    mirror = at(1 - xh, y, z)
    low, high = z == 0, z == 3
    mid = (z == 1) | (z == 2)
    top, base = y == 3, y == 0
    down_y = at(jnp.where(base, 1 - xh, xh), ym, z)
    up_y = at(jnp.where(top, 1 - xh, xh), yp, z)
    inner_y = at(xh, jnp.where(base, 3, jnp.where(top, 0, y)), z)
    crossing = ((y == 1) & high) | ((y == 2) & low)
    part_sender = ((y == 1) & (z == 1)) | ((y == 2) & (z == 2))
    part_to = at(1 - xh, y, jnp.where(y == 1, 3, 0))
    part_from = at(1 - xh, y, jnp.where(y == 1, 1, 2))
    split = ((y == 1) & low) | ((y == 2) & high)
    outer = base | top
    beside_y = at(xh, jnp.where(y < 2, 1 - y, 5 - y), z)
    over = at(xh, jnp.where(y == 1, 0, 3), jnp.where(y == 1, 3, 0))
    over_from = at(xh, jnp.where(base, 1, 2), z)
    split_from = at(xh, jnp.where(base, 1, 2), 3 - z)
    relay = (base & high) | (top & low)
    relayed = (top & high) | (base & low)
    barrier = pltpu.get_barrier_semaphore()

    def greet(peer):
        pl.semaphore_signal(barrier, inc=1, device_id=peer, device_id_type=MESH)

    for peer in (along(1), along(2), along(3), up_z, down_z, up_y, down_y):
        greet(peer)
    pl.when(part_sender)(lambda: greet(part_to))
    pl.when(crossing)(lambda: greet(part_from))
    pl.when(crossing | split)(lambda: greet(mirror))
    pl.when(split)(lambda: greet(over))
    pl.when(relay)(lambda: greet(split_from))
    pl.when(relay | relayed)(lambda: greet(inner_y))
    extra = jnp.where(part_sender, 1, 0) + jnp.where(crossing | split, 2, 0)
    extra = extra + jnp.where(relay | relayed, 1, 0) + jnp.where(relay, 1, 0)
    pl.semaphore_wait(barrier, 7 + extra)

    def window(j, h, part=None):
        shift, size = (0, BLK) if part is None else (part.start, part.size)
        return W.at[h, :, pl.ds(pl.multiple_of((TR * j - 2) * TS + shift, TS), size)]

    net = Net(send_sem, recv_sem)
    send, recv = net.send, net.recv
    HEAD, LAST = pl.ds(0, TS), pl.ds(2 * TS, TS)

    def tail(first):
        return pl.ds(pl.multiple_of(jnp.where(first, 0, 2 * TS), TS), TS)

    lists = ((rows, CR), (cols, CC), (lats, CL), (live, CN))
    local = [pltpu.make_async_copy(src, dst.at[0], local_sem.at[i]) for i, (src, dst) in enumerate(lists)]
    local += [pltpu.make_async_copy(vec.at[h], window(6, h), local_sem.at[4 + h]) for h in HALVES]
    local.append(pltpu.make_async_copy(angles, phase, local_sem.at[9]))
    local.append(pltpu.make_async_copy(hop, GA.at[pl.ds(0, SLOTS)], local_sem.at[6]))
    for copy in local:
        copy.start()

    member = {0: z, -1: zm, 1: zp, 2: z2}

    def y_sends(u, h, only=None):
        dz = member[u] - z
        src = vec.at[h] if u == 0 else window(6 + dz, h)
        down_dst, up_dst = window(10 + dz, h), window(2 + dz, h)
        down_ok, up_ok = (None, None) if u == 0 else (y > 0, y < 3)
        if only is not None:
            down_ok, up_ok = down_ok & only, up_ok & only
        if u == 2:
            send(f"y-{u}{h}", down_ok & (z >= 2), src, down_dst, down_y)
            send(f"y-{u}{h}", down_ok & (z < 2), src.at[:, HEAD], window(10 + dz, h, HEAD), down_y)
            send(f"y+{u}{h}", up_ok & (z < 2), src, up_dst, up_y)
            send(f"y+{u}{h}", up_ok & (z >= 2), src.at[:, LAST], window(2 + dz, h, LAST), up_y)
        else:
            send(f"y-{u}{h}", down_ok & (z != 0) if u == -1 else down_ok, src, down_dst, down_y)
            send(f"y+{u}{h}", up_ok & (z != 3) if u == 1 else up_ok, src, up_dst, up_y)

    def y_recvs(u, h):
        dz = member[u] - z
        down_dst, up_dst = window(10 + dz, h), window(2 + dz, h)
        down_ok, up_ok = (None, None) if u == 0 else (y < 3, y > 0)
        if u == 2:
            recv(f"y-{u}{h}", down_ok & (z >= 2), down_dst, up_y)
            recv(f"y-{u}{h}", down_ok & (z < 2), window(10 + dz, h, HEAD), up_y)
            recv(f"y+{u}{h}", up_ok & (z < 2), up_dst, down_y)
            recv(f"y+{u}{h}", up_ok & (z >= 2), window(2 + dz, h, LAST), down_y)
        else:
            recv(f"y-{u}{h}", down_ok & (z != 0) if u == -1 else down_ok, down_dst, up_y)
            recv(f"y+{u}{h}", up_ok & (z != 3) if u == 1 else up_ok, up_dst, down_y)

    def both(when, ok):
        return ok if when is None else when & ok

    def spread(h):
        a, b = (None, None) if h else (top, base)
        send(f"a1{h}", both(a, z < 3), window(10, h), window(9, h), up_z)
        send(f"b1{h}", both(b, z > 0), window(2, h), window(3, h), down_z)
        send(f"a2{h}", a, window(10, h), window(jnp.where(low, 7, 11), h), down_z)
        send(f"b2{h}", b, window(2, h), window(jnp.where(high, 5, 1), h), up_z)

    def spread_on(h):
        a, b = (None, None) if h else (top, base)
        recv(f"a1{h}", both(a, z > 0), window(9, h), down_z)
        recv(f"b1{h}", both(b, z < 3), window(3, h), up_z)
        recv(f"a2{h}", a, window(jnp.where(high, 7, 11), h), up_z)
        recv(f"b2{h}", b, window(jnp.where(low, 5, 1), h), down_z)
        if h:
            send(f"a3{h}", mid, window(9, h), window(8, h), up_z)
            send(f"b3{h}", mid, window(3, h), window(4, h), down_z)
        else:
            send(f"a3{h}", both(a, low | high), window(jnp.where(low, 11, 7), h), window(8, h), down_z)
            send(f"b3{h}", both(b, low | high), window(jnp.where(low, 5, 1), h), window(4, h), up_z)
        send(f"a4{h}", both(a, mid), window(11, h, HEAD), window(12, h, HEAD), down_z)
        send(f"b4{h}", both(b, mid), window(1, h, LAST), window(0, h, LAST), up_z)

    def spread_last(h):
        a, b = (None, None) if h else (top, base)
        recv(f"a3{h}", both(a, z >= 2), window(8, h), down_z)
        recv(f"b3{h}", both(b, z < 2), window(4, h), down_z)
        recv(f"a4{h}", both(a, z < 2), window(12, h, HEAD), up_z)
        recv(f"b4{h}", both(b, z >= 2), window(0, h, LAST), down_z)

    near_to, near_from = (low & (y > 0)) | (high & (y < 3)), (low & (y < 3)) | (high & (y > 0))
    near = at(xh, jnp.where(low, ym, yp), z)
    near_src = at(xh, jnp.where(low, yp, ym), z)
    across = at(xh, y, jnp.where(low, 3, 0))
    across_from = (high & (y < 3)) | (low & (y > 0))
    block, beside = jnp.where(low, 10, 2), jnp.where(low, 11, 1)
    far, far_part = jnp.where(low, 11, 1), jnp.where(low, 12, 0)
    got, got_part = jnp.where(low, 1, 11), jnp.where(low, 0, 12)

    def second(h):
        send(f"d{h}", near_to, window(block, h), X.at[0, h], near)

    def second_part(h, ok):
        send(f"dp{h}", near_to & ok, window(beside, h, tail(low)), X.at[1, h, :, tail(low)], near)

    crossed = jnp.where(y == 1, 3, 9)

    def cross():
        send("g0", crossing, window(crossed, 0), S.at[0, 0], mirror)

    y_sends(0, 1)
    send("z-0", None, vec.at[0], window(6 + z - zp, 0), up_z)
    send("z+1", None, vec.at[1], window(6 + z - zm, 1), down_z)
    y_sends(0, 0)
    send("z-1", None, vec.at[1], window(6 + z - zp, 1), up_z)
    send("z+0", None, vec.at[0], window(6 + z - zm, 0), down_z)
    for h in HALVES:
        send(f"gp{h}", part_sender, vec.at[h, :, tail(y == 1)], S.at[1, h, :, tail(y == 1)], part_to)

    def pieces(c):
        if c < CHUNKS - 1:
            return ((f"{c}", None, pl.ds(c * PER, PER)),)
        end = SLOTS - AROUND
        return (("e", None, pl.ds(c * PER, end - c * PER)), ("f", ~outer, pl.ds(end, AROUND)))

    def chunk(c):
        for name, when, part in pieces(c):
            send(f"x{name}", when, hop.at[part], GB.at[0, part], along(2))

    def forward(c):
        for name, when, part in pieces(c):
            recv(f"x{name}", when, GB.at[0, part], along(2))
            send(f"o{name}", when, GB.at[0, part], GB.at[1, part], along(1))

    around = pl.ds(SLOTS - AROUND, AROUND)
    send("g1", split, vec.at[1], S.at[0, 1], mirror)
    send("r", outer, hop.at[around], R.at[0], beside_y)
    for c in range(3):
        chunk(c)
    for flip in (1, 2, 3):
        for i, (src, dst) in enumerate(lists):
            send(f"c{flip}{i}", None, src, dst.at[flip], along(flip))
    send("sib", None, hop, GA.at[pl.ds(SLOTS, SLOTS)], along(1))

    def ranked():
        none = 2 * SLOTS
        blocks = lax.broadcasted_iota(jnp.int32, (TS, SLOTS), 0)
        place = lax.broadcasted_iota(jnp.int32, (TS, SLOTS), 1)
        waves = (jnp.cos(phase[...]), jnp.sin(phase[...]))
        found, scales = [], []
        for m in range(2):
            r = CR[m] - row * TR
            w = CC[m] - (row * TR + r - BAND)
            w = jnp.where(w < 0, w + TORB, w)
            w = jnp.where(w >= TORB, w - TORB, w)
            b = jnp.where(place[:1] < CN[m], r * WIDE + w, -1)
            found.append(jnp.where(blocks == b, place + m * SLOTS, none))
            scales.append(
                [
                    sum(jnp.where(CL[m] == n, waves[p][k : k + 1, n : n + 1], 0.0) for n in range(NLAT))
                    for k in range(2)
                    for p in range(2)
                ]
            )
        lane = lax.broadcasted_iota(jnp.int32, (TS, TS), 1)
        chosen, scaled = jnp.zeros((TS, TS), jnp.int32), jnp.zeros((TS, TS), jnp.float32)
        used = [jnp.zeros((TS, SLOTS), jnp.int32)] * 2
        for d in range(DEPTH):
            best = [jnp.min(f, axis=1, keepdims=True) for f in found]
            best = jnp.minimum(best[0], best[1])
            hits = [(f == best) & (f < none) for f in found]
            chosen = jnp.where(lane == d, jnp.where(best < none, best, 0), chosen)
            for j in range(4):
                total = sum(
                    jnp.sum(jnp.where(hits[m], scales[m][j], 0.0), axis=1, keepdims=True) for m in range(2)
                )
                scaled = jnp.where(lane == 4 * d + j, total, scaled)
            used = [jnp.where(hits[m], 1, used[m]) for m in range(2)]
            found = [jnp.where(hits[m], none, found[m]) for m in range(2)]
        picks[...] = chosen
        factors[...] = scaled
        for m in range(2):
            U[m] = jnp.max(used[m], axis=0, keepdims=True)

    tables = [
        pltpu.make_async_copy(picks, pick, local_sem.at[7]),
        pltpu.make_async_copy(factors, factor, local_sem.at[8]),
    ]

    def fill(b, _):
        r = b // WIDE
        columns = pl.ds(pl.multiple_of((b - r * WIDE) * TS, TS), TS)
        chosen = [pick[b, d] for d in range(DEPTH)]
        scale = [[factor[b, 4 * d + j] for j in range(4)] for d in range(DEPTH)]
        size = 32
        for at_row in range(0, TS, size):
            tiles = [GA[c, pl.ds(at_row, size), :].astype(jnp.float32) for c in chosen]
            for k in range(2):
                for p in range(2):
                    total = tiles[0] * scale[0][2 * k + p]
                    for d in range(1, DEPTH):
                        total += tiles[d] * scale[d][2 * k + p]
                    (H0, H1)[k][r, pl.ds(p * TS + at_row, size), columns] = total
        return 0

    filled = [0]

    def some(count):
        start, filled[0] = filled[0], min(filled[0] + count, TR * WIDE)
        lax.fori_loop(start, filled[0], fill, 0)

    recv("z-0", None, window(6 + zm - z, 0), down_z)
    send("w0", None, window(6 + zm - z, 0), window(6 + zm - zp, 0), up_z)
    y_sends(-1, 0)
    recv("z+1", None, window(6 + zp - z, 1), up_z)
    send("w1", None, window(6 + zp - z, 1), window(6 + zp - zm, 1), down_z)
    recv("g1", split, S.at[0, 1], mirror)
    send("e1", split, S.at[0, 1], E.at[0, 1], over)
    y_recvs(0, 1)
    spread(1)
    second(1)
    for i, (_, dst) in enumerate(lists):
        recv(f"c1{i}", None, dst.at[1], along(1))
    recv("sib", None, GA.at[pl.ds(SLOTS, SLOTS)], along(1))
    for copy in local:
        copy.wait()
    ranked()
    for copy in tables:
        copy.start()
    recv("z+0", None, window(6 + zp - z, 0), up_z)
    y_sends(1, 0)
    recv("z-1", None, window(6 + zm - z, 1), down_z)
    cross()
    recv("r", ~outer, R.at[0], beside_y)
    send("q", ~outer, R.at[0], R.at[1], along(2))
    for c in range(3, CHUNKS):
        chunk(c)
    for copy in tables:
        copy.wait()
    some(10)
    y_recvs(0, 0)
    second(0)
    spread(0)
    some(10)
    recv("w0", None, window(6 + z2 - z, 0), down_z)
    y_sends(2, 0, ~crossing)
    some(10)
    recv("w1", None, window(6 + z2 - z, 1), up_z)
    for h in (1, 0):
        recv(f"d{h}", near_from, X.at[0, h], near_src)
        send(f"f{h}", near_from, X.at[0, h], window(far, h), across)
    some(10)
    recv("g0", crossing, S.at[0, 0], mirror)
    send("e0", crossing, S.at[0, 0], E.at[0, 0], beside_y)
    y_sends(2, 0, crossing)
    for h in HALVES:
        recv(f"gp{h}", crossing, S.at[1, h, :, tail(y == 1)], part_from)
        send(f"ep{h}", crossing, S.at[1, h, :, tail(y == 1)], E.at[1, h, :, tail(y == 1)], beside_y)
    def onward(h):
        recv(f"e{h}", relay, E.at[0, h], split_from if h else over_from)
        send(f"f{h}", relay, E.at[0, h], window(got, h), inner_y)

    def onward_part(h):
        recv(f"ep{h}", relay, E.at[1, h, :, tail(high)], over_from)
        send(f"fp{h}", relay, E.at[1, h, :, tail(high)], window(got_part, h, tail(high)), inner_y)

    some(10)
    y_recvs(-1, 0)
    y_recvs(1, 0)
    second_part(0, (low & (y < 3)) | (high & (y > 0)))
    spread_on(1)
    second_part(1, low | high)
    some(10)
    onward(1)
    onward(0)
    some(10)
    spread_on(0)
    second_part(0, (low & top) | (high & base))
    for h in HALVES:
        onward_part(h)
    some(10)
    recv("q", ~outer, R.at[1], along(2))
    send("p", ~outer, R.at[1], GB.at[0, around], beside_y)
    for c in range(3):
        forward(c)
    some(TR * WIDE)
    for h in HALVES:
        recv(f"dp{h}", near_from, X.at[1, h, :, tail(low)], near_src)
        send(f"fp{h}", near_from, X.at[1, h, :, tail(low)], window(far_part, h, tail(low)), across)
    rim = low | high
    next_to = at(xh, y, jnp.where(low, 1, 2))
    for h in (1, 0):
        recv(f"f{h}", rim, window(got, h), across)
        send(f"l{h}", rim, window(got, h, tail(high)), window(got_part, h, tail(high)), next_to)
    for c in range(3, CHUNKS - 2):
        forward(c)
    y_recvs(2, 0)
    for h in HALVES:
        spread_last(h)
        recv(f"fp{h}", rim, window(got_part, h, tail(high)), across)
        recv(f"l{h}", mid, window(jnp.where(z == 1, 0, 12), h, tail(z == 2)), at(xh, y, jnp.where(z == 1, 0, 3)))
    for flip in (2, 3):
        for i, (_, dst) in enumerate(lists):
            recv(f"c{flip}{i}", None, dst.at[flip], along(flip))
    recv("p", outer, GB.at[0, around], beside_y)
    send("of", outer, GB.at[0, around], GB.at[1, around], along(1))
    for c in range(CHUNKS - 2, CHUNKS):
        forward(c)
    for c in range(CHUNKS):
        for name, _, part in pieces(c):
            recv(f"o{name}", None, GB.at[1, part], along(1))
    net.finish()


def gather_all(phase, hop, lists, vec):
    block = vec.shape
    any_space = pl.BlockSpec(memory_space=pl.ANY)
    vmem = pl.BlockSpec(memory_space=pltpu.VMEM)
    sems = 104
    return pl.pallas_call(
        gather_kernel,
        out_shape=(
            pltpu.VMEM((2 * SLOTS,) + hop.shape[1:], hop.dtype),
            pltpu.VMEM((2,) + hop.shape, hop.dtype),
            pltpu.VMEM(block[:2] + (SPAN * TS,) + block[3:], vec.dtype),
            *[pltpu.VMEM(MATRIX, jnp.float32)] * 2,
            pltpu.VMEM((2, 1, SLOTS), jnp.int32),
            *[pltpu.VMEM((4,) + a.shape, a.dtype) for a in lists],
            *[pltpu.HBM((2,) + block, vec.dtype)] * 3,
            pltpu.HBM((2, AROUND) + hop.shape[1:], hop.dtype),
        ),
        in_specs=[pl.BlockSpec(memory_space=pltpu.HBM)] * 7,
        out_specs=(vmem,) + (any_space,) * 2 + (vmem,) * 7 + (any_space,) * 4,
        scratch_shapes=[
            pltpu.VMEM(phase.shape, phase.dtype),
            pltpu.VMEM((TS, TS), jnp.int32),
            pltpu.VMEM((TS, TS), jnp.float32),
            pltpu.SMEM((TS, TS), jnp.int32),
            pltpu.SMEM((TS, TS), jnp.float32),
            pltpu.SemaphoreType.DMA((sems,)),
            pltpu.SemaphoreType.DMA((sems,)),
            pltpu.SemaphoreType.DMA((10,)),
        ],
        compiler_params=pltpu.CompilerParams(
            collective_id=0, has_side_effects=True, vmem_limit_bytes=GATHER_VMEM
        ),
        name="gather",
    )(*[a if a.size == 1 else pltpu.with_memory_space_constraint(a, pltpu.HBM) for a in (phase, hop, *lists, vec)])[:10]


def product_kernel(phase, GA, GB, W, Z0, Z1, U, CR, CC, CL, CN, out, H0, H1, O, NR, NC, NL, NN, NU, rest, factor, table, sems):
    row = lax.axis_index("rows")
    H = (H0, H1)
    scalars = [
        pltpu.make_async_copy(src, dst, sems.at[30 + i])
        for i, (src, dst) in enumerate(((CR, NR), (CC, NC), (CL, NL), (CN, NN), (U, NU)))
    ]
    for copy in scalars:
        copy.start()
    factor[0:2, :] = jnp.cos(phase[...])
    factor[2:4, :] = jnp.sin(phase[...])
    factors = pltpu.make_async_copy(factor, table, sems.at[35])
    factors.start()

    for copy in scalars + [factors]:
        copy.wait()
    part = 32
    left = 0
    for m in range(2):

        def keep(i, n, m=m):
            rest[n] = m * SLOTS + i
            return n + 1 - NU[m, 0, i]

        left = lax.fori_loop(0, NN[m, 0, 0], keep, left)
    for m in (1, 2, 3):
        count = left if m == 1 else NN[m, 0, 0]

        def add(i, _, m=m, count=count):
            for one in [GROUP * i + j for j in range(GROUP)]:
                if m == 1:
                    slot = jnp.where(one < count, rest[one], 0)
                    n = jnp.where(slot >= SLOTS, 1, 0)
                    item, tiles = slot - n * SLOTS, GA.at[slot]
                else:
                    n, item, tiles = m, one, GB.at[m - 2, one]
                r = jnp.clip(NR[n, 0, item] - row * TR, 0, TR - 1)
                w = NC[n, 0, item] - (row * TR + r - BAND)
                w = jnp.where(w < 0, w + TORB, w)
                w = jnp.clip(jnp.where(w >= TORB, w - TORB, w), 0, WIDE - 1)
                cols = pl.ds(pl.multiple_of(w * TS, TS), TS)
                lat = NL[n, 0, item]
                scale = [jnp.where(one < count, table[2 * p + k, lat], 0.0) for k in range(2) for p in range(2)]
                for at in range(0, TS, part):
                    tile = tiles[pl.ds(at, part), :].astype(jnp.float32)
                    for k in range(2):
                        for p in range(2):
                            H[k][r, pl.ds(p * TS + at, part), cols] += tile * scale[2 * k + p]
            return 0

        lax.fori_loop(0, (count + GROUP - 1) // GROUP, add, 0)
    done = []
    for k in range(2):
        for r in range(TR):
            step = TR * k + r
            if step >= 2:
                done[step - 2].wait()
            rows = pl.ds(r * TS, TS)
            o = [jnp.zeros((2 * TS, NV), jnp.float32)] * 2
            for start, size in ((0, CUT), (CUT, WIDE - CUT)):
                left = H[k][r, :, start * TS : (start + size) * TS].astype(jnp.bfloat16)
                first = (r + start) * TS
                o = [
                    o[q]
                    + jnp.dot(
                        left,
                        W[k, q, first : first + size * TS, :],
                        preferred_element_type=jnp.float32,
                    )
                    for q in range(2)
                ]
            O[step % 2, 0] = o[0][:TS] - o[1][TS:]
            O[step % 2, 1] = o[1][:TS] + o[0][TS:]
            done.append(pltpu.make_async_copy(O.at[step % 2], out.at[k, :, rows], sems.at[36 + step]))
            done[-1].start()
    for copy in done[-2:]:
        copy.wait()


def product(phase, GA, GB, W, H0, H1, lists):
    any_space = pl.BlockSpec(memory_space=pl.ANY)
    vmem = pl.BlockSpec(memory_space=pltpu.VMEM)
    return pl.pallas_call(
        product_kernel,
        out_shape=(jax.ShapeDtypeStruct((2, 2, BLK, NV), jnp.float32),) + (pltpu.VMEM(MATRIX, jnp.float32),) * 2,
        input_output_aliases={4: 1, 5: 2},
        in_specs=[vmem] * 6 + [any_space] * 5,
        out_specs=(any_space, vmem, vmem),
        scratch_shapes=[
            pltpu.VMEM((2, 2, TS, NV), jnp.float32),
            *[pltpu.SMEM((4, 1, SLOTS), jnp.int32)] * 3,
            pltpu.SMEM((4, 1, 1), jnp.int32),
            pltpu.SMEM((2, 1, SLOTS), jnp.int32),
            pltpu.SMEM((2 * SLOTS + 8,), jnp.int32),
            pltpu.VMEM((4, NLAT), jnp.float32),
            pltpu.SMEM((4, NLAT), jnp.float32),
            pltpu.SemaphoreType.DMA((42,)),
        ],
        compiler_params=pltpu.CompilerParams(vmem_limit_bytes=4900 * 1024),
        name="product",
    )(phase, GA, GB, W, H0, H1, *lists)[0]


def body(hoppings, tile_rows, tile_cols, tile_lats, tile_counts, phase_angle, vectors):
    hop = hoppings[0]
    GA, GB, W, H0, H1, U, *lists = gather_all(phase_angle, hop, (tile_rows, tile_cols, tile_lats, tile_counts), vectors)
    return product(phase_angle, GA, GB, W, H0, H1, (U, *lists))


def solution(mesh):
    return jax.shard_map(
        body,
        mesh=mesh,
        in_specs=(
            P("rows", "ka", None, None),
            P("rows", "ka"),
            P("rows", "ka"),
            P("rows", "ka"),
            P("rows", "ka"),
            P("ka", None),
            P("ka", None, "rows", None),
        ),
        out_specs=P("ka", None, "rows", None),
        check_vma=False,
    )
```

time: 111 us -> 115 us (1.036)
  Pallas kernels: 111 us -> 113 us
    pallas_call x2, Pallas kernels: 111 us -> 113 us  [the longest x1 91.6 us: gather_all(): pl.pallas_call(gather_kernel, out_shape=(pltpu.VMEM((2 * SLOTS,) + hop.sh...]
where the time goes in v7:
time: 115 us
  Pallas kernels  113 us (98%)
    pallas_call x1, Pallas kernels, gather_all(): pl.pallas_call(gather_kernel, out_shape=(pltpu.VMEM((2 * SLOTS,) + hop.sh...  91.6 us
    pallas_call x1, Pallas kernels, product(): pl.pallas_call(product_kernel, out_shape=(jax.ShapeDtypeStruct((2, 2, BLK...  21.8 us

profile of v7, /device:TPU:1, one launch (start us, length us, event | category | flops | bytes accessed | tf_op | source)
XLA Modules:
  0.0 114.8 jit_solution(6916998691646574854)
XLA Ops:
  0.7 91.6 %gather.1 = (bf16[192,128,128]{2,1,0:T(8,128)(2,1)S(1)}, bf16[2,96,128,128]{3,2,1,0:T(8,128)(2,1)S(1)}, bf16[2,2,4480,256]{3,2,1,0:T(8,128)(2,1)S(1)}, f32[3,256...) custom-call(f32[2,9]{1,0:T(2,128)} %phase.1, ...), custom_call_target="tpu_custom_call" | custom-call | tf_op jit(solution)/shard_map/gather/pallas_call | solution.py:430
  92.3 0.0 copy-start
  92.3 0.7 copy-done
  92.9 21.8 %product.1 = (f32[2,2,384,256]{3,2,1,0:T(8,128)}, f32[3,256,4224]{2,1,0:T(8,128)S(1)}, f32[3,256,4224]{2,1,0:T(8,128)S(1)}) custom-call(f32[2,9]{1,0:T(2,128)S(1)} %copy-done, bf16[192,128,128]{2,1,0:T(8,128)(2,1)S(1)} %get-tuple-element.16.GA, bf16[2,96,128,128]{3,2,1,0:T(8,128)(2,1)S(1)} %get-tuple-element.17.GB, ...), custom_call_target="tpu_custom_call", output_to_operand_aliasing={{1}: (4, {}), {2}: (5, {})} | custom-call | tf_op jit(solution)/shard_map/product/pallas_call | solution.py:543
Async XLA Ops:
  92.3 0.7 copy-start

commit v8 on v7

--- a/solution.py
+++ b/solution.py
@@ -20,8 +20,7 @@
 AROUND = 6
 GATHER_VMEM = 1024 * 1024
 GROUP = 4
-DEPTH = 2
-CUT = 16
+DEPTH = 3
 WIDE = 2 * BAND + 1
 MATRIX = (TR, 2 * TS, WIDE * TS)
 SPAN = WIDE + TR - 1
@@ -62,7 +61,7 @@
 
 
 def gather_kernel(
-    angles, hop, rows, cols, lats, live, vec, GA, GB, W, H0, H1, U, CR, CC, CL, CN, S, X, E, R,
+    angles, hop, rows, cols, lats, live, vec, GA, GB, W, H0, H1, waves, U, CR, CC, CL, CN, S, X, E, R,
     phase, picks, factors, pick, factor, send_sem, recv_sem, local_sem,
 ):
     ka = lax.axis_index("ka")
@@ -256,7 +255,8 @@
         none = 2 * SLOTS
         blocks = lax.broadcasted_iota(jnp.int32, (TS, SLOTS), 0)
         place = lax.broadcasted_iota(jnp.int32, (TS, SLOTS), 1)
-        waves = (jnp.cos(phase[...]), jnp.sin(phase[...]))
+        wave = (jnp.cos(phase[...]), jnp.sin(phase[...]))
+        waves[0:2, :], waves[2:4, :] = wave
         found, scales = [], []
         for m in range(2):
             r = CR[m] - row * TR
@@ -267,7 +267,7 @@
             found.append(jnp.where(blocks == b, place + m * SLOTS, none))
             scales.append(
                 [
-                    sum(jnp.where(CL[m] == n, waves[p][k : k + 1, n : n + 1], 0.0) for n in range(NLAT))
+                    sum(jnp.where(CL[m] == n, wave[p][k : k + 1, n : n + 1], 0.0) for n in range(NLAT))
                     for k in range(2)
                     for p in range(2)
                 ]
@@ -434,13 +434,14 @@
             pltpu.VMEM((2,) + hop.shape, hop.dtype),
             pltpu.VMEM(block[:2] + (SPAN * TS,) + block[3:], vec.dtype),
             *[pltpu.VMEM(MATRIX, jnp.float32)] * 2,
+            pltpu.VMEM((4, NLAT), jnp.float32),
             pltpu.VMEM((2, 1, SLOTS), jnp.int32),
             *[pltpu.VMEM((4,) + a.shape, a.dtype) for a in lists],
             *[pltpu.HBM((2,) + block, vec.dtype)] * 3,
             pltpu.HBM((2, AROUND) + hop.shape[1:], hop.dtype),
         ),
         in_specs=[pl.BlockSpec(memory_space=pltpu.HBM)] * 7,
-        out_specs=(vmem,) + (any_space,) * 2 + (vmem,) * 7 + (any_space,) * 4,
+        out_specs=(vmem,) + (any_space,) * 2 + (vmem,) * 8 + (any_space,) * 4,
         scratch_shapes=[
             pltpu.VMEM(phase.shape, phase.dtype),
             pltpu.VMEM((TS, TS), jnp.int32),
@@ -455,24 +456,19 @@
             collective_id=0, has_side_effects=True, vmem_limit_bytes=GATHER_VMEM
         ),
         name="gather",
-    )(*[a if a.size == 1 else pltpu.with_memory_space_constraint(a, pltpu.HBM) for a in (phase, hop, *lists, vec)])[:10]
-
-
-def product_kernel(phase, GA, GB, W, Z0, Z1, U, CR, CC, CL, CN, out, H0, H1, O, NR, NC, NL, NN, NU, rest, factor, table, sems):
+    )(*[a if a.size == 1 else pltpu.with_memory_space_constraint(a, pltpu.HBM) for a in (phase, hop, *lists, vec)])[:11]
+
+
+def product_kernel(GA, GB, W, Z0, Z1, waves, U, CR, CC, CL, CN, out, H0, H1, O, NR, NC, NL, NN, NU, rest, table, sems):
     row = lax.axis_index("rows")
     H = (H0, H1)
     scalars = [
         pltpu.make_async_copy(src, dst, sems.at[30 + i])
-        for i, (src, dst) in enumerate(((CR, NR), (CC, NC), (CL, NL), (CN, NN), (U, NU)))
+        for i, (src, dst) in enumerate(((CR, NR), (CC, NC), (CL, NL), (CN, NN), (U, NU), (waves, table)))
     ]
     for copy in scalars:
         copy.start()
-    factor[0:2, :] = jnp.cos(phase[...])
-    factor[2:4, :] = jnp.sin(phase[...])
-    factors = pltpu.make_async_copy(factor, table, sems.at[35])
-    factors.start()
-
-    for copy in scalars + [factors]:
+    for copy in scalars:
         copy.wait()
     part = 32
     left = 0
@@ -512,59 +508,51 @@
     done = []
     for k in range(2):
         for r in range(TR):
-            step = TR * k + r
-            if step >= 2:
-                done[step - 2].wait()
+            left = H[k][r].astype(jnp.bfloat16)
             rows = pl.ds(r * TS, TS)
-            o = [jnp.zeros((2 * TS, NV), jnp.float32)] * 2
-            for start, size in ((0, CUT), (CUT, WIDE - CUT)):
-                left = H[k][r, :, start * TS : (start + size) * TS].astype(jnp.bfloat16)
-                first = (r + start) * TS
-                o = [
-                    o[q]
-                    + jnp.dot(
-                        left,
-                        W[k, q, first : first + size * TS, :],
-                        preferred_element_type=jnp.float32,
-                    )
-                    for q in range(2)
-                ]
-            O[step % 2, 0] = o[0][:TS] - o[1][TS:]
-            O[step % 2, 1] = o[1][:TS] + o[0][TS:]
-            done.append(pltpu.make_async_copy(O.at[step % 2], out.at[k, :, rows], sems.at[36 + step]))
+            o = [
+                jnp.dot(
+                    left,
+                    W[k, q, r * TS : (r + WIDE) * TS, :],
+                    preferred_element_type=jnp.float32,
+                )
+                for q in range(2)
+            ]
+            O[k, 0, rows, :] = o[0][:TS] - o[1][TS:]
+            O[k, 1, rows, :] = o[1][:TS] + o[0][TS:]
+            done.append(pltpu.make_async_copy(O.at[k, :, rows], out.at[k, :, rows], sems.at[36 + TR * k + r]))
             done[-1].start()
-    for copy in done[-2:]:
+    for copy in done:
         copy.wait()
 
 
-def product(phase, GA, GB, W, H0, H1, lists):
+def product(GA, GB, W, H0, H1, lists):
     any_space = pl.BlockSpec(memory_space=pl.ANY)
     vmem = pl.BlockSpec(memory_space=pltpu.VMEM)
     return pl.pallas_call(
         product_kernel,
         out_shape=(jax.ShapeDtypeStruct((2, 2, BLK, NV), jnp.float32),) + (pltpu.VMEM(MATRIX, jnp.float32),) * 2,
-        input_output_aliases={4: 1, 5: 2},
-        in_specs=[vmem] * 6 + [any_space] * 5,
+        input_output_aliases={3: 1, 4: 2},
+        in_specs=[vmem] * 5 + [any_space] * 6,
         out_specs=(any_space, vmem, vmem),
         scratch_shapes=[
-            pltpu.VMEM((2, 2, TS, NV), jnp.float32),
+            pltpu.VMEM((2, 2, BLK, NV), jnp.float32),
             *[pltpu.SMEM((4, 1, SLOTS), jnp.int32)] * 3,
             pltpu.SMEM((4, 1, 1), jnp.int32),
             pltpu.SMEM((2, 1, SLOTS), jnp.int32),
             pltpu.SMEM((2 * SLOTS + 8,), jnp.int32),
-            pltpu.VMEM((4, NLAT), jnp.float32),
             pltpu.SMEM((4, NLAT), jnp.float32),
             pltpu.SemaphoreType.DMA((42,)),
         ],
-        compiler_params=pltpu.CompilerParams(vmem_limit_bytes=4900 * 1024),
+        compiler_params=pltpu.CompilerParams(vmem_limit_bytes=5860 * 1024),
         name="product",
-    )(phase, GA, GB, W, H0, H1, *lists)[0]
+    )(GA, GB, W, H0, H1, *lists)[0]
 
 
 def body(hoppings, tile_rows, tile_cols, tile_lats, tile_counts, phase_angle, vectors):
     hop = hoppings[0]
-    GA, GB, W, H0, H1, U, *lists = gather_all(phase_angle, hop, (tile_rows, tile_cols, tile_lats, tile_counts), vectors)
-    return product(phase_angle, GA, GB, W, H0, H1, (U, *lists))
+    GA, GB, W, H0, H1, waves, U, *lists = gather_all(phase_angle, hop, (tile_rows, tile_cols, tile_lats, tile_counts), vectors)
+    return product(GA, GB, W, H0, H1, (waves, U, *lists))
 
 
 def solution(mesh):

time: 115 us -> 108 us (0.939)
  Pallas kernels: 113 us -> 107 us
    pallas_call x1, Pallas kernels: 21.8 us -> 15 us  [product(): pl.pallas_call(product_kernel, out_shape=(jax.ShapeDtypeStruct((2, 2, BLK...]
where the time goes in v8:
time: 108 us; the launch traced here: 107 us
  Pallas kernels  107 us (99%)
    pallas_call x1, Pallas kernels, gather_all(): pl.pallas_call(gather_kernel, out_shape=(pltpu.VMEM((2 * SLOTS,) + hop.sh...  91.6 us
    pallas_call x1, Pallas kernels, product(): pl.pallas_call(product_kernel, out_shape=(jax.ShapeDtypeStruct((2, 2, BLK...  15 us

profile of v8, /device:TPU:1, one launch (start us, length us, event | category | flops | bytes accessed | tf_op | source)
XLA Modules:
  0.0 107.3 jit_solution(5277029754378617348)
XLA Ops:
  0.7 91.6 %gather.1 = (bf16[192,128,128]{2,1,0:T(8,128)(2,1)S(1)}, bf16[2,96,128,128]{3,2,1,0:T(8,128)(2,1)S(1)}, bf16[2,2,4480,256]{3,2,1,0:T(8,128)(2,1)S(1)}, f32[3,256...) custom-call(f32[2,9]{1,0:T(2,128)} %angles.1, ...), custom_call_target="tpu_custom_call" | custom-call | tf_op jit(solution)/shard_map/gather/pallas_call | solution.py:430
  92.3 15.0 %product.1 = (f32[2,2,384,256]{3,2,1,0:T(8,128)}, f32[3,256,4224]{2,1,0:T(8,128)S(1)}, f32[3,256,4224]{2,1,0:T(8,128)S(1)}) custom-call(bf16[192,128,128]{2,1,0:T(8,128)(2,1)S(1)} %get-tuple-element.17.GA, bf16[2,96,128,128]{3,2,1,0:T(8,128)(2,1)S(1)} %get-tuple-element.18.GB, ...), custom_call_target="tpu_custom_call", output_to_operand_aliasing={{1}: (3, {}), {2}: (4, {})} | custom-call | tf_op jit(solution)/shard_map/product/pallas_call | solution.py:532

commit v9 on v8

--- a/solution.py
+++ b/solution.py
@@ -21,6 +21,7 @@
 GATHER_VMEM = 1024 * 1024
 GROUP = 4
 DEPTH = 3
+EARLY = 60
 WIDE = 2 * BAND + 1
 MATRIX = (TR, 2 * TS, WIDE * TS)
 SPAN = WIDE + TR - 1
@@ -61,7 +62,7 @@
 
 
 def gather_kernel(
-    angles, hop, rows, cols, lats, live, vec, GA, GB, W, H0, H1, waves, U, CR, CC, CL, CN, S, X, E, R,
+    angles, hop, rows, cols, lats, live, vec, GA, GE, GL, W, H0, H1, waves, U, CR, CC, CL, CN, S, X, E, R,
     phase, picks, factors, pick, factor, send_sem, recv_sem, local_sem,
 ):
     ka = lax.axis_index("ka")
@@ -226,6 +227,11 @@
     for h in HALVES:
         send(f"gp{h}", part_sender, vec.at[h, :, tail(y == 1)], S.at[1, h, :, tail(y == 1)], part_to)
 
+    def remote(n, part):
+        if part.start < EARLY:
+            return GE.at[pl.ds(n * EARLY + part.start, part.size)]
+        return GL.at[n, pl.ds(part.start - EARLY, part.size)]
+
     def pieces(c):
         if c < CHUNKS - 1:
             return ((f"{c}", None, pl.ds(c * PER, PER)),)
@@ -234,12 +240,12 @@
 
     def chunk(c):
         for name, when, part in pieces(c):
-            send(f"x{name}", when, hop.at[part], GB.at[0, part], along(2))
+            send(f"x{name}", when, hop.at[part], remote(0, part), along(2))
 
     def forward(c):
         for name, when, part in pieces(c):
-            recv(f"x{name}", when, GB.at[0, part], along(2))
-            send(f"o{name}", when, GB.at[0, part], GB.at[1, part], along(1))
+            recv(f"x{name}", when, remote(0, part), along(2))
+            send(f"o{name}", when, remote(0, part), remote(1, part), along(1))
 
     around = pl.ds(SLOTS - AROUND, AROUND)
     send("g1", split, vec.at[1], S.at[0, 1], mirror)
@@ -251,23 +257,23 @@
             send(f"c{flip}{i}", None, src, dst.at[flip], along(flip))
     send("sib", None, hop, GA.at[pl.ds(SLOTS, SLOTS)], along(1))
 
-    def ranked():
-        none = 2 * SLOTS
+    def ranked(pair, extent, depth):
+        none = 2 * extent
         blocks = lax.broadcasted_iota(jnp.int32, (TS, SLOTS), 0)
         place = lax.broadcasted_iota(jnp.int32, (TS, SLOTS), 1)
         wave = (jnp.cos(phase[...]), jnp.sin(phase[...]))
         waves[0:2, :], waves[2:4, :] = wave
         found, scales = [], []
-        for m in range(2):
+        for n, m in enumerate(pair):
             r = CR[m] - row * TR
             w = CC[m] - (row * TR + r - BAND)
             w = jnp.where(w < 0, w + TORB, w)
             w = jnp.where(w >= TORB, w - TORB, w)
-            b = jnp.where(place[:1] < CN[m], r * WIDE + w, -1)
-            found.append(jnp.where(blocks == b, place + m * SLOTS, none))
+            b = jnp.where(place[:1] < jnp.minimum(CN[m], extent), r * WIDE + w, -1)
+            found.append(jnp.where(blocks == b, place + n * extent, none))
             scales.append(
                 [
-                    sum(jnp.where(CL[m] == n, wave[p][k : k + 1, n : n + 1], 0.0) for n in range(NLAT))
+                    sum(jnp.where(CL[m] == v, wave[p][k : k + 1, v : v + 1], 0.0) for v in range(NLAT))
                     for k in range(2)
                     for p in range(2)
                 ]
@@ -275,7 +281,7 @@
         lane = lax.broadcasted_iota(jnp.int32, (TS, TS), 1)
         chosen, scaled = jnp.zeros((TS, TS), jnp.int32), jnp.zeros((TS, TS), jnp.float32)
         used = [jnp.zeros((TS, SLOTS), jnp.int32)] * 2
-        for d in range(DEPTH):
+        for d in range(depth):
             best = [jnp.min(f, axis=1, keepdims=True) for f in found]
             best = jnp.minimum(best[0], best[1])
             hits = [(f == best) & (f < none) for f in found]
@@ -289,35 +295,38 @@
             found = [jnp.where(hits[m], none, found[m]) for m in range(2)]
         picks[...] = chosen
         factors[...] = scaled
-        for m in range(2):
-            U[m] = jnp.max(used[m], axis=0, keepdims=True)
+        for n, m in enumerate(pair):
+            U[m] = jnp.max(used[n], axis=0, keepdims=True)
 
     tables = [
         pltpu.make_async_copy(picks, pick, local_sem.at[7]),
         pltpu.make_async_copy(factors, factor, local_sem.at[8]),
     ]
 
-    def fill(b, _):
+    def fill(b, source, depth, more):
         r = b // WIDE
         columns = pl.ds(pl.multiple_of((b - r * WIDE) * TS, TS), TS)
-        chosen = [pick[b, d] for d in range(DEPTH)]
-        scale = [[factor[b, 4 * d + j] for j in range(4)] for d in range(DEPTH)]
+        chosen = [pick[b, d] for d in range(depth)]
+        scale = [[factor[b, 4 * d + j] for j in range(4)] for d in range(depth)]
         size = 32
         for at_row in range(0, TS, size):
-            tiles = [GA[c, pl.ds(at_row, size), :].astype(jnp.float32) for c in chosen]
+            tiles = [source[c, pl.ds(at_row, size), :].astype(jnp.float32) for c in chosen]
             for k in range(2):
                 for p in range(2):
                     total = tiles[0] * scale[0][2 * k + p]
-                    for d in range(1, DEPTH):
+                    for d in range(1, depth):
                         total += tiles[d] * scale[d][2 * k + p]
-                    (H0, H1)[k][r, pl.ds(p * TS + at_row, size), columns] = total
+                    where = (r, pl.ds(p * TS + at_row, size), columns)
+                    if more:
+                        total += (H0, H1)[k][where]
+                    (H0, H1)[k][where] = total
         return 0
 
     filled = [0]
 
     def some(count):
         start, filled[0] = filled[0], min(filled[0] + count, TR * WIDE)
-        lax.fori_loop(start, filled[0], fill, 0)
+        lax.fori_loop(start, filled[0], lambda b, _: fill(b, GA, DEPTH, False), 0)
 
     recv("z-0", None, window(6 + zm - z, 0), down_z)
     send("w0", None, window(6 + zm - z, 0), window(6 + zm - zp, 0), up_z)
@@ -334,7 +343,7 @@
     recv("sib", None, GA.at[pl.ds(SLOTS, SLOTS)], along(1))
     for copy in local:
         copy.wait()
-    ranked()
+    ranked((0, 1), SLOTS, DEPTH)
     for copy in tables:
         copy.start()
     recv("z+0", None, window(6 + zp - z, 0), up_z)
@@ -390,7 +399,7 @@
         onward_part(h)
     some(10)
     recv("q", ~outer, R.at[1], along(2))
-    send("p", ~outer, R.at[1], GB.at[0, around], beside_y)
+    send("p", ~outer, R.at[1], remote(0, around), beside_y)
     for c in range(3):
         forward(c)
     some(TR * WIDE)
@@ -402,23 +411,34 @@
     for h in (1, 0):
         recv(f"f{h}", rim, window(got, h), across)
         send(f"l{h}", rim, window(got, h, tail(high)), window(got_part, h, tail(high)), next_to)
-    for c in range(3, CHUNKS - 2):
+    for c in range(3, EARLY // PER):
+        forward(c)
+    for flip in (2, 3):
+        for i, (_, dst) in enumerate(lists):
+            recv(f"c{flip}{i}", None, dst.at[flip], along(flip))
+    for c in range(EARLY // PER):
+        for name, _, part in pieces(c):
+            recv(f"o{name}", None, remote(1, part), along(1))
+    ranked((2, 3), EARLY, DEPTH - 1)
+    for copy in tables:
+        copy.start()
+    for copy in tables:
+        copy.wait()
+    lax.fori_loop(0, TR * WIDE, lambda b, _: fill(b, GE, DEPTH - 1, True), 0)
+    for c in range(EARLY // PER, CHUNKS - 2):
         forward(c)
     y_recvs(2, 0)
     for h in HALVES:
         spread_last(h)
         recv(f"fp{h}", rim, window(got_part, h, tail(high)), across)
         recv(f"l{h}", mid, window(jnp.where(z == 1, 0, 12), h, tail(z == 2)), at(xh, y, jnp.where(z == 1, 0, 3)))
-    for flip in (2, 3):
-        for i, (_, dst) in enumerate(lists):
-            recv(f"c{flip}{i}", None, dst.at[flip], along(flip))
-    recv("p", outer, GB.at[0, around], beside_y)
-    send("of", outer, GB.at[0, around], GB.at[1, around], along(1))
+    recv("p", outer, remote(0, around), beside_y)
+    send("of", outer, remote(0, around), remote(1, around), along(1))
     for c in range(CHUNKS - 2, CHUNKS):
         forward(c)
-    for c in range(CHUNKS):
+    for c in range(EARLY // PER, CHUNKS):
         for name, _, part in pieces(c):
-            recv(f"o{name}", None, GB.at[1, part], along(1))
+            recv(f"o{name}", None, remote(1, part), along(1))
     net.finish()
 
 
@@ -431,17 +451,18 @@
         gather_kernel,
         out_shape=(
             pltpu.VMEM((2 * SLOTS,) + hop.shape[1:], hop.dtype),
-            pltpu.VMEM((2,) + hop.shape, hop.dtype),
+            pltpu.VMEM((2 * EARLY,) + hop.shape[1:], hop.dtype),
+            pltpu.VMEM((2, SLOTS - EARLY) + hop.shape[1:], hop.dtype),
             pltpu.VMEM(block[:2] + (SPAN * TS,) + block[3:], vec.dtype),
             *[pltpu.VMEM(MATRIX, jnp.float32)] * 2,
             pltpu.VMEM((4, NLAT), jnp.float32),
-            pltpu.VMEM((2, 1, SLOTS), jnp.int32),
+            pltpu.VMEM((4, 1, SLOTS), jnp.int32),
             *[pltpu.VMEM((4,) + a.shape, a.dtype) for a in lists],
             *[pltpu.HBM((2,) + block, vec.dtype)] * 3,
             pltpu.HBM((2, AROUND) + hop.shape[1:], hop.dtype),
         ),
         in_specs=[pl.BlockSpec(memory_space=pltpu.HBM)] * 7,
-        out_specs=(vmem,) + (any_space,) * 2 + (vmem,) * 8 + (any_space,) * 4,
+        out_specs=(vmem,) * 2 + (any_space,) * 2 + (vmem,) * 8 + (any_space,) * 4,
         scratch_shapes=[
             pltpu.VMEM(phase.shape, phase.dtype),
             pltpu.VMEM((TS, TS), jnp.int32),
@@ -456,10 +477,10 @@
             collective_id=0, has_side_effects=True, vmem_limit_bytes=GATHER_VMEM
         ),
         name="gather",
-    )(*[a if a.size == 1 else pltpu.with_memory_space_constraint(a, pltpu.HBM) for a in (phase, hop, *lists, vec)])[:11]
-
-
-def product_kernel(GA, GB, W, Z0, Z1, waves, U, CR, CC, CL, CN, out, H0, H1, O, NR, NC, NL, NN, NU, rest, table, sems):
+    )(*[a if a.size == 1 else pltpu.with_memory_space_constraint(a, pltpu.HBM) for a in (phase, hop, *lists, vec)])[:12]
+
+
+def product_kernel(GA, GE, GL, W, Z0, Z1, waves, U, CR, CC, CL, CN, out, H0, H1, O, NR, NC, NL, NN, NU, rest, table, sems):
     row = lax.axis_index("rows")
     H = (H0, H1)
     scalars = [
@@ -471,25 +492,33 @@
     for copy in scalars:
         copy.wait()
     part = 32
-    left = 0
-    for m in range(2):
-
-        def keep(i, n, m=m):
-            rest[n] = m * SLOTS + i
-            return n + 1 - NU[m, 0, i]
-
-        left = lax.fori_loop(0, NN[m, 0, 0], keep, left)
-    for m in (1, 2, 3):
-        count = left if m == 1 else NN[m, 0, 0]
-
-        def add(i, _, m=m, count=count):
+    def passed(pair, extent):
+        count = 0
+        for m in pair:
+
+            def keep(i, n, m=m):
+                rest[n] = m * SLOTS + i
+                return n + 1 - NU[m, 0, i]
+
+            count = lax.fori_loop(0, jnp.minimum(NN[m, 0, 0], extent), keep, count)
+        return count
+
+    for group in range(4):
+        if group < 2:
+            count = passed((2 * group, 2 * group + 1), (SLOTS, EARLY)[group])
+        else:
+            count = jnp.maximum(NN[group, 0, 0] - EARLY, 0)
+
+        def add(i, _, group=group, count=count):
             for one in [GROUP * i + j for j in range(GROUP)]:
-                if m == 1:
-                    slot = jnp.where(one < count, rest[one], 0)
-                    n = jnp.where(slot >= SLOTS, 1, 0)
-                    item, tiles = slot - n * SLOTS, GA.at[slot]
+                if group < 2:
+                    slot = jnp.where(one < count, rest[one], 2 * group * SLOTS)
+                    n = jnp.where(slot >= (2 * group + 1) * SLOTS, 2 * group + 1, 2 * group)
+                    item = slot - n * SLOTS
+                    tiles = GE.at[item + (n - 2) * EARLY] if group else GA.at[slot]
                 else:
-                    n, item, tiles = m, one, GB.at[m - 2, one]
+                    late = jnp.minimum(one, SLOTS - EARLY - 1)
+                    n, item, tiles = group, late + EARLY, GL.at[group - 2, late]
                 r = jnp.clip(NR[n, 0, item] - row * TR, 0, TR - 1)
                 w = NC[n, 0, item] - (row * TR + r - BAND)
                 w = jnp.where(w < 0, w + TORB, w)
@@ -526,33 +555,33 @@
         copy.wait()
 
 
-def product(GA, GB, W, H0, H1, lists):
+def product(GA, GE, GL, W, H0, H1, lists):
     any_space = pl.BlockSpec(memory_space=pl.ANY)
     vmem = pl.BlockSpec(memory_space=pltpu.VMEM)
     return pl.pallas_call(
         product_kernel,
         out_shape=(jax.ShapeDtypeStruct((2, 2, BLK, NV), jnp.float32),) + (pltpu.VMEM(MATRIX, jnp.float32),) * 2,
-        input_output_aliases={3: 1, 4: 2},
-        in_specs=[vmem] * 5 + [any_space] * 6,
+        input_output_aliases={4: 1, 5: 2},
+        in_specs=[vmem] * 6 + [any_space] * 6,
         out_specs=(any_space, vmem, vmem),
         scratch_shapes=[
             pltpu.VMEM((2, 2, BLK, NV), jnp.float32),
             *[pltpu.SMEM((4, 1, SLOTS), jnp.int32)] * 3,
             pltpu.SMEM((4, 1, 1), jnp.int32),
-            pltpu.SMEM((2, 1, SLOTS), jnp.int32),
+            pltpu.SMEM((4, 1, SLOTS), jnp.int32),
             pltpu.SMEM((2 * SLOTS + 8,), jnp.int32),
             pltpu.SMEM((4, NLAT), jnp.float32),
             pltpu.SemaphoreType.DMA((42,)),
         ],
         compiler_params=pltpu.CompilerParams(vmem_limit_bytes=5860 * 1024),
         name="product",
-    )(GA, GB, W, H0, H1, *lists)[0]
+    )(GA, GE, GL, W, H0, H1, *lists)[0]
 
 
 def body(hoppings, tile_rows, tile_cols, tile_lats, tile_counts, phase_angle, vectors):
     hop = hoppings[0]
-    GA, GB, W, H0, H1, waves, U, *lists = gather_all(phase_angle, hop, (tile_rows, tile_cols, tile_lats, tile_counts), vectors)
-    return product(GA, GB, W, H0, H1, (waves, U, *lists))
+    GA, GE, GL, W, H0, H1, waves, U, *lists = gather_all(phase_angle, hop, (tile_rows, tile_cols, tile_lats, tile_counts), vectors)
+    return product(GA, GE, GL, W, H0, H1, (waves, U, *lists))
 
 
 def solution(mesh):

time: 108 us -> 111 us (1.028)
  the two profiles are of different devices: /device:TPU:1 before, /device:TPU:97 now
where the time goes in v9:
time: 111 us
  Pallas kernels  111 us (100%)
    pallas_call x1, Pallas kernels, gather_all(): pl.pallas_call(gather_kernel, out_shape=(pltpu.VMEM((2 * SLOTS,) + hop.sh...  98 us
    pallas_call x1, Pallas kernels, product(): pl.pallas_call(product_kernel, out_shape=(jax.ShapeDtypeStruct((2, 2, BLK...  12.8 us

profile of v9, /device:TPU:97, one launch (start us, length us, event | category | flops | bytes accessed | tf_op | source)
XLA Modules:
  0.0 111.4 jit_solution(10320642698012444786)
XLA Ops:
  0.7 98.0 %gather.1 = (bf16[192,128,128]{2,1,0:T(8,128)(2,1)S(1)}, bf16[120,128,128]{2,1,0:T(8,128)(2,1)S(1)}, bf16[2,36,128,128]{3,2,1,0:T(8,128)(2,1)S(1)}, bf16[2,2,448...) custom-call(f32[2,9]{1,0:T(2,128)} %angles.1, ...), custom_call_target="tpu_custom_call" | custom-call | tf_op jit(solution)/shard_map/gather/pallas_call | solution.py:450
  98.6 12.8 %product.1 = (f32[2,2,384,256]{3,2,1,0:T(8,128)}, f32[3,256,4224]{2,1,0:T(8,128)S(1)}, f32[3,256,4224]{2,1,0:T(8,128)S(1)}) custom-call(bf16[192,128,128]{2,1,0:T(8,128)(2,1)S(1)} %get-tuple-element.18.GA, bf16[120,128,128]{2,1,0:T(8,128)(2,1)S(1)} %get-tuple-element.19.GE, ...), custom_call_target="tpu_custom_call", output_to_operand_aliasing={{1}: (4, {}), {2}: (5, {})} | custom-call | tf_op jit(solution)/shard_map/product/pallas_call | solution.py:561

commit v10 on v9

--- a/solution.py
+++ b/solution.py
@@ -18,7 +18,7 @@
 CHUNKS = 8
 PER = SLOTS // CHUNKS
 AROUND = 6
-GATHER_VMEM = 1024 * 1024
+GATHER_VMEM = 2 * 1024 * 1024
 GROUP = 4
 DEPTH = 3
 EARLY = 60
@@ -419,12 +419,21 @@
     for c in range(EARLY // PER):
         for name, _, part in pieces(c):
             recv(f"o{name}", None, remote(1, part), along(1))
-    ranked((2, 3), EARLY, DEPTH - 1)
-    for copy in tables:
-        copy.start()
-    for copy in tables:
-        copy.wait()
-    lax.fori_loop(0, TR * WIDE, lambda b, _: fill(b, GE, DEPTH - 1, True), 0)
+
+    @pl.when(relay)
+    def _():
+        for m in (2, 3):
+            U[m] = jnp.zeros((1, SLOTS), jnp.int32)
+
+    @pl.when(~relay)
+    def _():
+        ranked((2, 3), EARLY, DEPTH - 1)
+        for copy in tables:
+            copy.start()
+        for copy in tables:
+            copy.wait()
+        lax.fori_loop(0, TR * WIDE, lambda b, _: fill(b, GE, DEPTH - 1, True), 0)
+
     for c in range(EARLY // PER, CHUNKS - 2):
         forward(c)
     y_recvs(2, 0)

time: 111 us -> 108 us (0.973)
  the two profiles are of different devices: /device:TPU:97 before, /device:TPU:99 now
where the time goes in v10:
time: 108 us
  Pallas kernels  107 us (99%)
    pallas_call x1, Pallas kernels, gather_all(): pl.pallas_call(gather_kernel, out_shape=(pltpu.VMEM((2 * SLOTS,) + hop.sh...  90.7 us
    pallas_call x1, Pallas kernels, product(): pl.pallas_call(product_kernel, out_shape=(jax.ShapeDtypeStruct((2, 2, BLK...  16.2 us

profile of v10, /device:TPU:99, one launch (start us, length us, event | category | flops | bytes accessed | tf_op | source)
XLA Modules:
  0.0 107.6 jit_solution(4438629945291133031)
XLA Ops:
  0.7 90.7 %gather.1 = (bf16[192,128,128]{2,1,0:T(8,128)(2,1)S(1)}, bf16[120,128,128]{2,1,0:T(8,128)(2,1)S(1)}, bf16[2,36,128,128]{3,2,1,0:T(8,128)(2,1)S(1)}, bf16[2,2,448...) custom-call(f32[2,9]{1,0:T(2,128)} %angles.1, ...), custom_call_target="tpu_custom_call" | custom-call | tf_op jit(solution)/shard_map/gather/pallas_call | solution.py:459
  91.4 16.2 %product.1 = (f32[2,2,384,256]{3,2,1,0:T(8,128)}, f32[3,256,4224]{2,1,0:T(8,128)S(1)}, f32[3,256,4224]{2,1,0:T(8,128)S(1)}) custom-call(bf16[192,128,128]{2,1,0:T(8,128)(2,1)S(1)} %get-tuple-element.18.GA, bf16[120,128,128]{2,1,0:T(8,128)(2,1)S(1)} %get-tuple-element.19.GE, ...), custom_call_target="tpu_custom_call", output_to_operand_aliasing={{1}: (4, {}), {2}: (5, {})} | custom-call | tf_op jit(solution)/shard_map/product/pallas_call | solution.py:570
